TPU v7x, 32 devices: a whole 2x2x4 slice. The times are simulated.
32 devices in a mesh: shell: 2 (over x), pix: 16 (over z, y, core).
Axes of the slice: x: 2, y: 2, z: 4, core: 2. Of those that a mesh axis runs over, the one named last changes fastest.
Arguments:
- block_tile: int32 [4, 1024], P('shell'), may hold values from 0 to 2047, as said below
- cell_index: int32 [4, 1024, 512], P('shell', 'pix'), may hold values from 0 to 2047
- masses: bfloat16 [4, 1024, 512], P('shell', 'pix'), may hold values from 0.125 to 8, as said below
- plane_coef: float32 [4], P('shell'), may hold values from 0.1 to 0.4
- plane_dist: float32 [4], P('shell'), may hold values from 0.2 to 1
- source_inv: float32 [4], P('shell'), may hold values from 0.5 to 1
Outputs:
- convergence: float32 [4, 2048, 2048], P('shell', 'pix')
- shear_one: float32 [4, 2048, 2048], P('shell', 'pix')
- shear_two: float32 [4, 2048, 2048], P('shell', 'pix')
Inputs may be any that keep to these rules, and one draw needn't show every extreme that they name: `block_tile`: each row is 16 aligned runs of 64 entries, one run per index of pix. The entries of a run are distinct, and at most 8 of them lie in one index's rows of tiles (tile b lies in the rows of index b // 128). In every plane some index receives exactly 8 tiles from every run. `masses`: positive particle weights.
All inputs are finite; a program needn't handle non-finite values.
Results may differ from a plain program's by a relative error of at most 0.0003.
Values sent between devices are 32-bit elements; how exact they have to be, the bound alone decides.
A program may use at most 64 MiB of HBM per device.

v0:
```python
from functools import partial
import math

import jax
import jax.numpy as jnp
from jax import lax
from jax.experimental import pallas as pl
from jax.experimental.pallas import tpu as pltpu
from jax.sharding import PartitionSpec as P
import numpy as np

L = 2048
TR = 16
TC = 128


HIGHEST = lax.Precision.HIGHEST


def entering(value, axis, join, neutral):
    count, mine = (lax.axis_size(axis), lax.axis_index(axis))
    pieces = jax.tree.map(lambda part: lax.all_gather(part, axis), value)
    running = jax.tree.map(
        lambda part, zero: jnp.full_like(part, 0) + jnp.asarray(zero, part.dtype), value, neutral
    )

    def lap(position, running):
        longer = join(running, jax.tree.map(lambda part: part[position], pieces))
        return jax.tree.map(lambda new, old: jnp.where(position < mine, new, old), longer, running)

    return lax.fori_loop(0, count - 1, lap, running)


def dft_table(left_size, right_size, period, sign_value):
    left_idx = jnp.arange(left_size)[:, None]
    right_idx = jnp.arange(right_size)[None, :]
    angle = 2.0 * math.pi / period * (left_idx * right_idx % period).astype(jnp.float32)
    return (jnp.cos(angle), sign_value * jnp.sin(angle))


def mix_outer(table, real_part, imag_part):
    cosine, sine_part = table
    contract = partial(jnp.einsum, "ab,...bc->...ac", precision=HIGHEST)
    return (
        contract(cosine, real_part) - contract(sine_part, imag_part),
        contract(sine_part, real_part) + contract(cosine, imag_part),
    )


def mix_inner(table, real_part, imag_part):
    cosine, sine_part = table
    product = partial(jnp.matmul, precision=HIGHEST)
    return (
        product(real_part, cosine) - product(imag_part, sine_part),
        product(real_part, sine_part) + product(imag_part, cosine),
    )


def twist(table, real_part, imag_part):
    cosine, sine_part = table
    return (real_part * cosine - imag_part * sine_part, real_part * sine_part + imag_part * cosine)


def transform_last(real_part, imag_part, sign_value):
    length = real_part.shape[-1]
    inner = math.gcd(length, 128)
    outer = length // inner
    leading = real_part.shape[:-1]
    real_part = real_part.reshape(leading + (outer, inner))
    imag_part = imag_part.reshape(leading + (outer, inner))
    outer_table = dft_table(outer, outer, outer, sign_value)
    inner_table = dft_table(inner, inner, inner, sign_value)
    twiddle = dft_table(outer, inner, length, sign_value)
    if sign_value < 0:
        real_part, imag_part = mix_outer(outer_table, real_part, imag_part)
        real_part, imag_part = twist(twiddle, real_part, imag_part)
        real_part, imag_part = mix_inner(inner_table, real_part, imag_part)
    else:
        real_part, imag_part = mix_inner(inner_table, real_part, imag_part)
        real_part, imag_part = twist(twiddle, real_part, imag_part)
        real_part, imag_part = mix_outer(outer_table, real_part, imag_part)
    return (real_part.reshape(leading + (length,)), imag_part.reshape(leading + (length,)))


def frequency_of(position, length):
    inner = math.gcd(length, 128)
    outer = length // inner
    frequency = position // inner + outer * (position % inner)
    signed = jnp.where(frequency >= length // 2, frequency - length, frequency).astype(jnp.float32)
    keep_mask = (frequency != length // 2).astype(jnp.float32)
    return (signed, keep_mask)


def add_pairs(earlier_pair, later_pair):
    return (earlier_pair[0] + later_pair[0], earlier_pair[1] + later_pair[1])


def deposit_group(item):
    cell_ids, weights = item
    tile_rows = cell_ids // TC
    tile_cols = cell_ids % TC
    row_hot = jnp.where(
        tile_rows[:, None, :] == jnp.arange(TR)[None, :, None],
        weights[:, None, :],
        jnp.zeros((), jnp.bfloat16),
    )
    col_hot = (tile_cols[:, :, None] == jnp.arange(TC)[None, None, :]).astype(jnp.bfloat16)
    return jnp.einsum("grk,gkc->grc", row_hot, col_hot, preferred_element_type=jnp.float32)


def rows_to_sending(packed, groups, slab, cols_own):
    count, fields = (packed.shape[0], packed.shape[1])
    return (
        packed.reshape(count, fields, slab, groups, cols_own)
        .transpose(3, 0, 1, 4, 2)
        .reshape(groups, count, fields, cols_own * slab)
    )


def arrived_to_columns(arrived, groups, slab, cols_own):
    count, fields = (arrived.shape[1], arrived.shape[2])
    return (
        arrived.reshape(groups, count, fields, cols_own, slab)
        .transpose(1, 2, 3, 0, 4)
        .reshape(count, fields, cols_own, groups * slab)
    )


def columns_to_sending(stacked, groups, slab, cols_own):
    count, fields = (stacked.shape[0], stacked.shape[1])
    return (
        stacked.reshape(count, fields, cols_own, groups, slab)
        .transpose(3, 0, 1, 2, 4)
        .reshape(groups, count, fields, cols_own * slab)
    )


def landed_to_rows(landed, groups, slab, cols_own):
    count, fields = (landed.shape[1], landed.shape[2])
    return (
        landed.reshape(groups, count, fields, cols_own, slab)
        .transpose(1, 2, 4, 0, 3)
        .reshape(count, fields, slab, groups * cols_own)
    )


def local(block_tile, cell_index, masses, plane_coef, plane_dist, source_inv):
    groups = lax.axis_size("pix")
    my_index = lax.axis_index("pix")
    planes, local_tiles, per_tile = cell_index.shape
    slab = L // groups
    per_owner = slab // TR * (L // TC)
    cap = max(1, 2 * local_tiles // groups)
    flat = TR * TC
    batch_tiles = 8
    deposited = lax.map(
        deposit_group,
        (cell_index.reshape(-1, batch_tiles, per_tile), masses.reshape(-1, batch_tiles, per_tile)),
    )
    tile_sums = deposited.reshape(planes, local_tiles, flat)
    table = block_tile.reshape(planes, groups, local_tiles)
    owner = table // per_owner
    earlier = jnp.arange(local_tiles)[:, None] < jnp.arange(local_tiles)[None, :]
    same_owner = owner[:, :, :, None] == owner[:, :, None, :]
    rank = jnp.sum(jnp.where(same_owner & earlier[None, None], 1, 0), axis=2)
    slot = owner * cap + rank
    my_slots = lax.dynamic_index_in_dim(slot, my_index, axis=1, keepdims=False)
    slot_grid = jnp.arange(groups)[:, None] * cap + jnp.arange(cap)[None, :]
    send_hot = (my_slots[:, None, None, :] == slot_grid[None, :, :, None]).astype(jnp.float32)
    outgoing = jnp.einsum("pnct,ptf->npcf", send_hot, tile_sums, precision=HIGHEST)
    incoming = lax.all_to_all(outgoing, "pix", split_axis=0, concat_axis=0, tiled=True)
    local_index = table - my_index * per_owner
    is_mine = owner == my_index
    tile_hot = (is_mine[..., None] & (local_index[..., None] == jnp.arange(per_owner))).astype(
        jnp.float32
    )
    slot_hot = (rank[..., None] == jnp.arange(cap)).astype(jnp.float32)
    placing = jnp.einsum("pstl,pstc->plsc", tile_hot, slot_hot, precision=HIGHEST)
    slab_tiles = jnp.einsum("plsc,spcf->plf", placing, incoming, precision=HIGHEST)
    density = (
        slab_tiles.reshape(planes, slab // TR, L // TC, TR, TC)
        .transpose(0, 1, 3, 2, 4)
        .reshape(planes, slab, L)
    )
    total = lax.psum(jnp.sum(density, axis=(1, 2)), "pix")
    contrast = density / (total / (L * L))[:, None, None] - 1.0
    near_local = jnp.cumsum(plane_coef[:, None, None] * contrast, axis=0)
    far_local = jnp.cumsum((plane_coef * plane_dist)[:, None, None] * contrast, axis=0)
    blank = jnp.zeros((slab, L), jnp.float32)
    near_before, far_before = entering(
        (near_local[-1], far_local[-1]), "shell", add_pairs, (blank, blank)
    )
    convergence = near_before + near_local - source_inv[:, None, None] * (far_before + far_local)
    cols_own = L // groups
    wave_x, keep_x = frequency_of(my_index * cols_own + jnp.arange(cols_own), L)
    wave_y, keep_y = frequency_of(jnp.arange(L), L)
    wave_x = wave_x[:, None]
    wave_y = wave_y[None, :]
    both_keep = keep_x[:, None] * keep_y[None, :]
    wave_power = jnp.maximum(wave_x * wave_x + wave_y * wave_y, 1.0)
    kernel_one = both_keep * (wave_x * wave_x - wave_y * wave_y) / wave_power
    kernel_two = both_keep * 2.0 * wave_x * wave_y / wave_power
    scale = 1.0 / (L * L)
    spec_real, spec_imag = transform_last(convergence[0::2], convergence[1::2], -1.0)
    sending = rows_to_sending(jnp.stack([spec_real, spec_imag], axis=1), groups, slab, cols_own)
    arrived = lax.all_to_all(sending, "pix", split_axis=0, concat_axis=0, tiled=True)
    columns = arrived_to_columns(arrived, groups, slab, cols_own)
    row_real, row_imag = transform_last(columns[:, 0], columns[:, 1], -1.0)
    first_real, first_imag = transform_last(row_real * kernel_one, row_imag * kernel_one, 1.0)
    second_real, second_imag = transform_last(row_real * kernel_two, row_imag * kernel_two, 1.0)
    stacked = jnp.stack([first_real, first_imag, second_real, second_imag], axis=1)
    landed = lax.all_to_all(
        columns_to_sending(stacked, groups, slab, cols_own),
        "pix",
        split_axis=0,
        concat_axis=0,
        tiled=True,
    )
    row_layout = landed_to_rows(landed, groups, slab, cols_own)
    even_one, odd_one = transform_last(row_layout[:, 0], row_layout[:, 1], 1.0)
    even_two, odd_two = transform_last(row_layout[:, 2], row_layout[:, 3], 1.0)
    shear_one = jnp.stack([even_one, odd_one], axis=1).reshape(planes, slab, L)
    shear_two = jnp.stack([even_two, odd_two], axis=1).reshape(planes, slab, L)
    return (convergence, shear_one * scale, shear_two * scale)


INNER = 128
OUTER = L // INNER
HALF_BLOCKS = OUTER // 2


def block_columns():
    cols = np.zeros((HALF_BLOCKS, INNER), np.int64)
    for b in range(HALF_BLOCKS - 1):
        cols[b] = b + 1 + OUTER * np.arange(INNER)
    half = np.arange(INNER // 2)
    cols[-1] = np.concatenate([OUTER * half, HALF_BLOCKS + OUTER * half])
    return cols


def split_table(table):
    high = table.astype(jnp.bfloat16)
    low = (table - high.astype(np.float64)).astype(jnp.bfloat16)
    return high, low


def row_tables():
    n2 = np.arange(INNER)
    out = np.zeros((HALF_BLOCKS, 2 * INNER, 2 * INNER))
    cols = block_columns()
    for b in range(HALF_BLOCKS):
        angle = 2 * np.pi / L * ((n2[:, None] * cols[b][None, :]) % L)
        co, si = np.cos(angle), np.sin(angle)
        if b < HALF_BLOCKS - 1:
            out[b] = np.block([[co, -si], [si, co]])
        else:
            h = INNER // 2
            out[b, :INNER, :h] = co[:, :h]
            out[b, :INNER, INNER : INNER + h] = -si[:, :h]
            out[b, INNER:, h:INNER] = co[:, h:]
            out[b, INNER:, INNER + h :] = -si[:, h:]
    return split_table(out)


def column_tables():
    idx = np.arange(INNER)
    angle = 2 * np.pi / INNER * ((idx[:, None] * idx[None, :]) % INNER)
    co, si = np.cos(angle), np.sin(angle)
    return split_table(np.block([[co, si], [-si, co]]))


def twiddle_tables():
    angle = 2 * np.pi / L * (np.arange(OUTER)[:, None] * np.arange(INNER)[None, :])
    return np.cos(angle).astype(np.float32), (-np.sin(angle)).astype(np.float32)


def times_root(value, k, n, sign):
    re, im = value
    k = k % n
    if k == 0:
        return value
    if 4 * k == n:
        return (-im, re) if sign > 0 else (im, -re)
    angle = 2 * math.pi * k / n
    c, s = math.cos(angle), sign * math.sin(angle)
    if 8 * k == n or 8 * k == 3 * n:
        if c > 0:
            return ((re - im) * c, (re + im) * c) if sign > 0 else ((re + im) * c, (im - re) * c)
        c = -c
        return ((re + im) * -c, (re - im) * c) if sign > 0 else ((im - re) * c, (re + im) * -c)
    return (re * c - im * s, re * s + im * c)


def fft_list(values, sign):
    n = len(values)
    if n == 1:
        return values
    even = fft_list(values[0::2], sign)
    odd = fft_list(values[1::2], sign)
    odd = [times_root(v, k, n, sign) for k, v in enumerate(odd)]
    return [(a[0] + b[0], a[1] + b[1]) for a, b in zip(even, odd)] + [
        (a[0] - b[0], a[1] - b[1]) for a, b in zip(even, odd)
    ]


def split_value(value):
    high = value.astype(jnp.bfloat16)
    return high, (value - high.astype(jnp.float32)).astype(jnp.bfloat16)


def three_pass(left, right, dims):
    dot = lambda a, b: lax.dot_general(a, b, (dims, ((), ())), preferred_element_type=jnp.float32)
    return dot(left[0], right[0]) + (dot(left[0], right[1]) + dot(left[1], right[0]))


def pack_kernel(slot_ref, list_ref, *out_refs):
    planes, tiles, size, _ = list_ref.shape
    groups, rows, _ = out_refs[0].shape
    cap = rows // size - 1
    for p in range(planes):
        out_ref = out_refs[p]
        out_ref[...] = jnp.zeros_like(out_ref)
        total = jnp.sum(list_ref[p, :, size // 2 :, :], axis=(0, 1))
        total = jnp.sum(total.reshape(1, TC), axis=1, keepdims=True)
        out_ref[:, cap * size :, :] = jnp.broadcast_to(total[None], (groups, size, TC))

        def tile(t, _):
            slot = slot_ref[p, t]
            rows_at = pl.ds(pl.multiple_of((slot % cap) * size, size), size)
            out_ref[slot // cap, rows_at, :] = list_ref[p, t]
            return 0

        lax.fori_loop(0, tiles, tile, 0)


def assemble_kernel(size, place_ref, in_ref, out_ref, held):
    groups, rows, _ = in_ref.shape
    cap = rows // size - 1
    tiles = out_ref.shape[0]
    half = size // 2
    held[...] = jnp.zeros_like(held)
    total = in_ref[0, cap * size : cap * size + 1, 0:1]
    for s in range(1, groups):
        total = total + in_ref[s, cap * size : cap * size + 1, 0:1]
    row_id = lax.broadcasted_iota(jnp.int32, (TR, TC), 0)
    col_id = lax.broadcasted_iota(jnp.int32, (TC, TC), 0)

    def source(s, _):
        for c in range(cap):
            at = place_ref[s * cap + c]
            entry = in_ref[s, c * size : (c + 1) * size, :]
            cells = entry[:half].astype(jnp.int32)
            row_hot, col_hot = [], []
            for i in range(half):
                cell = cells[i : i + 1]
                row_hot.append(jnp.where(row_id == cell // TC, entry[half + i : half + i + 1], 0.0))
                col_hot.append(jnp.where(col_id == cell % TC, 1.0, 0.0))
            held[at] = held[at] + lax.dot_general(
                jnp.concatenate(row_hot, axis=1).astype(jnp.bfloat16),
                jnp.concatenate(col_hot, axis=1).astype(jnp.bfloat16),
                (((1,), (1,)), ((), ())),
                preferred_element_type=jnp.float32,
            )
        return 0

    lax.fori_loop(0, groups, source, 0)
    factor = jnp.where(total > 0.0, (L * L) / total, 0.0)
    out_ref[...] = held[0:tiles] * factor[None] - 1.0


def row_forward_kernel(mix_ref, near0, near1, far0, far1, high_ref, low_ref, conv_ref, out_ref, held):
    tile_rows = near0.shape[0] // OUTER

    def chunk(t, _):
        rows = pl.ds(pl.multiple_of(t * TR, TR), TR)
        packed = []
        for n in range(OUTER):
            at = t * OUTER + n
            fields = (near0[at], near1[at], far0[at], far1[at])
            pair = []
            for i in range(2):
                value = mix_ref[i, 0] * fields[0]
                for j in range(1, 4):
                    value = value + mix_ref[i, j] * fields[j]
                conv_ref[i, rows, n * INNER : (n + 1) * INNER] = value
                pair.append(value)
            packed.append(tuple(pair))
        z = fft_list(packed, -1)
        for k in range(1, HALF_BLOCKS):
            (ar, ai), (br, bi) = z[k], z[OUTER - k]
            held[k - 1, 0, rows, :INNER] = 0.5 * (ar + br)
            held[k - 1, 0, rows, INNER:] = 0.5 * (ai - bi)
            held[k - 1, 1, rows, :INNER] = 0.5 * (ai + bi)
            held[k - 1, 1, rows, INNER:] = 0.5 * (br - ar)
        for p in range(2):
            held[HALF_BLOCKS - 1, p, rows, :INNER] = z[0][p]
            held[HALF_BLOCKS - 1, p, rows, INNER:] = z[HALF_BLOCKS][p]
        return 0

    lax.fori_loop(0, tile_rows, chunk, 0)

    def block(b, _):
        slab = tile_rows * TR
        value = held[b].reshape(2 * slab, 2 * INNER)
        result = three_pass(split_value(value), (high_ref[b], low_ref[b]), ((1,), (0,)))
        for p in range(2):
            for half in range(2):
                out_ref[b, p, half] = result[
                    p * slab : (p + 1) * slab, half * INNER : (half + 1) * INNER
                ]
        return 0

    lax.fori_loop(0, HALF_BLOCKS, block, 0)


def column_kernel(in_ref, col_ref, twr_ref, twi_ref, high_ref, low_ref, back_high_ref, back_low_ref, out_ref, held, *back):
    def twist_of(k, rows):
        return twr_ref[k, rows, :], twi_ref[k, rows, :]

    def forward(t, _):
        rows = pl.ds(pl.multiple_of(t * 8, 8), 8)
        z = fft_list([(in_ref[n, 0, rows, :], in_ref[n, 1, rows, :]) for n in range(OUTER)], -1)
        for k in range(OUTER):
            re, im = z[k]
            if k:
                c, s = twist_of(k, rows)
                re, im = re * c - im * s, re * s + im * c
            held[k, 0, rows, :] = re
            held[k, 1, rows, :] = im
        return 0

    lax.fori_loop(0, INNER // 8, forward, 0)
    signed_v = col_ref[0:1]
    weight = col_ref[1:2]
    inner_id = lax.broadcasted_iota(jnp.int32, (INNER, INNER), 0)

    def middle(k, _):
        value = held[k].reshape(2 * INNER, INNER)
        spectrum = three_pass((high_ref[...], low_ref[...]), split_value(value), ((1,), (0,)))
        u = k + OUTER * inner_id
        signed_u = jnp.where(u >= L // 2, u - L, u).astype(jnp.float32)
        scale = jnp.where(u == L // 2, 0.0, weight)
        uu, vv = signed_u * signed_u, signed_v * signed_v
        over = scale / jnp.maximum(uu + vv, 1.0)
        kernels = ((vv - uu) * over, 2.0 * signed_v * signed_u * over)
        for f in range(2):
            twice = jnp.concatenate([kernels[f], kernels[f]], axis=0)
            result = three_pass(
                (back_high_ref[...], back_low_ref[...]), split_value(spectrum * twice), ((1,), (0,))
            )
            re, im = result[:INNER], result[INNER:]
            c, s = twr_ref[k], twi_ref[k]
            back[f][k, 0] = re * c + im * s
            back[f][k, 1] = im * c - re * s
        return 0

    lax.fori_loop(0, OUTER, middle, 0)
    for f in range(2):

        def inverse(t, _):
            rows = pl.ds(pl.multiple_of(t * 8, 8), 8)
            x = fft_list([(back[f][k, 0, rows, :], back[f][k, 1, rows, :]) for k in range(OUTER)], 1)
            for n in range(OUTER):
                out_ref[n, f, 0, rows, :] = x[n][0]
                out_ref[n, f, 1, rows, :] = x[n][1]
            return 0

        lax.fori_loop(0, INNER // 8, inverse, 0)


def row_inverse_kernel(in_ref, high_ref, low_ref, one_ref, two_ref, held):
    slab = in_ref.shape[4]
    for f, out_ref in enumerate((one_ref, two_ref)):

        def block(b, _):
            value = jnp.concatenate(
                [jnp.concatenate([in_ref[b, p, f, 0], in_ref[b, p, f, 1]], axis=1) for p in range(2)], axis=0
            )
            held[b] = three_pass(split_value(value), (high_ref[b], low_ref[b]), ((1,), (1,))).reshape(
                2, slab, 2 * INNER
            )
            return 0

        lax.fori_loop(0, HALF_BLOCKS, block, 0)

        def chunk(t, _):
            rows = pl.ds(pl.multiple_of(t * 8, 8), 8)
            z = [None] * OUTER
            last = HALF_BLOCKS - 1
            z[0] = (held[last, 0, rows, :INNER], held[last, 1, rows, :INNER])
            z[HALF_BLOCKS] = (held[last, 0, rows, INNER:], held[last, 1, rows, INNER:])
            for k in range(1, HALF_BLOCKS):
                ar, ai = held[k - 1, 0, rows, :INNER], held[k - 1, 0, rows, INNER:]
                br, bi = held[k - 1, 1, rows, :INNER], held[k - 1, 1, rows, INNER:]
                z[k] = (ar - bi, ai + br)
                z[OUTER - k] = (ar + bi, br - ai)
            x = fft_list(z, 1)
            for n in range(OUTER):
                for p in range(2):
                    out_ref[p, rows, n * INNER : (n + 1) * INNER] = x[n][p]
            return 0

        lax.fori_loop(0, slab // 8, chunk, 0)


def call(body, outs, scratch=(), smem=(0,), count=1, megabytes=48, flops=0):
    space = [
        pl.BlockSpec(memory_space=pltpu.SMEM if i in smem else pltpu.VMEM) for i in range(count)
    ]
    return pl.pallas_call(
        body,
        out_shape=outs,
        in_specs=space,
        out_specs=jax.tree.map(lambda _: pl.BlockSpec(memory_space=pltpu.VMEM), outs),
        scratch_shapes=list(scratch),
        compiler_params=pltpu.CompilerParams(vmem_limit_bytes=megabytes << 20),
        cost_estimate=pl.CostEstimate(flops=flops, bytes_accessed=4 << 20, transcendentals=0),
    )


def shape(*dims):
    return jax.ShapeDtypeStruct(dims, jnp.float32)


def local_fast(block_tile, cell_index, masses, plane_coef, plane_dist, source_inv):
    groups = lax.axis_size("pix")
    me = lax.axis_index("pix")
    mine_shell = lax.axis_index("shell")
    planes, local_tiles, per_tile = cell_index.shape
    slab = L // groups
    per_owner = slab // TR * (L // TC)
    cap = max(1, 2 * local_tiles // groups)

    pairs = [(0, 1)]
    other = lax.ppermute(jnp.concatenate([plane_coef, plane_dist]), "shell", pairs)
    other_coef = jnp.where(mine_shell > 0, other[:planes], 0.0)
    other_dist = other[planes:]

    earlier = jnp.arange(local_tiles)[:, None] < jnp.arange(local_tiles)[None, :]
    wanted = me * cap + jnp.arange(cap)

    def routes(tiles):
        table = tiles.reshape(planes, groups, local_tiles)
        owner = table // per_owner
        same_owner = owner[:, :, :, None] == owner[:, :, None, :]
        rank = jnp.sum(jnp.where(same_owner & earlier[None, None], 1, 0), axis=2)
        slot = owner * cap + rank
        here = slot[:, :, None, :] == wanted[None, None, :, None]
        local_index = table - me * per_owner
        place = jnp.sum(jnp.where(here, local_index[:, :, None, :] + 1, 0), axis=3)
        place = jnp.where(place > 0, place - 1, per_owner).reshape(planes, groups * cap)
        return slot, place

    slot, place = routes(block_tile)
    _, other_place = routes(lax.ppermute(block_tile, "shell", pairs))
    my_slots = lax.dynamic_index_in_dim(slot, me, axis=1, keepdims=False)

    half = per_tile // TC
    as_lists = lambda part: part.astype(jnp.float32).reshape(planes, local_tiles, half, TC)
    lists = jnp.concatenate([as_lists(cell_index), as_lists(masses)], axis=2)
    outgoing = call(
        pack_kernel, [shape(groups, (cap + 1) * 2 * half, TC)] * planes, count=2, flops=1 << 20
    )(my_slots, lists)
    deposit = lambda where, entries: call(
        partial(assemble_kernel, 2 * half),
        shape(per_owner, TR, TC),
        [pltpu.VMEM((per_owner + 1, TR, TC), jnp.float32)],
        count=2,
        flops=1 << 31,
    )(where, entries)
    near, far = [], []
    for p in range(planes):
        incoming = lax.all_to_all(outgoing[p], "pix", split_axis=0, concat_axis=0, tiled=True)
        passed = lax.ppermute(incoming, "shell", pairs)
        near.append(deposit(place[p], incoming))
        far.append(deposit(other_place[p], passed))

    own = plane_coef[None, :] * (1.0 - source_inv[:, None] * plane_dist[None, :])
    own = jnp.where(jnp.arange(planes)[None, :] <= jnp.arange(planes)[:, None], own, 0.0)
    before = other_coef[None, :] * (1.0 - source_inv[:, None] * other_dist[None, :])
    mix = jnp.concatenate([own, before], axis=1)

    row_high, row_low = row_tables()
    convergence, sending = call(
        row_forward_kernel,
        [shape(planes, slab, L), shape(HALF_BLOCKS, planes, 2, slab, INNER)],
        [pltpu.VMEM((HALF_BLOCKS, planes, slab, 2 * INNER), jnp.float32)],
        count=7,
        flops=1 << 30,
    )(mix, *near, *far, row_high, row_low)
    arrived = lax.all_to_all(
        sending.reshape(groups, 2, slab, INNER), "pix", split_axis=0, concat_axis=0, tiled=True
    )

    columns = jnp.asarray(block_columns().astype(np.float32))
    mine = lax.dynamic_index_in_dim(columns, me // planes, axis=0, keepdims=False)
    special = (me // planes == HALF_BLOCKS - 1) & (mine > 0)
    weight = jnp.where(special, 2.0, 1.0) / (L * L)
    signed = jnp.where(mine >= L // 2, mine - L, mine)
    col_info = jnp.stack([signed, weight])
    col_high, col_low = column_tables()
    tw_real, tw_imag = twiddle_tables()
    spread = lambda t: jnp.broadcast_to(jnp.asarray(t)[:, :, None], (OUTER, INNER, INNER))
    leaving = call(
        column_kernel,
        shape(groups, 2, 2, slab, INNER),
        [pltpu.VMEM((OUTER, 2, INNER, INNER), jnp.float32)] * 3,
        smem=(),
        count=8,
        flops=1 << 31,
    )(arrived, col_info, spread(tw_real), spread(tw_imag), col_high, col_low, col_high.T.copy(), col_low.T.copy())
    landed = lax.all_to_all(leaving, "pix", split_axis=0, concat_axis=0, tiled=True)
    shear_one, shear_two = call(
        row_inverse_kernel,
        [shape(planes, slab, L)] * 2,
        [pltpu.VMEM((HALF_BLOCKS, planes, slab, 2 * INNER), jnp.float32)],
        smem=(),
        count=3,
        flops=1 << 31,
    )(landed.reshape(HALF_BLOCKS, planes, 2, 2, slab, INNER), row_high, row_low)
    return convergence, shear_one, shear_two


def solution(mesh):
    placed = (
        P("shell", None),
        P("shell", "pix", None),
        P("shell", "pix", None),
        P("shell"),
        P("shell"),
        P("shell"),
    )
    shells, groups = mesh.shape["shell"], mesh.shape["pix"]

    def body(block_tile, cell_index, *rest):
        fits = (
            shells == 2
            and cell_index.shape[0] == 2
            and groups == OUTER
            and cell_index.shape[2] % (4 * TC) == 0
        )
        return (local_fast if fits else local)(block_tile, cell_index, *rest)

    return jax.shard_map(
        body,
        mesh=mesh,
        in_specs=placed,
        out_specs=(P("shell", "pix", None), P("shell", "pix", None), P("shell", "pix", None)),
        check_vma=False,
    )
```

profile of v0, /device:TPU:1, one launch (start us, length us, event | category | flops | bytes accessed | tf_op | source)
XLA Modules:
  0.0 267.1 jit_solution(12473461303227991477)
XLA Ops:
  0.6 3.9 %collective-permute-start.1 = (s32[2,1024]{1,0:T(2,128)}, s32[2,1024]{1,0:T(2,128)S(1)}, u32[]{:S(2)}, u32[]{:S(2)}) collective-permute-start(s32[2,1024]{1,0:T(2,128)} %param.15), channel_id=1, source_target_pairs={{0,16},{1,17},{2,18},{3,19},{4,20},{5,21},{6,22},{7,23},{8,24},{9,... | collective-permute-start | bytes 24584 | tf_op jit(solution)/shard_map/ppermute | solution.py:555
  4.6 0.8 reshape.212
  5.4 1.0 convert_element_type.4
  6.4 0.0 copy-start.7
  6.4 0.0 copy-start.8
  6.4 0.0 copy-start.9
  6.4 0.1 reshape.213
  6.5 1.0 reshape.220
  7.5 0.1 pad_maximum_fusion.list_ref
  7.6 0.0 collective-permute-done.1
  7.6 0.1 reshape.216
  7.7 0.8 select_reduce_fusion
  8.6 3.5 %shard_map.166 = (f32[16,72,128]{2,1,0:T(8,128)}, f32[16,72,128]{2,1,0:T(8,128)}) custom-call(s32[2,64]{1,0:T(2,128)S(1)} %bitcast.3, f32[2,64,8,128]{3,2,1,0:T(8,128)S(1)} %pad_maximum_fusion.list_ref), custom_call_target="tpu_custom_call" | custom-call | flops 1048576 | bytes 4194304 | tf_op jit(solution)/shard_map/pallas_call | solution.py:561
  12.1 6.8 %all-to-all-start.1 = ((f32[16,72,128]{2,1,0:T(8,128)}), f32[16,72,128]{2,1,0:T(8,128)S(1)}, u32[]{:S(2)}, u32[]{:S(2)}) async-start(f32[16,72,128]{2,1,0:T(8,128)} %get-tuple-element.10), calls=%async_computation.1 | async-start | bytes 1179648 | tf_op jit(solution)/shard_map/all_to_all | solution.py:573
  18.9 0.0 copy-done.7
  18.9 0.0 copy-done.8
  18.9 0.1 pad_maximum_fusion.3
  19.0 2.4 collective-permute-start
  21.4 0.7 collective-permute-done
  22.1 0.1 broadcast_select_fusion
  22.2 0.0 copy-done.9
  22.2 0.1 compare_select_fusion.1
  22.2 11.9 %all-to-all-done.1.in_ref = f32[16,72,128]{2,1,0:T(8,128)S(1)} async-done(((f32[16,72,128]{2,1,0:T(8,128)}), f32[16,72,128]{2,1,0:T(8,128)S(1)}, u32[]{:S(2)}, u32[]{:S(2)}) %all-to-all-start.1) | async-done | bytes 589856 | tf_op jit(solution)/shard_map/all_to_all | solution.py:573
  34.1 4.7 %all-to-all-start = ((f32[16,72,128]{2,1,0:T(8,128)}), f32[16,72,128]{2,1,0:T(8,128)S(1)}, u32[]{:S(2)}, u32[]{:S(2)}) async-start(f32[16,72,128]{2,1,0:T(8,128)} %get-tuple-element.9), calls=%async_computation | async-start | bytes 1179648 | tf_op jit(solution)/shard_map/all_to_all | solution.py:573
  38.7 0.1 pad_maximum_fusion.1.mix_ref
  38.8 1.2 select_reduce_fusion.2
  40.1 0.1 squeeze.22.place_ref
  40.1 0.1 squeeze.21.place_ref
  40.2 2.4 collective-permute-start.3
  42.7 0.1 squeeze.20.place_ref
  42.8 0.1 squeeze.18.place_ref
  42.9 11.0 %all-to-all-done.in_ref = f32[16,72,128]{2,1,0:T(8,128)S(1)} async-done(((f32[16,72,128]{2,1,0:T(8,128)}), f32[16,72,128]{2,1,0:T(8,128)S(1)}, u32[]{:S(2)}, u32[]{:S(2)}) %all-to-all-start) | async-done | bytes 589856 | tf_op jit(solution)/shard_map/all_to_all | solution.py:573
  53.9 2.4 collective-permute-start.2
  56.4 7.2 %shard_map.168.near1 = f32[128,16,128]{2,1,0:T(8,128)S(1)} custom-call(s32[128]{0:T(128)S(1)} %squeeze.20.place_ref, f32[16,72,128]{2,1,0:T(8,128)S(1)} %all-to-all-done.1.in_ref), custom_call_target="tpu_custom_call" | custom-call | flops 2147483648 | bytes 4194304 | tf_op jit(solution)/shard_map/pallas_call | solution.py:564
  63.5 7.2 %shard_map.167.near0 = f32[128,16,128]{2,1,0:T(8,128)S(1)} custom-call(s32[128]{0:T(128)S(1)} %squeeze.18.place_ref, f32[16,72,128]{2,1,0:T(8,128)S(1)} %all-to-all-done.in_ref), custom_call_target="tpu_custom_call" | custom-call | flops 2147483648 | bytes 4194304 | tf_op jit(solution)/shard_map/pallas_call | solution.py:564
  70.7 0.0 collective-permute-done.3.in_ref
  70.7 7.2 %shard_map.170.far1 = f32[128,16,128]{2,1,0:T(8,128)S(1)} custom-call(s32[128]{0:T(128)S(1)} %squeeze.22.place_ref, f32[16,72,128]{2,1,0:T(8,128)S(1)} %collective-permute-done.3.in_ref), custom_call_target="tpu_custom_call" | custom-call | flops 2147483648 | bytes 4194304 | tf_op jit(solution)/shard_map/pallas_call | solution.py:564
  78.0 0.0 copy-start.1
  78.0 0.0 collective-permute-done.2.in_ref
  78.0 7.2 %shard_map.169.far0 = f32[128,16,128]{2,1,0:T(8,128)S(1)} custom-call(s32[128]{0:T(128)S(1)} %squeeze.21.place_ref, f32[16,72,128]{2,1,0:T(8,128)S(1)} %collective-permute-done.2.in_ref), custom_call_target="tpu_custom_call" | custom-call | flops 2147483648 | bytes 4194304 | tf_op jit(solution)/shard_map/pallas_call | solution.py:564
  85.2 0.0 copy-done.1
  85.2 6.2 %shard_map.171 = (f32[2,128,2048]{2,1,0:T(8,128)}, f32[8,2,2,128,128]{4,3,2,1,0:T(8,128)}) custom-call(f32[2,4]{1,0:T(2,128)S(1)} %pad_maximum_fusion.1.mix_ref, f32[128,16,128]{2,1,0:T(8,128)S(1)} %shard_map.167.near0, f32[128,16,128]{2,1,0:T(8,128)S(1)} %shard_map.168.near1, f32[128,16,128]{2,1,0:T(8,128)S(1)} %shard_map.169.far0, ...), custom_call_target="tpu_custom_call" | custom-call | flops 1073741824 | bytes 4194304 | tf_op jit(solution)/shard_map/pallas_call | solution.py:584
  91.5 0.0 copy-start.6
  91.5 5.1 %all-to-all-start.2 = ((f32[16,2,128,128]{3,2,1,0:T(8,128)}), f32[16,2,128,128]{3,2,1,0:T(8,128)S(1)}, u32[]{:S(2)}, u32[]{:S(2)}) async-start(f32[16,2,128,128]{3,2,1,0:T(8,128)} %bitcast.5), calls=%async_computation.2 | async-start | bytes 4194304 | tf_op jit(solution)/shard_map/all_to_all | solution.py:591
  96.5 0.0 copy-start.2
  96.5 0.0 copy-start.3
  96.5 0.0 copy-start.4
  96.6 0.8 compare_select_fusion
  97.4 40.7 %all-to-all-done.2.in_ref = f32[16,2,128,128]{3,2,1,0:T(8,128)S(1)} async-done(((f32[16,2,128,128]{3,2,1,0:T(8,128)}), f32[16,2,128,128]{3,2,1,0:T(8,128)S(1)}, u32[]{:S(2)}, u32[]{:S(2)}) %all-to-all-start.2) | async-done | bytes 2097184 | tf_op jit(solution)/shard_map/all_to_all | solution.py:591
  138.0 0.0 copy-start.5
  138.1 1.1 broadcast_in_dim.93.twr_ref
  139.1 0.0 copy-done.6
  139.1 0.3 broadcast_in_dim.94.twi_ref
  139.5 0.0 copy-done.2
  139.5 0.0 copy-done.3
  139.5 0.0 copy-done.4
  139.5 0.0 copy-done.5
  139.5 13.8 %shard_map.172 = f32[16,2,2,128,128]{4,3,2,1,0:T(8,128)} custom-call(f32[16,2,128,128]{3,2,1,0:T(8,128)S(1)} %all-to-all-done.2.in_ref, f32[2,128]{1,0:T(2,128)S(1)} %pad_maximum_fusion.2.col_ref, f32[16,128,128]{2,1,0:T(8,128)S(1)} %broadcast_in_dim.93.twr_ref, f32[16,128,128]{2,1,0:T(8,128)S(1)} %broadcast_in_dim.94.twi_ref, ...), custom_call_target="tpu_custom_call" | custom-call | flops 2147483648 | bytes 4194304 | tf_op jit(solution)/shard_map/pallas_call | solution.py:604
  153.3 0.0 copy-start
  153.3 103.5 %all_to_all.20 = f32[16,2,2,128,128]{4,3,2,1,0:T(8,128)} all-to-all(f32[16,2,2,128,128]{4,3,2,1,0:T(8,128)} %shard_map.172), channel_id=1, replica_groups=mesh['shell'=2,'pix'=16] {'pix'}, dimensions={0} | all-to-all | bytes 8388608 | tf_op jit(solution)/shard_map/all_to_all | solution.py:612
  256.9 0.0 copy-done
  256.9 10.2 %shard_map.173 = (f32[2,128,2048]{2,1,0:T(8,128)}, f32[2,128,2048]{2,1,0:T(8,128)}) custom-call(f32[8,2,2,2,128,128]{5,4,3,2,1,0:T(8,128)} %bitcast.4, bf16[8,256,256]{2,1,0:T(8,128)(2,1)S(1)} %copy-done.1, bf16[8,256,256]{2,1,0:T(8,128)(2,1)S(1)} %copy-done), custom_call_target="tpu_custom_call" | custom-call | flops 2147483648 | bytes 4194304 | tf_op jit(solution)/shard_map/pallas_call | solution.py:613
  (11 shorter events, 0.1 us)
Async XLA Ops:
  0.6 7.0 %collective-permute-start.1 = (s32[2,1024]{1,0:T(2,128)}, s32[2,1024]{1,0:T(2,128)S(1)}, u32[]{:S(2)}, u32[]{:S(2)}) collective-permute-start(s32[2,1024]{1,0:T(2,128)} %param.15), channel_id=1, source_target_pairs={{0,16},{1,17},{2,18},{3,19},{4,20},{5,21},{6,22},{7,23},{8,24},{9,... | collective-permute-start | bytes 24584 | tf_op jit(solution)/shard_map/ppermute | solution.py:555
  6.4 12.5 %copy-start.7 = (f32[2]{0:T(128)S(1)}, f32[2]{0:T(128)}, u32[]{:S(2)}) copy-start(f32[2]{0:T(128)} %param.19) | copy-start | bytes 28
  6.4 12.5 %copy-start.8 = (f32[2]{0:T(128)S(1)}, f32[2]{0:T(128)}, u32[]{:S(2)}) copy-start(f32[2]{0:T(128)} %param.18) | copy-start | bytes 28
  6.4 15.8 %copy-start.9 = (f32[2]{0:T(128)S(1)}, f32[2]{0:T(128)}, u32[]{:S(2)}) copy-start(f32[2]{0:T(128)} %param.20) | copy-start | bytes 28
  12.1 22.0 %all-to-all-start.1 = ((f32[16,72,128]{2,1,0:T(8,128)}), f32[16,72,128]{2,1,0:T(8,128)S(1)}, u32[]{:S(2)}, u32[]{:S(2)}) async-start(f32[16,72,128]{2,1,0:T(8,128)} %get-tuple-element.10), calls=%async_computation.1 | async-start | bytes 1179648 | tf_op jit(solution)/shard_map/all_to_all | solution.py:573
  19.0 3.1 %collective-permute-start = (f32[4]{0:T(128)S(1)}, f32[4]{0:T(128)S(1)}, u32[]{:S(2)}, u32[]{:S(2)}) collective-permute-start(f32[4]{0:T(128)S(1)} %pad_maximum_fusion.3), channel_id=1, source_target_pairs={{0,16},{1,17},{2,18},{3,19},{4,20},{5,21},{6,22},{7,23},{8,24},{9,... | collective-permute-start | bytes 56 | tf_op jit(solution)/shard_map/ppermute | solution.py:535
  34.1 19.8 %all-to-all-start = ((f32[16,72,128]{2,1,0:T(8,128)}), f32[16,72,128]{2,1,0:T(8,128)S(1)}, u32[]{:S(2)}, u32[]{:S(2)}) async-start(f32[16,72,128]{2,1,0:T(8,128)} %get-tuple-element.9), calls=%async_computation | async-start | bytes 1179648 | tf_op jit(solution)/shard_map/all_to_all | solution.py:573
  40.2 30.5 %collective-permute-start.3 = (f32[16,72,128]{2,1,0:T(8,128)S(1)}, f32[16,72,128]{2,1,0:T(8,128)S(1)}, u32[]{:S(2)}, u32[]{:S(2)}) collective-permute-start(f32[16,72,128]{2,1,0:T(8,128)S(1)} %all-to-all-done.1.in_ref), channel_id=1, source_target_pairs={{0,16},{1,17},{2,18},{3,19},{4,20},{5,21},{6,22},{7,23},{8,24},{9,... | collective-permute-start | bytes 1769480 | tf_op jit(solution)/shard_map/ppermute | solution.py:574
  53.9 24.1 %collective-permute-start.2 = (f32[16,72,128]{2,1,0:T(8,128)S(1)}, f32[16,72,128]{2,1,0:T(8,128)S(1)}, u32[]{:S(2)}, u32[]{:S(2)}) collective-permute-start(f32[16,72,128]{2,1,0:T(8,128)S(1)} %all-to-all-done.in_ref), channel_id=1, source_target_pairs={{0,16},{1,17},{2,18},{3,19},{4,20},{5,21},{6,22},{7,23},{8,24},{9,... | collective-permute-start | bytes 1769480 | tf_op jit(solution)/shard_map/ppermute | solution.py:574
  78.0 7.3 %copy-start.1 = (bf16[8,256,256]{2,1,0:T(8,128)(2,1)S(1)}, bf16[8,256,256]{2,1,0:T(8,128)(2,1)}, u32[]{:S(2)}) copy-start(bf16[8,256,256]{2,1,0:T(8,128)(2,1)} %constant.100.clone.high_ref) | copy-start | bytes 3145732
  91.5 47.7 %copy-start.6 = (f32[16,128]{1,0:T(8,128)S(1)}, f32[16,128]{1,0:T(8,128)}, u32[]{:S(2)}) copy-start(f32[16,128]{1,0:T(8,128)} %constant.104.clone) | copy-start | bytes 24580
  91.5 46.6 %all-to-all-start.2 = ((f32[16,2,128,128]{3,2,1,0:T(8,128)}), f32[16,2,128,128]{3,2,1,0:T(8,128)S(1)}, u32[]{:S(2)}, u32[]{:S(2)}) async-start(f32[16,2,128,128]{3,2,1,0:T(8,128)} %bitcast.5), calls=%async_computation.2 | async-start | bytes 4194304 | tf_op jit(solution)/shard_map/all_to_all | solution.py:591
  96.5 42.9 %copy-start.2 = (bf16[256,256]{1,0:T(8,128)(2,1)S(1)}, bf16[256,256]{1,0:T(8,128)(2,1)}, u32[]{:S(2)}) copy-start(bf16[256,256]{1,0:T(8,128)(2,1)} %constant.108.clone.back_low_ref) | copy-start | bytes 393220
  96.5 42.9 %copy-start.3 = (bf16[256,256]{1,0:T(8,128)(2,1)S(1)}, bf16[256,256]{1,0:T(8,128)(2,1)}, u32[]{:S(2)}) copy-start(bf16[256,256]{1,0:T(8,128)(2,1)} %constant.107.clone.back_high_ref) | copy-start | bytes 393220
  96.5 42.9 %copy-start.4 = (bf16[256,256]{1,0:T(8,128)(2,1)S(1)}, bf16[256,256]{1,0:T(8,128)(2,1)}, u32[]{:S(2)}) copy-start(bf16[256,256]{1,0:T(8,128)(2,1)} %constant.106.clone.low_ref) | copy-start | bytes 393220
  138.0 1.4 copy-start.5
  153.3 103.5 %copy-start = (bf16[8,256,256]{2,1,0:T(8,128)(2,1)S(1)}, bf16[8,256,256]{2,1,0:T(8,128)(2,1)}, u32[]{:S(2)}) copy-start(bf16[8,256,256]{2,1,0:T(8,128)(2,1)} %constant.101.clone.low_ref) | copy-start | bytes 3145732
where the time goes:
time: 268 us; the launch traced here: 267 us
  blocking collectives  104 us (39%)
  waiting for transfers between devices  64.3 us (24%)
  Pallas kernels  62.6 us (23%)
  starting transfers between devices  27.7 us (10%)
  other arithmetic  4.26 us (2%)
  local copies, waits for them, and re-layouts  3.75 us (1%)
    all_to_all x1, blocking collectives, local_fast(): lax.all_to_all(leaving, 'pix', split_axis=0, concat_axis=0, tiled=True)  104 us
    all_to_all x1, waiting for transfers between devices, local_fast(): lax.all_to_all(sending.reshape(groups, 2, slab, INNER), 'pix', split_axis...  40.7 us
    pallas_call x4, Pallas kernels, local_fast(): call(partial(assemble_kernel, 2 * half), shape(per_owner, TR, TC), [pltpu...  28.8 us
    all_to_all x2, waiting for transfers between devices, local_fast(): lax.all_to_all(outgoing[p], 'pix', split_axis=0, concat_axis=0, tiled=True)  22.9 us
    pallas_call x1, Pallas kernels, local_fast(): call(column_kernel, shape(groups, 2, 2, slab, INNER), [pltpu.VMEM((OUTER,...  13.8 us
    all_to_all x2, starting transfers between devices, local_fast(): lax.all_to_all(outgoing[p], 'pix', split_axis=0, concat_axis=0, tiled=True)  11.5 us
    pallas_call x1, Pallas kernels, local_fast(): call(row_inverse_kernel, [shape(planes, slab, L)] * 2, [pltpu.VMEM((HALF_...  10.2 us
    pallas_call x1, Pallas kernels, local_fast(): call(row_forward_kernel, [shape(planes, slab, L), shape(HALF_BLOCKS, plan...  6.23 us
  transfers between devices with their start and end apart: 7, of which 4 were waited for; matrix products, arithmetic and copies ran while one was open for 2% of the time, Pallas kernels for 8%

commit v1 on v0

--- a/solution.py
+++ b/solution.py
@@ -227,6 +227,8 @@
 INNER = 128
 OUTER = L // INNER
 HALF_BLOCKS = OUTER // 2
+CHUNKS = 4
+MESH = pl.DeviceIdType.MESH
 
 
 def block_columns():
@@ -333,177 +335,358 @@
         lax.fori_loop(0, tiles, tile, 0)
 
 
-def assemble_kernel(size, place_ref, in_ref, out_ref, held):
-    groups, rows, _ = in_ref.shape
+def assemble_kernel(size, mix_ref, *refs):
+    count = (len(refs) - 2) // 2
+    places, lists = refs[:count], refs[count : 2 * count]
+    conv_ref, held = refs[2 * count :]
+    groups, rows, _ = lists[0].shape
     cap = rows // size - 1
-    tiles = out_ref.shape[0]
+    tiles = held.shape[1] - 1
     half = size // 2
     held[...] = jnp.zeros_like(held)
-    total = in_ref[0, cap * size : cap * size + 1, 0:1]
-    for s in range(1, groups):
-        total = total + in_ref[s, cap * size : cap * size + 1, 0:1]
-    row_id = lax.broadcasted_iota(jnp.int32, (TR, TC), 0)
-    col_id = lax.broadcasted_iota(jnp.int32, (TC, TC), 0)
-
-    def source(s, _):
-        for c in range(cap):
-            at = place_ref[s * cap + c]
-            entry = in_ref[s, c * size : (c + 1) * size, :]
-            cells = entry[:half].astype(jnp.int32)
-            row_hot, col_hot = [], []
-            for i in range(half):
-                cell = cells[i : i + 1]
-                row_hot.append(jnp.where(row_id == cell // TC, entry[half + i : half + i + 1], 0.0))
-                col_hot.append(jnp.where(col_id == cell % TC, 1.0, 0.0))
-            held[at] = held[at] + lax.dot_general(
-                jnp.concatenate(row_hot, axis=1).astype(jnp.bfloat16),
-                jnp.concatenate(col_hot, axis=1).astype(jnp.bfloat16),
-                (((1,), (1,)), ((), ())),
-                preferred_element_type=jnp.float32,
-            )
-        return 0
-
-    lax.fori_loop(0, groups, source, 0)
-    factor = jnp.where(total > 0.0, (L * L) / total, 0.0)
-    out_ref[...] = held[0:tiles] * factor[None] - 1.0
-
-
-def row_forward_kernel(mix_ref, near0, near1, far0, far1, high_ref, low_ref, conv_ref, out_ref, held):
-    tile_rows = near0.shape[0] // OUTER
+    as_small = lambda ids: ids.astype(jnp.float32).astype(jnp.bfloat16)
+    row_id = as_small(lax.broadcasted_iota(jnp.int32, (TR, TC), 0))
+    col_id = as_small(lax.broadcasted_iota(jnp.int32, (TC, TC), 0))
+    one, zero = jnp.ones((), jnp.bfloat16), jnp.zeros((), jnp.bfloat16)
+    factors = []
+    for q in range(count):
+        place_ref, in_ref = places[q], lists[q]
+
+        def source(s, _):
+            for c in range(cap):
+                at = place_ref[s * cap + c]
+                entry = in_ref[s, c * size : (c + 1) * size, :]
+                cells = entry[:half].astype(jnp.int32)
+                cell_rows, cell_cols = as_small(cells // TC), as_small(cells % TC)
+                weights = entry[half:].astype(jnp.bfloat16)
+                row_hot, col_hot = [], []
+                for i in range(half):
+                    row_hot.append(jnp.where(row_id == cell_rows[i : i + 1], weights[i : i + 1], zero))
+                    col_hot.append(jnp.where(col_id == cell_cols[i : i + 1], one, zero))
+                held[q, at] = held[q, at] + lax.dot_general(
+                    jnp.concatenate(row_hot, axis=1),
+                    jnp.concatenate(col_hot, axis=1),
+                    (((1,), (1,)), ((), ())),
+                    preferred_element_type=jnp.float32,
+                )
+            return 0
+
+        lax.fori_loop(0, groups, source, 0)
+        total = in_ref[0, cap * size : cap * size + 1, 0:1]
+        for s in range(1, groups):
+            total = total + in_ref[s, cap * size : cap * size + 1, 0:1]
+        factors.append((L * L) / total)
 
     def chunk(t, _):
         rows = pl.ds(pl.multiple_of(t * TR, TR), TR)
-        packed = []
         for n in range(OUTER):
             at = t * OUTER + n
-            fields = (near0[at], near1[at], far0[at], far1[at])
-            pair = []
-            for i in range(2):
+            fields = [held[q, at] * factors[q] - 1.0 for q in range(count)]
+            for i in range(conv_ref.shape[0]):
                 value = mix_ref[i, 0] * fields[0]
-                for j in range(1, 4):
+                for j in range(1, count):
                     value = value + mix_ref[i, j] * fields[j]
                 conv_ref[i, rows, n * INNER : (n + 1) * INNER] = value
-                pair.append(value)
-            packed.append(tuple(pair))
-        z = fft_list(packed, -1)
-        for k in range(1, HALF_BLOCKS):
-            (ar, ai), (br, bi) = z[k], z[OUTER - k]
-            held[k - 1, 0, rows, :INNER] = 0.5 * (ar + br)
-            held[k - 1, 0, rows, INNER:] = 0.5 * (ai - bi)
-            held[k - 1, 1, rows, :INNER] = 0.5 * (ai + bi)
-            held[k - 1, 1, rows, INNER:] = 0.5 * (br - ar)
-        for p in range(2):
-            held[HALF_BLOCKS - 1, p, rows, :INNER] = z[0][p]
-            held[HALF_BLOCKS - 1, p, rows, INNER:] = z[HALF_BLOCKS][p]
         return 0
 
-    lax.fori_loop(0, tile_rows, chunk, 0)
-
-    def block(b, _):
-        slab = tile_rows * TR
-        value = held[b].reshape(2 * slab, 2 * INNER)
-        result = three_pass(split_value(value), (high_ref[b], low_ref[b]), ((1,), (0,)))
-        for p in range(2):
-            for half in range(2):
-                out_ref[b, p, half] = result[
-                    p * slab : (p + 1) * slab, half * INNER : (half + 1) * INNER
-                ]
+    lax.fori_loop(0, tiles // OUTER, chunk, 0)
+
+
+def signal_all(peers):
+    barrier = pltpu.get_barrier_semaphore()
+    for peer in peers:
+        pl.semaphore_signal(barrier, inc=1, device_id=peer, device_id_type=MESH)
+    pl.semaphore_wait(barrier, len(peers))
+
+
+def swap_lists_kernel(*refs):
+    planes = (len(refs) - 5) // 3
+    out_refs, in_refs, far_refs = refs[:planes], refs[planes : 2 * planes], refs[2 * planes : 3 * planes]
+    send, recv, pass_send, pass_recv, own_sem = refs[3 * planes :]
+    groups = out_refs[0].shape[0]
+    me, shell = lax.axis_index("pix"), lax.axis_index("shell")
+    signal_all([{"pix": (me + o) % groups} for o in range(1, groups)] + [{"shell": 1 - shell}])
+
+    def direct(p, o):
+        to = (me + o) % groups
+        return pltpu.make_async_remote_copy(
+            src_ref=out_refs[p].at[to],
+            dst_ref=in_refs[p].at[me],
+            send_sem=send.at[p, o],
+            recv_sem=recv.at[p, o],
+            device_id={"pix": to},
+            device_id_type=MESH,
+        )
+
+    def landing(p, o):
+        source = (me + groups - o) % groups
+        return pltpu.make_async_remote_copy(
+            src_ref=out_refs[p].at[source],
+            dst_ref=in_refs[p].at[source],
+            send_sem=send.at[p, o],
+            recv_sem=recv.at[p, o],
+            device_id={"pix": source},
+            device_id_type=MESH,
+        )
+
+    def onward(p, o):
+        source = (me + groups - o) % groups
+        return pltpu.make_async_remote_copy(
+            src_ref=in_refs[p].at[source],
+            dst_ref=far_refs[p].at[source],
+            send_sem=pass_send.at[p, o],
+            recv_sem=pass_recv.at[p, o],
+            device_id={"shell": 1 - shell},
+            device_id_type=MESH,
+        )
+
+    def own(p):
+        return pltpu.make_async_copy(out_refs[p].at[me], in_refs[p].at[me], own_sem.at[p])
+
+    for p in range(planes):
+        for j in range(1, groups):
+            direct(p, (j + groups // 2 - 1) % (groups - 1) + 1).start()
+        own(p).start()
+    for p in range(planes):
+        own(p).wait()
+        onward(p, 0).start()
+        for j in range(1, groups):
+            o = (j + groups // 2 - 1) % (groups - 1) + 1
+            landing(p, o).wait_recv()
+            onward(p, o).start()
+    for p in range(planes):
+        for o in range(groups):
+            onward(p, o).wait()
+            if o:
+                direct(p, o).wait_send()
+
+
+def shear_kernel(
+    conv_ref, col_ref, twr_ref, twi_ref, high_ref, low_ref, colh_ref, coll_ref, backh_ref, backl_ref,
+    one_ref, two_ref, held_row, sending, arrived, held, twist_in, kern, back, leaving, landed, held_inv,
+    fsend, frecv, rsend, rrecv,
+):
+    groups, _, slab, _ = sending.shape
+    span = held_row.shape[2]
+    chunks = slab // span
+    me = lax.axis_index("pix")
+    signal_all([{"pix": (me + o) % groups} for o in range(1, groups)])
+
+    def rows_of(c):
+        return pl.ds(pl.multiple_of(c * span, span), span)
+
+    def go_copy(c, o, peer, slot):
+        return pltpu.make_async_remote_copy(
+            src_ref=sending.at[peer, :, rows_of(c), :],
+            dst_ref=arrived.at[slot, :, rows_of(c), :],
+            send_sem=fsend.at[c, o],
+            recv_sem=frecv.at[c, o],
+            device_id={"pix": peer},
+            device_id_type=MESH,
+        )
+
+    def back_copy(f, c, o, peer, slot):
+        return pltpu.make_async_remote_copy(
+            src_ref=leaving.at[peer, f, :, rows_of(c), :],
+            dst_ref=landed.at[slot, f, :, rows_of(c), :],
+            send_sem=rsend.at[f, c, o],
+            recv_sem=rrecv.at[f, c, o],
+            device_id={"pix": peer},
+            device_id_type=MESH,
+        )
+
+    def to_peer(o):
+        return (me + o) % groups
+
+    def from_peer(o):
+        return (me + groups - o) % groups
+
+    def each_peer(action):
+        def step(j, _):
+            action((j + groups // 2 - 1) % (groups - 1) + 1)
+            return 0
+
+        lax.fori_loop(1, groups, step, 0)
+
+    def forward_rows(c, _):
+        def radix(t, _):
+            rows = pl.ds(pl.multiple_of(c * span + t * 8, 8), 8)
+            near = pl.ds(pl.multiple_of(t * 8, 8), 8)
+            z = fft_list(
+                [
+                    tuple(conv_ref[i, rows, n * INNER : (n + 1) * INNER] for i in range(2))
+                    for n in range(OUTER)
+                ],
+                -1,
+            )
+            for k in range(1, HALF_BLOCKS):
+                (ar, ai), (br, bi) = z[k], z[OUTER - k]
+                held_row[k - 1, 0, near, :INNER] = 0.5 * (ar + br)
+                held_row[k - 1, 0, near, INNER:] = 0.5 * (ai - bi)
+                held_row[k - 1, 1, near, :INNER] = 0.5 * (ai + bi)
+                held_row[k - 1, 1, near, INNER:] = 0.5 * (br - ar)
+            for p in range(2):
+                held_row[HALF_BLOCKS - 1, p, near, :INNER] = z[0][p]
+                held_row[HALF_BLOCKS - 1, p, near, INNER:] = z[HALF_BLOCKS][p]
+            return 0
+
+        lax.fori_loop(0, span // 8, radix, 0)
+
+        def block(j, _):
+            b = (me // 2 + 1 + j) % HALF_BLOCKS
+            value = held_row[b].reshape(2 * span, 2 * INNER)
+            result = three_pass(split_value(value), (high_ref[b], low_ref[b]), ((1,), (0,)))
+            for p in range(2):
+                for half in range(2):
+                    sending[2 * b + p, half, rows_of(c), :] = result[
+                        p * span : (p + 1) * span, half * INNER : (half + 1) * INNER
+                    ]
+            return 0
+
+        lax.fori_loop(0, HALF_BLOCKS, block, 0)
+        each_peer(lambda o: go_copy(c, o, to_peer(o), me).start())
+        for half in range(2):
+            arrived[me, half, rows_of(c), :] = sending[me, half, rows_of(c), :]
         return 0
 
-    lax.fori_loop(0, HALF_BLOCKS, block, 0)
-
-
-def column_kernel(in_ref, col_ref, twr_ref, twi_ref, high_ref, low_ref, back_high_ref, back_low_ref, out_ref, held, *back):
-    def twist_of(k, rows):
-        return twr_ref[k, rows, :], twi_ref[k, rows, :]
-
-    def forward(t, _):
-        rows = pl.ds(pl.multiple_of(t * 8, 8), 8)
-        z = fft_list([(in_ref[n, 0, rows, :], in_ref[n, 1, rows, :]) for n in range(OUTER)], -1)
-        for k in range(OUTER):
-            re, im = z[k]
-            if k:
-                c, s = twist_of(k, rows)
-                re, im = re * c - im * s, re * s + im * c
-            held[k, 0, rows, :] = re
-            held[k, 1, rows, :] = im
-        return 0
-
-    lax.fori_loop(0, INNER // 8, forward, 0)
+    lax.fori_loop(0, chunks, forward_rows, 0)
+
     signed_v = col_ref[0:1]
     weight = col_ref[1:2]
     inner_id = lax.broadcasted_iota(jnp.int32, (INNER, INNER), 0)
 
-    def middle(k, _):
-        value = held[k].reshape(2 * INNER, INNER)
-        spectrum = three_pass((high_ref[...], low_ref[...]), split_value(value), ((1,), (0,)))
+    def prepare(k, _):
+        for i, ref in enumerate((twr_ref, twi_ref)):
+            twist_in[i, k] = jnp.broadcast_to(ref[pl.ds(k, 1), :], (INNER, INNER)).T
         u = k + OUTER * inner_id
         signed_u = jnp.where(u >= L // 2, u - L, u).astype(jnp.float32)
         scale = jnp.where(u == L // 2, 0.0, weight)
         uu, vv = signed_u * signed_u, signed_v * signed_v
         over = scale / jnp.maximum(uu + vv, 1.0)
-        kernels = ((vv - uu) * over, 2.0 * signed_v * signed_u * over)
+        kern[0, k] = (vv - uu) * over
+        kern[1, k] = 2.0 * signed_v * signed_u * over
+        return 0
+
+    lax.fori_loop(0, OUTER, prepare, 0)
+
+    def forward_columns(c, _):
+        each_peer(lambda o: go_copy(c, o, from_peer(o), from_peer(o)).wait_recv())
+
+        def radix(t, _):
+            rows = pl.ds(pl.multiple_of(c * span + t * 8, 8), 8)
+            z = fft_list([(arrived[n, 0, rows, :], arrived[n, 1, rows, :]) for n in range(OUTER)], -1)
+            for k in range(OUTER):
+                re, im = z[k]
+                if k:
+                    cs, sn = twist_in[0, k, rows, :], twist_in[1, k, rows, :]
+                    re, im = re * cs - im * sn, re * sn + im * cs
+                held[k, 0, rows, :] = re
+                held[k, 1, rows, :] = im
+            return 0
+
+        lax.fori_loop(0, span // 8, radix, 0)
+        return 0
+
+    lax.fori_loop(0, chunks, forward_columns, 0)
+
+    def middle(j, _):
+        pair = jnp.concatenate([held[2 * j + i].reshape(2 * INNER, INNER) for i in range(2)], axis=1)
+        spectrum = three_pass((colh_ref[...], coll_ref[...]), split_value(pair), ((1,), (0,)))
+        for i in range(2):
+            k = 2 * j + i
+            mine = spectrum[:, i * INNER : (i + 1) * INNER]
+            fields = jnp.concatenate(
+                [
+                    jnp.concatenate([mine[:INNER] * kern[f, k], mine[INNER:] * kern[f, k]], axis=0)
+                    for f in range(2)
+                ],
+                axis=1,
+            )
+            result = three_pass((backh_ref[...], backl_ref[...]), split_value(fields), ((1,), (0,)))
+            cs, sn = twist_in[0, k], twist_in[1, k]
+            for f in range(2):
+                at = slice(f * INNER, (f + 1) * INNER)
+                re, im = result[:INNER, at], result[INNER:, at]
+                back[f, k, 0] = re * cs + im * sn
+                back[f, k, 1] = im * cs - re * sn
+        return 0
+
+    lax.fori_loop(0, OUTER // 2, middle, 0)
+
+    def inverse_columns(q, _):
+        f, c = q // chunks, q % chunks
+
+        def radix(t, _):
+            rows = pl.ds(pl.multiple_of(c * span + t * 8, 8), 8)
+            x = fft_list([(back[f, k, 0, rows, :], back[f, k, 1, rows, :]) for k in range(OUTER)], 1)
+            for n in range(OUTER):
+                leaving[n, f, 0, rows, :] = x[n][0]
+                leaving[n, f, 1, rows, :] = x[n][1]
+            return 0
+
+        lax.fori_loop(0, span // 8, radix, 0)
+        each_peer(lambda o: back_copy(f, c, o, to_peer(o), me).start())
+        for part in range(2):
+            landed[me, f, part, rows_of(c), :] = leaving[me, f, part, rows_of(c), :]
+        return 0
+
+    lax.fori_loop(0, 2 * chunks, inverse_columns, 0)
+
+    for f, out_ref in enumerate((one_ref, two_ref)):
+
+        def inverse_rows(c, _):
+            each_peer(lambda o: back_copy(f, c, o, from_peer(o), from_peer(o)).wait_recv())
+
+            def block(b, _):
+                value = jnp.concatenate(
+                    [
+                        jnp.concatenate(
+                            [landed[2 * b + p, f, part, rows_of(c), :] for part in range(2)], axis=1
+                        )
+                        for p in range(2)
+                    ],
+                    axis=0,
+                )
+                held_inv[b] = three_pass(
+                    split_value(value), (high_ref[b], low_ref[b]), ((1,), (1,))
+                ).reshape(2, span, 2 * INNER)
+                return 0
+
+            lax.fori_loop(0, HALF_BLOCKS, block, 0)
+
+            def radix(t, _):
+                near = pl.ds(pl.multiple_of(t * 8, 8), 8)
+                rows = pl.ds(pl.multiple_of(c * span + t * 8, 8), 8)
+                z = [None] * OUTER
+                last = HALF_BLOCKS - 1
+                z[0] = (held_inv[last, 0, near, :INNER], held_inv[last, 1, near, :INNER])
+                z[HALF_BLOCKS] = (held_inv[last, 0, near, INNER:], held_inv[last, 1, near, INNER:])
+                for k in range(1, HALF_BLOCKS):
+                    ar, ai = held_inv[k - 1, 0, near, :INNER], held_inv[k - 1, 0, near, INNER:]
+                    br, bi = held_inv[k - 1, 1, near, :INNER], held_inv[k - 1, 1, near, INNER:]
+                    z[k] = (ar - bi, ai + br)
+                    z[OUTER - k] = (ar + bi, br - ai)
+                x = fft_list(z, 1)
+                for n in range(OUTER):
+                    for p in range(2):
+                        out_ref[p, rows, n * INNER : (n + 1) * INNER] = x[n][p]
+                return 0
+
+            lax.fori_loop(0, span // 8, radix, 0)
+            return 0
+
+        lax.fori_loop(0, chunks, inverse_rows, 0)
+
+    def drain(c, _):
+        each_peer(lambda o: go_copy(c, o, to_peer(o), me).wait_send())
         for f in range(2):
-            twice = jnp.concatenate([kernels[f], kernels[f]], axis=0)
-            result = three_pass(
-                (back_high_ref[...], back_low_ref[...]), split_value(spectrum * twice), ((1,), (0,))
-            )
-            re, im = result[:INNER], result[INNER:]
-            c, s = twr_ref[k], twi_ref[k]
-            back[f][k, 0] = re * c + im * s
-            back[f][k, 1] = im * c - re * s
+            each_peer(lambda o: back_copy(f, c, o, to_peer(o), me).wait_send())
         return 0
 
-    lax.fori_loop(0, OUTER, middle, 0)
-    for f in range(2):
-
-        def inverse(t, _):
-            rows = pl.ds(pl.multiple_of(t * 8, 8), 8)
-            x = fft_list([(back[f][k, 0, rows, :], back[f][k, 1, rows, :]) for k in range(OUTER)], 1)
-            for n in range(OUTER):
-                out_ref[n, f, 0, rows, :] = x[n][0]
-                out_ref[n, f, 1, rows, :] = x[n][1]
-            return 0
-
-        lax.fori_loop(0, INNER // 8, inverse, 0)
-
-
-def row_inverse_kernel(in_ref, high_ref, low_ref, one_ref, two_ref, held):
-    slab = in_ref.shape[4]
-    for f, out_ref in enumerate((one_ref, two_ref)):
-
-        def block(b, _):
-            value = jnp.concatenate(
-                [jnp.concatenate([in_ref[b, p, f, 0], in_ref[b, p, f, 1]], axis=1) for p in range(2)], axis=0
-            )
-            held[b] = three_pass(split_value(value), (high_ref[b], low_ref[b]), ((1,), (1,))).reshape(
-                2, slab, 2 * INNER
-            )
-            return 0
-
-        lax.fori_loop(0, HALF_BLOCKS, block, 0)
-
-        def chunk(t, _):
-            rows = pl.ds(pl.multiple_of(t * 8, 8), 8)
-            z = [None] * OUTER
-            last = HALF_BLOCKS - 1
-            z[0] = (held[last, 0, rows, :INNER], held[last, 1, rows, :INNER])
-            z[HALF_BLOCKS] = (held[last, 0, rows, INNER:], held[last, 1, rows, INNER:])
-            for k in range(1, HALF_BLOCKS):
-                ar, ai = held[k - 1, 0, rows, :INNER], held[k - 1, 0, rows, INNER:]
-                br, bi = held[k - 1, 1, rows, :INNER], held[k - 1, 1, rows, INNER:]
-                z[k] = (ar - bi, ai + br)
-                z[OUTER - k] = (ar + bi, br - ai)
-            x = fft_list(z, 1)
-            for n in range(OUTER):
-                for p in range(2):
-                    out_ref[p, rows, n * INNER : (n + 1) * INNER] = x[n][p]
-            return 0
-
-        lax.fori_loop(0, slab // 8, chunk, 0)
-
-
-def call(body, outs, scratch=(), smem=(0,), count=1, megabytes=48, flops=0):
+    lax.fori_loop(0, chunks, drain, 0)
+
+
+def call(body, outs, scratch=(), smem=(0,), count=1, megabytes=48, flops=0, group=None):
     space = [
         pl.BlockSpec(memory_space=pltpu.SMEM if i in smem else pltpu.VMEM) for i in range(count)
     ]
@@ -513,7 +696,11 @@
         in_specs=space,
         out_specs=jax.tree.map(lambda _: pl.BlockSpec(memory_space=pltpu.VMEM), outs),
         scratch_shapes=list(scratch),
-        compiler_params=pltpu.CompilerParams(vmem_limit_bytes=megabytes << 20),
+        compiler_params=pltpu.CompilerParams(
+            vmem_limit_bytes=megabytes << 20,
+            collective_id=group,
+            has_side_effects=group is not None,
+        ),
         cost_estimate=pl.CostEstimate(flops=flops, bytes_accessed=4 << 20, transcendentals=0),
     )
 
@@ -561,37 +748,34 @@
     outgoing = call(
         pack_kernel, [shape(groups, (cap + 1) * 2 * half, TC)] * planes, count=2, flops=1 << 20
     )(my_slots, lists)
-    deposit = lambda where, entries: call(
-        partial(assemble_kernel, 2 * half),
-        shape(per_owner, TR, TC),
-        [pltpu.VMEM((per_owner + 1, TR, TC), jnp.float32)],
-        count=2,
-        flops=1 << 31,
-    )(where, entries)
-    near, far = [], []
-    for p in range(planes):
-        incoming = lax.all_to_all(outgoing[p], "pix", split_axis=0, concat_axis=0, tiled=True)
-        passed = lax.ppermute(incoming, "shell", pairs)
-        near.append(deposit(place[p], incoming))
-        far.append(deposit(other_place[p], passed))
+    size = (cap + 1) * 2 * half
+    dma = lambda *dims: pltpu.SemaphoreType.DMA(dims)
+    swapped = call(
+        swap_lists_kernel,
+        [shape(groups, size, TC)] * (2 * planes),
+        [dma(planes, groups)] * 4 + [dma(planes)],
+        smem=(),
+        count=planes,
+        flops=1 << 30,
+        group=0,
+    )(*outgoing)
 
     own = plane_coef[None, :] * (1.0 - source_inv[:, None] * plane_dist[None, :])
     own = jnp.where(jnp.arange(planes)[None, :] <= jnp.arange(planes)[:, None], own, 0.0)
     before = other_coef[None, :] * (1.0 - source_inv[:, None] * other_dist[None, :])
     mix = jnp.concatenate([own, before], axis=1)
 
+    routed = [place[p] for p in range(planes)] + [other_place[p] for p in range(planes)]
+    convergence = call(
+        partial(assemble_kernel, 2 * half),
+        shape(planes, slab, L),
+        [pltpu.VMEM((2 * planes, per_owner + 1, TR, TC), jnp.float32)],
+        smem=tuple(range(2 * planes + 1)),
+        count=4 * planes + 1,
+        flops=1 << 32,
+    )(mix, *routed, *swapped)
+
     row_high, row_low = row_tables()
-    convergence, sending = call(
-        row_forward_kernel,
-        [shape(planes, slab, L), shape(HALF_BLOCKS, planes, 2, slab, INNER)],
-        [pltpu.VMEM((HALF_BLOCKS, planes, slab, 2 * INNER), jnp.float32)],
-        count=7,
-        flops=1 << 30,
-    )(mix, *near, *far, row_high, row_low)
-    arrived = lax.all_to_all(
-        sending.reshape(groups, 2, slab, INNER), "pix", split_axis=0, concat_axis=0, tiled=True
-    )
-
     columns = jnp.asarray(block_columns().astype(np.float32))
     mine = lax.dynamic_index_in_dim(columns, me // planes, axis=0, keepdims=False)
     special = (me // planes == HALF_BLOCKS - 1) & (mine > 0)
@@ -600,24 +784,35 @@
     col_info = jnp.stack([signed, weight])
     col_high, col_low = column_tables()
     tw_real, tw_imag = twiddle_tables()
-    spread = lambda t: jnp.broadcast_to(jnp.asarray(t)[:, :, None], (OUTER, INNER, INNER))
-    leaving = call(
-        column_kernel,
-        shape(groups, 2, 2, slab, INNER),
-        [pltpu.VMEM((OUTER, 2, INNER, INNER), jnp.float32)] * 3,
+    span = slab // CHUNKS
+    vmem = lambda *dims: pltpu.VMEM(dims, jnp.float32)
+    shear_one, shear_two = call(
+        shear_kernel,
+        [shape(planes, slab, L)] * 2,
+        [
+            vmem(HALF_BLOCKS, planes, span, 2 * INNER),
+            vmem(groups, 2, slab, INNER),
+            vmem(groups, 2, slab, INNER),
+            vmem(OUTER, 2, INNER, INNER),
+            vmem(2, OUTER, INNER, INNER),
+            vmem(2, OUTER, INNER, INNER),
+            vmem(2, OUTER, 2, INNER, INNER),
+            vmem(groups, 2, 2, slab, INNER),
+            vmem(groups, 2, 2, slab, INNER),
+            vmem(HALF_BLOCKS, planes, span, 2 * INNER),
+            dma(CHUNKS, groups),
+            dma(CHUNKS, groups),
+            dma(2, CHUNKS, groups),
+            dma(2, CHUNKS, groups),
+        ],
         smem=(),
-        count=8,
-        flops=1 << 31,
-    )(arrived, col_info, spread(tw_real), spread(tw_imag), col_high, col_low, col_high.T.copy(), col_low.T.copy())
-    landed = lax.all_to_all(leaving, "pix", split_axis=0, concat_axis=0, tiled=True)
-    shear_one, shear_two = call(
-        row_inverse_kernel,
-        [shape(planes, slab, L)] * 2,
-        [pltpu.VMEM((HALF_BLOCKS, planes, slab, 2 * INNER), jnp.float32)],
-        smem=(),
-        count=3,
-        flops=1 << 31,
-    )(landed.reshape(HALF_BLOCKS, planes, 2, 2, slab, INNER), row_high, row_low)
+        count=10,
+        flops=1 << 32,
+        group=1,
+    )(
+        convergence, col_info, jnp.asarray(tw_real), jnp.asarray(tw_imag), row_high, row_low,
+        col_high, col_low, col_high.T.copy(), col_low.T.copy(),
+    )
     return convergence, shear_one, shear_two
 
 

time: 268 us -> 251 us (0.937)
  Pallas kernels: 62.6 us -> 233 us
  blocking collectives: 104 us -> 0 us
  waiting for transfers between devices: 64.3 us -> 0.01 us
  starting transfers between devices: 27.7 us -> 5.22 us
    pallas_call x7 -> x3, Pallas kernels: 59.1 us -> 231 us  [the longest x1 162 us: local_fast(): call(shear_kernel, [shape(planes, slab, L)] * 2, [vmem(HALF_BLOCKS, plane...]
    all_to_all x1 -> x0, blocking collectives: 104 us -> none  [local_fast(): lax.all_to_all(leaving, 'pix', split_axis=0, concat_axis=0, tiled=True)]
    all_to_all x3 -> x0, waiting for transfers between devices: 63.6 us -> none  [the longest x1 40.7 us: local_fast(): lax.all_to_all(sending.reshape(groups, 2, slab, INNER), 'pix', split_axis...]
    all_to_all x3 -> x0, starting transfers between devices: 16.5 us -> none  [the longest x2 11.5 us: local_fast(): lax.all_to_all(outgoing[p], 'pix', split_axis=0, concat_axis=0, tiled=True)]
    ppermute x2 -> x0, starting transfers between devices: 4.87 us -> none  [local_fast(): passed = lax.ppermute(incoming, 'shell', pairs)]
    unnamed x20 -> x26, local copies, waits for them, and re-layouts: 0.05 us -> 3.73 us
  transfers between devices with their start and end apart: 7 -> 2, of which waited for: 4 -> 0; matrix products, arithmetic and copies ran while one was open for 2% -> 2% of each run, Pallas kernels for 8% -> 0%
where the time goes in v1:
time: 251 us
  Pallas kernels  233 us (93%)
  local copies, waits for them, and re-layouts  6.05 us (2%)
  starting transfers between devices  5.22 us (2%)
  other arithmetic  4.89 us (2%)
    pallas_call x1, Pallas kernels, local_fast(): call(shear_kernel, [shape(planes, slab, L)] * 2, [vmem(HALF_BLOCKS, plane...  162 us
    pallas_call x1, Pallas kernels, local_fast(): call(swap_lists_kernel, [shape(groups, size, TC)] * (2 * planes), [dma(pl...  40.1 us
    pallas_call x1, Pallas kernels, local_fast(): call(partial(assemble_kernel, 2 * half), shape(planes, slab, L), [pltpu.V...  29.1 us
  transfers between devices with their start and end apart: 2, of which 0 were waited for; matrix products, arithmetic and copies ran while one was open for 2% of the time, Pallas kernels for 0%

profile of v1, /device:TPU:1, one launch (start us, length us, event | category | flops | bytes accessed | tf_op | source)
XLA Modules:
  0.0 250.6 jit_solution(8790429613210381623)
XLA Ops:
  0.6 0.0 copy-start.9
  0.6 0.0 copy-start.10
  0.7 0.0 copy-start.11
  0.7 0.8 pad_maximum_fusion.3
  1.4 3.9 %collective-permute-start = (f32[4]{0:T(128)S(1)}, f32[4]{0:T(128)S(1)}, u32[]{:S(2)}, u32[]{:S(2)}) collective-permute-start(f32[4]{0:T(128)S(1)} %pad_maximum_fusion.3), channel_id=1, source_target_pairs={{0,16},{1,17},{2,18},{3,19},{4,20},{5,21},{6,22},{7,23},{8,24},{9,... | collective-permute-start | bytes 56 | tf_op jit(solution)/shard_map/ppermute | solution.py:722
  5.4 1.3 collective-permute-start.1
  6.7 0.8 reshape.204
  7.5 1.0 convert_element_type.4
  8.5 0.1 reshape.206
  8.6 1.0 reshape.210
  9.6 0.7 compare_select_fusion
  10.3 0.1 pad_maximum_fusion.list_ref
  10.4 0.0 collective-permute-done
  10.4 0.1 broadcast_select_fusion
  10.5 0.0 copy-done.9
  10.5 0.0 copy-done.10
  10.5 0.0 copy-done.11
  10.5 0.1 compare_select_fusion.1
  10.6 0.1 pad_maximum_fusion.1.mix_ref
  10.7 0.0 collective-permute-done.1
  10.7 0.1 reshape.205
  10.8 0.8 select_reduce_fusion
  11.6 1.2 select_reduce_fusion.2
  12.9 0.1 squeeze.21.refs_3_
  13.0 0.1 squeeze.20.refs_2_
  13.1 0.1 squeeze.19.refs_1_
  13.2 0.1 squeeze.18.refs_0_
  13.3 2.5 shard_map.166
  15.7 40.1 %shard_map.167 = (f32[16,72,128]{2,1,0:T(8,128)S(1)}, f32[16,72,128]{2,1,0:T(8,128)S(1)}, f32[16,72,128]{2,1,0:T(8,128)S(1)}, f32[16,72,128]{2,1,0:T(8,128)S(1)}) custom-call(f32[16,72,128]{2,1,0:T(8,128)S(1)} %get-tuple-element.11.refs_0_, f32[16,72,128]{2,1,0:T(8,128)S(1)} %get-tuple-element.12.refs_1_), custom_call_target="tpu_custom_call" | custom-call | flops 1073741824 | bytes 4194304 | tf_op jit(solution)/shard_map/pallas_call | solution.py:753
  55.9 0.0 copy-start
  55.9 0.0 copy-start.1
  55.9 0.0 copy-start.2
  55.9 0.0 copy-start.3
  55.9 0.0 copy-start.4
  55.9 0.0 copy-start.5
  56.0 0.0 copy-start.6
  56.0 0.0 copy-start.7
  56.0 29.1 %shard_map.168.conv_ref = f32[2,128,2048]{2,1,0:T(8,128)} custom-call(f32[2,4]{1,0:T(2,128)S(1)} %pad_maximum_fusion.1.mix_ref, s32[128]{0:T(128)S(1)} %squeeze.18.refs_0_, s32[128]{0:T(128)S(1)} %squeeze.19.refs_1_, s32[128]{0:T(128)S(1)} %squeeze.20.refs_2_, s32[128]{0:T(128)S(1)} %squeeze.21.refs_3_, f32[16,72,128]{2,1,0:T(8,128)S(1)} %get-tuple-element.13.refs_4_, ...), custom_call_target="tpu_custom_call" | custom-call | flops 4294967296 | bytes 4194304 | tf_op jit(solution)/shard_map/pallas_call | solution.py:769
  85.1 0.0 copy-done
  85.1 0.0 copy-done.1
  85.1 0.0 copy-done.2
  85.1 0.0 copy-done.3
  85.2 0.0 copy-done.4
  85.2 0.0 copy-done.5
  85.2 0.0 copy-done.6
  85.2 0.0 copy-done.7
  85.2 161.7 %shard_map.169 = (f32[2,128,2048]{2,1,0:T(8,128)S(1)}, f32[2,128,2048]{2,1,0:T(8,128)}) custom-call(f32[2,128,2048]{2,1,0:T(8,128)} %shard_map.168.conv_ref, f32[2,128]{1,0:T(2,128)S(1)} %pad_maximum_fusion.2.col_ref, f32[16,128]{1,0:T(8,128)S(1)} %copy-done.7, f32[16,128]{1,0:T(8,128)S(1)} %copy-done.6, bf16[8,256,256]{2,1,0:T(8,128)(2,1)S(1)} %copy-done.1, ...), custom_call_target="tpu_custom_call" | custom-call | flops 4294967296 | bytes 4194304 | tf_op jit(solution)/shard_map/pallas_call | solution.py:789
  246.9 0.0 copy-start.8
  246.9 1.3 copy.56
  248.2 1.0 copy-done.8
  249.3 1.3 copy.57
  (11 shorter events, 0.1 us)
Async XLA Ops:
  0.6 9.9 %copy-start.9 = (f32[2]{0:T(128)S(1)}, f32[2]{0:T(128)}, u32[]{:S(2)}) copy-start(f32[2]{0:T(128)} %param.19) | copy-start | bytes 28
  0.6 9.9 %copy-start.10 = (f32[2]{0:T(128)S(1)}, f32[2]{0:T(128)}, u32[]{:S(2)}) copy-start(f32[2]{0:T(128)} %param.18) | copy-start | bytes 28
  0.7 9.9 %copy-start.11 = (f32[2]{0:T(128)S(1)}, f32[2]{0:T(128)}, u32[]{:S(2)}) copy-start(f32[2]{0:T(128)} %param.20) | copy-start | bytes 28
  1.4 9.0 %collective-permute-start = (f32[4]{0:T(128)S(1)}, f32[4]{0:T(128)S(1)}, u32[]{:S(2)}, u32[]{:S(2)}) collective-permute-start(f32[4]{0:T(128)S(1)} %pad_maximum_fusion.3), channel_id=1, source_target_pairs={{0,16},{1,17},{2,18},{3,19},{4,20},{5,21},{6,22},{7,23},{8,24},{9,... | collective-permute-start | bytes 56 | tf_op jit(solution)/shard_map/ppermute | solution.py:722
  5.4 5.3 %collective-permute-start.1 = (s32[2,1024]{1,0:T(2,128)}, s32[2,1024]{1,0:T(2,128)S(1)}, u32[]{:S(2)}, u32[]{:S(2)}) collective-permute-start(s32[2,1024]{1,0:T(2,128)} %param.15), channel_id=1, source_target_pairs={{0,16},{1,17},{2,18},{3,19},{4,20},{5,21},{6,22},{7,23},{8,24},{9,... | collective-permute-start | bytes 24584 | tf_op jit(solution)/shard_map/ppermute | solution.py:742
  55.9 29.3 %copy-start = (bf16[8,256,256]{2,1,0:T(8,128)(2,1)S(1)}, bf16[8,256,256]{2,1,0:T(8,128)(2,1)}, u32[]{:S(2)}) copy-start(bf16[8,256,256]{2,1,0:T(8,128)(2,1)} %constant.104.clone.low_ref) | copy-start | bytes 3145732
  55.9 29.2 %copy-start.1 = (bf16[8,256,256]{2,1,0:T(8,128)(2,1)S(1)}, bf16[8,256,256]{2,1,0:T(8,128)(2,1)}, u32[]{:S(2)}) copy-start(bf16[8,256,256]{2,1,0:T(8,128)(2,1)} %constant.103.clone.high_ref) | copy-start | bytes 3145732
  55.9 29.2 %copy-start.2 = (bf16[256,256]{1,0:T(8,128)(2,1)S(1)}, bf16[256,256]{1,0:T(8,128)(2,1)}, u32[]{:S(2)}) copy-start(bf16[256,256]{1,0:T(8,128)(2,1)} %constant.108.clone.backl_ref) | copy-start | bytes 393220
  55.9 29.2 %copy-start.3 = (bf16[256,256]{1,0:T(8,128)(2,1)S(1)}, bf16[256,256]{1,0:T(8,128)(2,1)}, u32[]{:S(2)}) copy-start(bf16[256,256]{1,0:T(8,128)(2,1)} %constant.107.clone.backh_ref) | copy-start | bytes 393220
  55.9 29.2 %copy-start.4 = (bf16[256,256]{1,0:T(8,128)(2,1)S(1)}, bf16[256,256]{1,0:T(8,128)(2,1)}, u32[]{:S(2)}) copy-start(bf16[256,256]{1,0:T(8,128)(2,1)} %constant.106.clone.coll_ref) | copy-start | bytes 393220
  55.9 29.2 %copy-start.5 = (bf16[256,256]{1,0:T(8,128)(2,1)S(1)}, bf16[256,256]{1,0:T(8,128)(2,1)}, u32[]{:S(2)}) copy-start(bf16[256,256]{1,0:T(8,128)(2,1)} %constant.105.clone.colh_ref) | copy-start | bytes 393220
  56.0 29.2 %copy-start.6 = (f32[16,128]{1,0:T(8,128)S(1)}, f32[16,128]{1,0:T(8,128)}, u32[]{:S(2)}) copy-start(f32[16,128]{1,0:T(8,128)} %constant.102.clone.twi_ref) | copy-start | bytes 24580
  56.0 29.2 %copy-start.7 = (f32[16,128]{1,0:T(8,128)S(1)}, f32[16,128]{1,0:T(8,128)}, u32[]{:S(2)}) copy-start(f32[16,128]{1,0:T(8,128)} %constant.101.clone.twr_ref) | copy-start | bytes 24580
  246.9 2.3 copy-start.8

commit v2 on v1

--- a/solution.py
+++ b/solution.py
@@ -264,16 +264,25 @@
     return split_table(out)
 
 
-def column_tables():
+def row_order(slab):
+    at = np.arange(slab)
+    rows = slab // TR
+    return (at % rows) * TR + at // rows
+
+
+def column_table(order):
     idx = np.arange(INNER)
-    angle = 2 * np.pi / INNER * ((idx[:, None] * idx[None, :]) % INNER)
+    angle = 2 * np.pi / INNER * ((idx[:, None] * order[None, :]) % INNER)
     co, si = np.cos(angle), np.sin(angle)
-    return split_table(np.block([[co, si], [-si, co]]))
-
-
-def twiddle_tables():
-    angle = 2 * np.pi / L * (np.arange(OUTER)[:, None] * np.arange(INNER)[None, :])
-    return np.cos(angle).astype(np.float32), (-np.sin(angle)).astype(np.float32)
+    return np.block([[co, si], [-si, co]])
+
+
+def twiddle_tables(order):
+    out = []
+    for rows in (order, np.arange(INNER)):
+        angle = 2 * np.pi / L * (np.arange(OUTER)[:, None] * rows[None, :])
+        out += [np.cos(angle), -np.sin(angle)]
+    return np.stack(out).astype(np.float32)
 
 
 def times_root(value, k, n, sign):
@@ -315,81 +324,55 @@
     return dot(left[0], right[0]) + (dot(left[0], right[1]) + dot(left[1], right[0]))
 
 
-def pack_kernel(slot_ref, list_ref, *out_refs):
-    planes, tiles, size, _ = list_ref.shape
+def flipped(me, mask):
+    for bit in (1, 2, 4, 8):
+        me = me + ((mask // bit) % 2) * (bit - 2 * bit * ((me // bit) % 2))
+    return me
+
+
+def pack_kernel(tile_ref, coef_ref, dist_ref, cell_ref, mass_ref, *refs):
+    out_refs, (wide, taken) = refs[:-2], refs[-2:]
+    planes, tiles, per_tile = cell_ref.shape
+    half = per_tile // TC
+    size = 2 * half
     groups, rows, _ = out_refs[0].shape
     cap = rows // size - 1
+    per_owner = L // groups // TR * (L // TC)
+    me = lax.axis_index("pix")
+    lane = lax.broadcasted_iota(jnp.int32, (1, TC), 1)
     for p in range(planes):
         out_ref = out_refs[p]
+        for i in range(half):
+            at = slice(i * TC, (i + 1) * TC)
+            wide[i] = cell_ref[p, :, at].astype(jnp.float32)
+            wide[half + i] = mass_ref[p, :, at].astype(jnp.float32)
         out_ref[...] = jnp.zeros_like(out_ref)
-        total = jnp.sum(list_ref[p, :, size // 2 :, :], axis=(0, 1))
-        total = jnp.sum(total.reshape(1, TC), axis=1, keepdims=True)
-        out_ref[:, cap * size :, :] = jnp.broadcast_to(total[None], (groups, size, TC))
+        total = jnp.sum(jnp.sum(wide[half:], axis=0), axis=0, keepdims=True)
+        total = jnp.sum(total, axis=1, keepdims=True)
+        tail = jnp.where(lane < cap, -1.0, jnp.where(lane == cap, total, 0.0))
+        tail = jnp.where(lane == cap + 1, coef_ref[p], tail)
+        tail = jnp.where(lane == cap + 2, dist_ref[p], tail)
+        out_ref[:, cap * size :, :] = jnp.broadcast_to(tail[None], (groups, size, TC))
+
+        def clear(o, _):
+            taken[o] = 0
+            return 0
+
+        lax.fori_loop(0, groups, clear, 0)
 
         def tile(t, _):
-            slot = slot_ref[p, t]
-            rows_at = pl.ds(pl.multiple_of((slot % cap) * size, size), size)
-            out_ref[slot // cap, rows_at, :] = list_ref[p, t]
+            b = tile_ref[p, me * tiles + t]
+            owner = b // per_owner
+            rank = taken[owner]
+            taken[owner] = rank + 1
+            for i in range(size):
+                out_ref[owner, pl.ds(rank * size + i, 1), :] = wide[i, pl.ds(t, 1), :]
+            where_at = (b - owner * per_owner).astype(jnp.float32)
+            old = out_ref[owner, cap * size : cap * size + 1, :]
+            out_ref[owner, cap * size : cap * size + 1, :] = jnp.where(lane == rank, where_at, old)
             return 0
 
         lax.fori_loop(0, tiles, tile, 0)
-
-
-def assemble_kernel(size, mix_ref, *refs):
-    count = (len(refs) - 2) // 2
-    places, lists = refs[:count], refs[count : 2 * count]
-    conv_ref, held = refs[2 * count :]
-    groups, rows, _ = lists[0].shape
-    cap = rows // size - 1
-    tiles = held.shape[1] - 1
-    half = size // 2
-    held[...] = jnp.zeros_like(held)
-    as_small = lambda ids: ids.astype(jnp.float32).astype(jnp.bfloat16)
-    row_id = as_small(lax.broadcasted_iota(jnp.int32, (TR, TC), 0))
-    col_id = as_small(lax.broadcasted_iota(jnp.int32, (TC, TC), 0))
-    one, zero = jnp.ones((), jnp.bfloat16), jnp.zeros((), jnp.bfloat16)
-    factors = []
-    for q in range(count):
-        place_ref, in_ref = places[q], lists[q]
-
-        def source(s, _):
-            for c in range(cap):
-                at = place_ref[s * cap + c]
-                entry = in_ref[s, c * size : (c + 1) * size, :]
-                cells = entry[:half].astype(jnp.int32)
-                cell_rows, cell_cols = as_small(cells // TC), as_small(cells % TC)
-                weights = entry[half:].astype(jnp.bfloat16)
-                row_hot, col_hot = [], []
-                for i in range(half):
-                    row_hot.append(jnp.where(row_id == cell_rows[i : i + 1], weights[i : i + 1], zero))
-                    col_hot.append(jnp.where(col_id == cell_cols[i : i + 1], one, zero))
-                held[q, at] = held[q, at] + lax.dot_general(
-                    jnp.concatenate(row_hot, axis=1),
-                    jnp.concatenate(col_hot, axis=1),
-                    (((1,), (1,)), ((), ())),
-                    preferred_element_type=jnp.float32,
-                )
-            return 0
-
-        lax.fori_loop(0, groups, source, 0)
-        total = in_ref[0, cap * size : cap * size + 1, 0:1]
-        for s in range(1, groups):
-            total = total + in_ref[s, cap * size : cap * size + 1, 0:1]
-        factors.append((L * L) / total)
-
-    def chunk(t, _):
-        rows = pl.ds(pl.multiple_of(t * TR, TR), TR)
-        for n in range(OUTER):
-            at = t * OUTER + n
-            fields = [held[q, at] * factors[q] - 1.0 for q in range(count)]
-            for i in range(conv_ref.shape[0]):
-                value = mix_ref[i, 0] * fields[0]
-                for j in range(1, count):
-                    value = value + mix_ref[i, j] * fields[j]
-                conv_ref[i, rows, n * INNER : (n + 1) * INNER] = value
-        return 0
-
-    lax.fori_loop(0, tiles // OUTER, chunk, 0)
 
 
 def signal_all(peers):
@@ -399,122 +382,237 @@
     pl.semaphore_wait(barrier, len(peers))
 
 
-def swap_lists_kernel(*refs):
-    planes = (len(refs) - 5) // 3
-    out_refs, in_refs, far_refs = refs[:planes], refs[planes : 2 * planes], refs[2 * planes : 3 * planes]
-    send, recv, pass_send, pass_recv, own_sem = refs[3 * planes :]
-    groups = out_refs[0].shape[0]
-    me, shell = lax.axis_index("pix"), lax.axis_index("shell")
-    signal_all([{"pix": (me + o) % groups} for o in range(1, groups)] + [{"shell": 1 - shell}])
-
-    def direct(p, o):
-        to = (me + o) % groups
-        return pltpu.make_async_remote_copy(
-            src_ref=out_refs[p].at[to],
-            dst_ref=in_refs[p].at[me],
-            send_sem=send.at[p, o],
-            recv_sem=recv.at[p, o],
-            device_id={"pix": to},
-            device_id_type=MESH,
-        )
-
-    def landing(p, o):
-        source = (me + groups - o) % groups
-        return pltpu.make_async_remote_copy(
-            src_ref=out_refs[p].at[source],
-            dst_ref=in_refs[p].at[source],
-            send_sem=send.at[p, o],
-            recv_sem=recv.at[p, o],
-            device_id={"pix": source},
-            device_id_type=MESH,
-        )
-
-    def onward(p, o):
-        source = (me + groups - o) % groups
-        return pltpu.make_async_remote_copy(
-            src_ref=in_refs[p].at[source],
-            dst_ref=far_refs[p].at[source],
-            send_sem=pass_send.at[p, o],
-            recv_sem=pass_recv.at[p, o],
-            device_id={"shell": 1 - shell},
-            device_id_type=MESH,
-        )
-
-    def own(p):
-        return pltpu.make_async_copy(out_refs[p].at[me], in_refs[p].at[me], own_sem.at[p])
-
-    for p in range(planes):
-        for j in range(1, groups):
-            direct(p, (j + groups // 2 - 1) % (groups - 1) + 1).start()
-        own(p).start()
-    for p in range(planes):
-        own(p).wait()
-        onward(p, 0).start()
-        for j in range(1, groups):
-            o = (j + groups // 2 - 1) % (groups - 1) + 1
-            landing(p, o).wait_recv()
-            onward(p, o).start()
-    for p in range(planes):
-        for o in range(groups):
-            onward(p, o).wait()
-            if o:
-                direct(p, o).wait_send()
-
-
-def shear_kernel(
-    conv_ref, col_ref, twr_ref, twi_ref, high_ref, low_ref, colh_ref, coll_ref, backh_ref, backl_ref,
-    one_ref, two_ref, held_row, sending, arrived, held, twist_in, kern, back, leaving, landed, held_inv,
-    fsend, frecv, rsend, rrecv,
+def remote(source, target, send, recv, peer):
+    return pltpu.make_async_remote_copy(
+        src_ref=source,
+        dst_ref=target,
+        send_sem=send,
+        recv_sem=recv,
+        device_id=peer,
+        device_id_type=MESH,
+    )
+
+
+def lensing_kernel(
+    out0, out1, inv_ref, twist_ref, high_ref, low_ref, colh_ref, coll_ref, backh_ref, backl_ref,
+    conv_ref, one_ref, two_ref,
+    box, slots, place, field, held_row, sending, arrived, held, twist_in, kern, back, leaving, landed,
+    lsend, lrecv, psend, precv, fsend, frecv, rsend, rrecv,
 ):
-    groups, _, slab, _ = sending.shape
+    out_refs = (out0, out1)
+    planes = 2
+    groups, message, _ = out0.shape
+    slab = L // groups
+    half = 4
+    size = 2 * half
+    cap = message // size - 1
     span = held_row.shape[2]
     chunks = slab // span
-    me = lax.axis_index("pix")
-    signal_all([{"pix": (me + o) % groups} for o in range(1, groups)])
+    pitch = slots.shape[1] // (cap * groups)
+    tile_rows = slab // TR
+    me, shell = lax.axis_index("pix"), lax.axis_index("shell")
+    signal_all([{"pix": flipped(me, m)} for m in range(1, groups)] + [{"shell": 1 - shell}])
+
+    def direct(p, m):
+        peer = flipped(me, m)
+        return remote(
+            out_refs[p].at[peer], box.at[p, me], lsend.at[p, m], lrecv.at[p, m], {"pix": peer}
+        )
+
+    def landing(p, m):
+        peer = flipped(me, m)
+        return remote(
+            out_refs[p].at[peer], box.at[p, peer], lsend.at[p, m], lrecv.at[p, m], {"pix": peer}
+        )
+
+    def onward(p, m):
+        source = flipped(me, m)
+        first = out_refs[p].at[me] if isinstance(m, int) and m == 0 else box.at[p, source]
+        return remote(first, box.at[planes + p, source], psend.at[p, m], precv.at[p, m], {"shell": 1 - shell})
+
+    for low, high in ((1, groups // 2), (groups // 2, groups)):
+        for p in range(planes):
+
+            def start(m, _):
+                direct(p, m).start()
+                return 0
+
+            lax.fori_loop(low, high, start, 0)
+    for p in range(planes):
+        onward(p, 0).start()
+        box[p, me] = out_refs[p][me]
+
+    signed_v, weight = column_info(me, groups)
+    inner_id = lax.broadcasted_iota(jnp.int32, (INNER, INNER), 0)
+
+    def prepare(k, _):
+        for i in range(4):
+            twist_in[i, k] = jnp.broadcast_to(twist_ref[i, pl.ds(k, 1), :], (INNER, INNER)).T
+        u = k + OUTER * inner_id
+        signed_u = jnp.where(u >= L // 2, u - L, u).astype(jnp.float32)
+        scale = jnp.where(u == L // 2, 0.0, weight)
+        uu, vv = signed_u * signed_u, signed_v * signed_v
+        over = scale / jnp.maximum(uu + vv, 1.0)
+        kern[0, k] = (vv - uu) * over
+        kern[1, k] = 2.0 * signed_v * signed_u * over
+        return 0
+
+    as_small = lambda ids: ids.astype(jnp.float32).astype(jnp.bfloat16)
+    short, narrow = 2 * TR, TC // 2
+    row_id = as_small(lax.broadcasted_iota(jnp.int32, (short, TC), 0))
+    col_id = as_small(lax.broadcasted_iota(jnp.int32, (narrow, TC), 0))
+    one, zero = jnp.ones((), jnp.bfloat16), jnp.zeros((), jnp.bfloat16)
+
+    def deposit(q, s):
+        for c in range(cap):
+            entry = box[q, s, c * size : (c + 1) * size, :]
+            cells = entry[:half].astype(jnp.int32)
+            cell_rows = as_small(cells // TC + TR * ((cells // narrow) % 2))
+            cell_cols = as_small(cells % narrow)
+            weights = entry[half:].astype(jnp.bfloat16)
+            row_hot, col_hot = [], []
+            for i in range(half):
+                row_hot.append(jnp.where(row_id == cell_rows[i : i + 1], weights[i : i + 1], zero))
+                col_hot.append(jnp.where(col_id == cell_cols[i : i + 1], one, zero))
+            sums = lax.dot_general(
+                jnp.concatenate(row_hot, axis=1),
+                jnp.concatenate(col_hot, axis=1),
+                (((1,), (1,)), ((), ())),
+                preferred_element_type=jnp.float32,
+            )
+            at = pl.ds(pl.multiple_of((c * groups + s) * pitch, 8), TR)
+            slots[q, at, :] = jnp.concatenate([sums[:TR], sums[TR:]], axis=1)
+
+    def near_block(m):
+        def one_plane(p, _):
+            deposit(p, flipped(me, m))
+            return 0
+
+        lax.fori_loop(0, planes, one_plane, 0)
+
+    def far_block(m):
+        for p in range(planes):
+            onward(p, m).wait_recv()
+
+        def one_plane(p, _):
+            deposit(planes + p, flipped(me, m))
+            return 0
+
+        lax.fori_loop(0, planes, one_plane, 0)
+
+    def take(m):
+        for p in range(planes):
+            landing(p, m).wait_recv()
+            onward(p, m).start()
+
+    lag = 4
+    near_block(0)
+    lax.fori_loop(0, OUTER, prepare, 0)
+
+    def early(m, _):
+        take(m)
+        near_block(m)
+        return 0
+
+    lax.fori_loop(1, lag, early, 0)
+
+    def steady(m, _):
+        take(m)
+        near_block(m)
+        far_block(m - lag)
+        return 0
+
+    lax.fori_loop(lag, groups, steady, 0)
+
+    def late(m, _):
+        far_block(m)
+        return 0
+
+    lax.fori_loop(groups - lag, groups, late, 0)
+
+    lane_id = lax.broadcasted_iota(jnp.int32, (groups, TC), 1)
+    tile_id = ((lane_id % tile_rows) * OUTER + lane_id // tile_rows).astype(jnp.float32)
+    gains, shifts = [[], []], [0.0, 0.0]
+    for q in range(2 * planes):
+        tails = box[q, :, cap * size, :]
+        hot = [jnp.where(tails[:, c : c + 1] == tile_id, 1.0, 0.0) for c in range(cap)]
+        place[q] = jnp.concatenate(hot, axis=0).T.astype(jnp.bfloat16)
+        total = jnp.sum(tails[:, cap : cap + 1], axis=0, keepdims=True)
+        coef, dist = tails[0:1, cap + 1 : cap + 2], tails[0:1, cap + 2 : cap + 3]
+        for i in range(planes):
+            mixed = coef * (1.0 - inv_ref[i] * dist)
+            if q >= planes:
+                mixed = jnp.where(shell > 0, mixed, 0.0)
+            elif q > i:
+                mixed = jnp.zeros_like(mixed)
+            gains[i].append(mixed * ((L * L) / total))
+            shifts[i] = shifts[i] + mixed
 
     def rows_of(c):
         return pl.ds(pl.multiple_of(c * span, span), span)
 
-    def go_copy(c, o, peer, slot):
-        return pltpu.make_async_remote_copy(
-            src_ref=sending.at[peer, :, rows_of(c), :],
-            dst_ref=arrived.at[slot, :, rows_of(c), :],
-            send_sem=fsend.at[c, o],
-            recv_sem=frecv.at[c, o],
-            device_id={"pix": peer},
-            device_id_type=MESH,
+    def go_copy(c, m, arriving=False):
+        peer = flipped(me, m)
+        return remote(
+            sending.at[peer, :, rows_of(c), :],
+            arrived.at[peer if arriving else me, :, rows_of(c), :],
+            fsend.at[c, m],
+            frecv.at[c, m],
+            {"pix": peer},
         )
 
-    def back_copy(f, c, o, peer, slot):
-        return pltpu.make_async_remote_copy(
-            src_ref=leaving.at[peer, f, :, rows_of(c), :],
-            dst_ref=landed.at[slot, f, :, rows_of(c), :],
-            send_sem=rsend.at[f, c, o],
-            recv_sem=rrecv.at[f, c, o],
-            device_id={"pix": peer},
-            device_id_type=MESH,
+    def back_copy(f, c, m, arriving=False):
+        peer = flipped(me, m)
+        return remote(
+            leaving.at[peer, f, :, rows_of(c), :],
+            landed.at[peer if arriving else me, f, :, rows_of(c), :],
+            rsend.at[f, c, m],
+            rrecv.at[f, c, m],
+            {"pix": peer},
         )
 
-    def to_peer(o):
-        return (me + o) % groups
-
-    def from_peer(o):
-        return (me + groups - o) % groups
-
     def each_peer(action):
-        def step(j, _):
-            action((j + groups // 2 - 1) % (groups - 1) + 1)
+        def step(m, _):
+            action(m)
             return 0
 
         lax.fori_loop(1, groups, step, 0)
 
+    def field_rows(r, n):
+        return pl.ds(pl.multiple_of(r * TC + n * tile_rows, tile_rows), tile_rows)
+
     def forward_rows(c, _):
-        def radix(t, _):
-            rows = pl.ds(pl.multiple_of(c * span + t * 8, 8), 8)
-            near = pl.ds(pl.multiple_of(t * 8, 8), 8)
+        def mass_rows(j, _):
+            r = c * (span // tile_rows) + 2 * j
+            sums = []
+            for q in range(2 * planes):
+                pair = jnp.concatenate(
+                    [slots[q, pl.ds(r + i, cap * groups, stride=pitch), :] for i in range(2)], axis=1
+                )
+                high = pair.astype(jnp.bfloat16)
+                rest = pair - high.astype(jnp.float32)
+                middle = rest.astype(jnp.bfloat16)
+                low = (rest - middle.astype(jnp.float32)).astype(jnp.bfloat16)
+                dot = lambda part: jnp.dot(place[q], part, preferred_element_type=jnp.float32)
+                sums.append(dot(high) + (dot(middle) + dot(low)))
+            for i in range(planes):
+                value = gains[i][0] * sums[0]
+                for q in range(1, 2 * planes):
+                    value = value + gains[i][q] * sums[q]
+                value = value - shifts[i]
+                for e in range(2):
+                    at = pl.ds(pl.multiple_of((r + e) * TC, TC), TC)
+                    field[i, at, :] = value[:, e * TC : (e + 1) * TC]
+            return 0
+
+        lax.fori_loop(0, span // tile_rows // 2, mass_rows, 0)
+
+        def radix(j, _):
+            r = c * (span // tile_rows) + j
+            near = pl.ds(pl.multiple_of(j * tile_rows, tile_rows), tile_rows)
             z = fft_list(
                 [
-                    tuple(conv_ref[i, rows, n * INNER : (n + 1) * INNER] for i in range(2))
+                    tuple(field[i, field_rows(r, n), :] for i in range(2))
                     for n in range(OUTER)
                 ],
                 -1,
@@ -530,47 +628,40 @@
                 held_row[HALF_BLOCKS - 1, p, near, INNER:] = z[HALF_BLOCKS][p]
             return 0
 
-        lax.fori_loop(0, span // 8, radix, 0)
+        lax.fori_loop(0, span // tile_rows, radix, 0)
 
         def block(j, _):
             b = (me // 2 + 1 + j) % HALF_BLOCKS
             value = held_row[b].reshape(2 * span, 2 * INNER)
             result = three_pass(split_value(value), (high_ref[b], low_ref[b]), ((1,), (0,)))
             for p in range(2):
-                for half in range(2):
-                    sending[2 * b + p, half, rows_of(c), :] = result[
-                        p * span : (p + 1) * span, half * INNER : (half + 1) * INNER
+                for part in range(2):
+                    sending[2 * b + p, part, rows_of(c), :] = result[
+                        p * span : (p + 1) * span, part * INNER : (part + 1) * INNER
                     ]
             return 0
 
         lax.fori_loop(0, HALF_BLOCKS, block, 0)
-        each_peer(lambda o: go_copy(c, o, to_peer(o), me).start())
-        for half in range(2):
-            arrived[me, half, rows_of(c), :] = sending[me, half, rows_of(c), :]
+        each_peer(lambda m: go_copy(c, m).start())
+        for part in range(2):
+            arrived[me, part, rows_of(c), :] = sending[me, part, rows_of(c), :]
         return 0
 
     lax.fori_loop(0, chunks, forward_rows, 0)
 
-    signed_v = col_ref[0:1]
-    weight = col_ref[1:2]
-    inner_id = lax.broadcasted_iota(jnp.int32, (INNER, INNER), 0)
-
-    def prepare(k, _):
-        for i, ref in enumerate((twr_ref, twi_ref)):
-            twist_in[i, k] = jnp.broadcast_to(ref[pl.ds(k, 1), :], (INNER, INNER)).T
-        u = k + OUTER * inner_id
-        signed_u = jnp.where(u >= L // 2, u - L, u).astype(jnp.float32)
-        scale = jnp.where(u == L // 2, 0.0, weight)
-        uu, vv = signed_u * signed_u, signed_v * signed_v
-        over = scale / jnp.maximum(uu + vv, 1.0)
-        kern[0, k] = (vv - uu) * over
-        kern[1, k] = 2.0 * signed_v * signed_u * over
+    def show(t, _):
+        for i in range(planes):
+            for n in range(OUTER):
+                for r in range(0, TR, 8):
+                    rows = pl.ds(pl.multiple_of(t * TR + r, 8), 8)
+                    held_at = pl.ds(r * TC + n * tile_rows + t, 8, stride=TC)
+                    conv_ref[i, rows, n * TC : (n + 1) * TC] = field[i, held_at, :]
         return 0
 
-    lax.fori_loop(0, OUTER, prepare, 0)
+    lax.fori_loop(0, tile_rows, show, 0)
 
     def forward_columns(c, _):
-        each_peer(lambda o: go_copy(c, o, from_peer(o), from_peer(o)).wait_recv())
+        each_peer(lambda m: go_copy(c, m, True).wait_recv())
 
         def radix(t, _):
             rows = pl.ds(pl.multiple_of(c * span + t * 8, 8), 8)
@@ -603,7 +694,7 @@
                 axis=1,
             )
             result = three_pass((backh_ref[...], backl_ref[...]), split_value(fields), ((1,), (0,)))
-            cs, sn = twist_in[0, k], twist_in[1, k]
+            cs, sn = twist_in[2, k], twist_in[3, k]
             for f in range(2):
                 at = slice(f * INNER, (f + 1) * INNER)
                 re, im = result[:INNER, at], result[INNER:, at]
@@ -625,7 +716,7 @@
             return 0
 
         lax.fori_loop(0, span // 8, radix, 0)
-        each_peer(lambda o: back_copy(f, c, o, to_peer(o), me).start())
+        each_peer(lambda m: back_copy(f, c, m).start())
         for part in range(2):
             landed[me, f, part, rows_of(c), :] = leaving[me, f, part, rows_of(c), :]
         return 0
@@ -635,7 +726,7 @@
     for f, out_ref in enumerate((one_ref, two_ref)):
 
         def inverse_rows(c, _):
-            each_peer(lambda o: back_copy(f, c, o, from_peer(o), from_peer(o)).wait_recv())
+            each_peer(lambda m: back_copy(f, c, m, True).wait_recv())
 
             def block(b, _):
                 value = jnp.concatenate(
@@ -647,7 +738,7 @@
                     ],
                     axis=0,
                 )
-                held_inv[b] = three_pass(
+                held_row[b] = three_pass(
                     split_value(value), (high_ref[b], low_ref[b]), ((1,), (1,))
                 ).reshape(2, span, 2 * INNER)
                 return 0
@@ -659,11 +750,11 @@
                 rows = pl.ds(pl.multiple_of(c * span + t * 8, 8), 8)
                 z = [None] * OUTER
                 last = HALF_BLOCKS - 1
-                z[0] = (held_inv[last, 0, near, :INNER], held_inv[last, 1, near, :INNER])
-                z[HALF_BLOCKS] = (held_inv[last, 0, near, INNER:], held_inv[last, 1, near, INNER:])
+                z[0] = (held_row[last, 0, near, :INNER], held_row[last, 1, near, :INNER])
+                z[HALF_BLOCKS] = (held_row[last, 0, near, INNER:], held_row[last, 1, near, INNER:])
                 for k in range(1, HALF_BLOCKS):
-                    ar, ai = held_inv[k - 1, 0, near, :INNER], held_inv[k - 1, 0, near, INNER:]
-                    br, bi = held_inv[k - 1, 1, near, :INNER], held_inv[k - 1, 1, near, INNER:]
+                    ar, ai = held_row[k - 1, 0, near, :INNER], held_row[k - 1, 0, near, INNER:]
+                    br, bi = held_row[k - 1, 1, near, :INNER], held_row[k - 1, 1, near, INNER:]
                     z[k] = (ar - bi, ai + br)
                     z[OUTER - k] = (ar + bi, br - ai)
                 x = fft_list(z, 1)
@@ -678,12 +769,32 @@
         lax.fori_loop(0, chunks, inverse_rows, 0)
 
     def drain(c, _):
-        each_peer(lambda o: go_copy(c, o, to_peer(o), me).wait_send())
+        each_peer(lambda m: go_copy(c, m).wait_send())
         for f in range(2):
-            each_peer(lambda o: back_copy(f, c, o, to_peer(o), me).wait_send())
+            each_peer(lambda m: back_copy(f, c, m).wait_send())
         return 0
 
     lax.fori_loop(0, chunks, drain, 0)
+    for p in range(planes):
+        onward(p, 0).wait_send()
+
+        def settle(m, _):
+            direct(p, m).wait_send()
+            onward(p, m).wait_send()
+            return 0
+
+        lax.fori_loop(1, groups, settle, 0)
+
+
+def column_info(me, groups):
+    lane = lax.broadcasted_iota(jnp.int32, (1, INNER), 1)
+    b = me // 2
+    last = b == HALF_BLOCKS - 1
+    upper = lane // (INNER // 2)
+    folded = OUTER * (lane - upper * (INNER // 2)) + HALF_BLOCKS * upper
+    mine = jnp.where(last, folded, b + 1 + OUTER * lane)
+    weight = jnp.where(last & (mine > 0), 2.0, 1.0) / (L * L)
+    return jnp.where(mine >= L // 2, mine - L, mine).astype(jnp.float32), weight
 
 
 def call(body, outs, scratch=(), smem=(0,), count=1, megabytes=48, flops=0, group=None):
@@ -711,109 +822,64 @@
 
 def local_fast(block_tile, cell_index, masses, plane_coef, plane_dist, source_inv):
     groups = lax.axis_size("pix")
-    me = lax.axis_index("pix")
-    mine_shell = lax.axis_index("shell")
     planes, local_tiles, per_tile = cell_index.shape
     slab = L // groups
-    per_owner = slab // TR * (L // TC)
     cap = max(1, 2 * local_tiles // groups)
-
-    pairs = [(0, 1)]
-    other = lax.ppermute(jnp.concatenate([plane_coef, plane_dist]), "shell", pairs)
-    other_coef = jnp.where(mine_shell > 0, other[:planes], 0.0)
-    other_dist = other[planes:]
-
-    earlier = jnp.arange(local_tiles)[:, None] < jnp.arange(local_tiles)[None, :]
-    wanted = me * cap + jnp.arange(cap)
-
-    def routes(tiles):
-        table = tiles.reshape(planes, groups, local_tiles)
-        owner = table // per_owner
-        same_owner = owner[:, :, :, None] == owner[:, :, None, :]
-        rank = jnp.sum(jnp.where(same_owner & earlier[None, None], 1, 0), axis=2)
-        slot = owner * cap + rank
-        here = slot[:, :, None, :] == wanted[None, None, :, None]
-        local_index = table - me * per_owner
-        place = jnp.sum(jnp.where(here, local_index[:, :, None, :] + 1, 0), axis=3)
-        place = jnp.where(place > 0, place - 1, per_owner).reshape(planes, groups * cap)
-        return slot, place
-
-    slot, place = routes(block_tile)
-    _, other_place = routes(lax.ppermute(block_tile, "shell", pairs))
-    my_slots = lax.dynamic_index_in_dim(slot, me, axis=1, keepdims=False)
-
-    half = per_tile // TC
-    as_lists = lambda part: part.astype(jnp.float32).reshape(planes, local_tiles, half, TC)
-    lists = jnp.concatenate([as_lists(cell_index), as_lists(masses)], axis=2)
+    size = 2 * per_tile // TC
+    message = (cap + 1) * size
+    vmem = lambda *dims: pltpu.VMEM(dims, jnp.float32)
+    dma = lambda *dims: pltpu.SemaphoreType.DMA(dims)
     outgoing = call(
-        pack_kernel, [shape(groups, (cap + 1) * 2 * half, TC)] * planes, count=2, flops=1 << 20
-    )(my_slots, lists)
-    size = (cap + 1) * 2 * half
-    dma = lambda *dims: pltpu.SemaphoreType.DMA(dims)
-    swapped = call(
-        swap_lists_kernel,
-        [shape(groups, size, TC)] * (2 * planes),
-        [dma(planes, groups)] * 4 + [dma(planes)],
-        smem=(),
-        count=planes,
-        flops=1 << 30,
-        group=0,
-    )(*outgoing)
-
-    own = plane_coef[None, :] * (1.0 - source_inv[:, None] * plane_dist[None, :])
-    own = jnp.where(jnp.arange(planes)[None, :] <= jnp.arange(planes)[:, None], own, 0.0)
-    before = other_coef[None, :] * (1.0 - source_inv[:, None] * other_dist[None, :])
-    mix = jnp.concatenate([own, before], axis=1)
-
-    routed = [place[p] for p in range(planes)] + [other_place[p] for p in range(planes)]
-    convergence = call(
-        partial(assemble_kernel, 2 * half),
-        shape(planes, slab, L),
-        [pltpu.VMEM((2 * planes, per_owner + 1, TR, TC), jnp.float32)],
-        smem=tuple(range(2 * planes + 1)),
-        count=4 * planes + 1,
-        flops=1 << 32,
-    )(mix, *routed, *swapped)
-
+        pack_kernel,
+        [shape(groups, message, TC)] * planes,
+        [vmem(size, local_tiles, TC), pltpu.SMEM((groups,), jnp.int32)],
+        smem=(0, 1, 2),
+        count=5,
+        flops=1 << 20,
+    )(block_tile, plane_coef, plane_dist, cell_index, masses)
+
+    order = row_order(slab)
     row_high, row_low = row_tables()
-    columns = jnp.asarray(block_columns().astype(np.float32))
-    mine = lax.dynamic_index_in_dim(columns, me // planes, axis=0, keepdims=False)
-    special = (me // planes == HALF_BLOCKS - 1) & (mine > 0)
-    weight = jnp.where(special, 2.0, 1.0) / (L * L)
-    signed = jnp.where(mine >= L // 2, mine - L, mine)
-    col_info = jnp.stack([signed, weight])
-    col_high, col_low = column_tables()
-    tw_real, tw_imag = twiddle_tables()
+    forth, natural = column_table(order), column_table(np.arange(INNER))
+    col_high, col_low = split_table(forth)
+    back_high, back_low = split_table(natural.T)
     span = slab // CHUNKS
-    vmem = lambda *dims: pltpu.VMEM(dims, jnp.float32)
-    shear_one, shear_two = call(
-        shear_kernel,
-        [shape(planes, slab, L)] * 2,
+    pitch = 3 * TR // 2
+    return call(
+        lensing_kernel,
+        [shape(planes, slab, L)] * 3,
         [
+            vmem(2 * planes, groups, message, TC),
+            vmem(2 * planes, cap * groups * pitch, TC),
+            pltpu.VMEM((2 * planes, TC, TC), jnp.bfloat16),
+            vmem(planes, TR * TC, TC),
             vmem(HALF_BLOCKS, planes, span, 2 * INNER),
             vmem(groups, 2, slab, INNER),
             vmem(groups, 2, slab, INNER),
             vmem(OUTER, 2, INNER, INNER),
-            vmem(2, OUTER, INNER, INNER),
+            vmem(4, OUTER, INNER, INNER),
             vmem(2, OUTER, INNER, INNER),
             vmem(2, OUTER, 2, INNER, INNER),
             vmem(groups, 2, 2, slab, INNER),
             vmem(groups, 2, 2, slab, INNER),
-            vmem(HALF_BLOCKS, planes, span, 2 * INNER),
+            dma(planes, groups),
+            dma(planes, groups),
+            dma(planes, groups),
+            dma(planes, groups),
             dma(CHUNKS, groups),
             dma(CHUNKS, groups),
             dma(2, CHUNKS, groups),
             dma(2, CHUNKS, groups),
         ],
-        smem=(),
+        smem=(2,),
         count=10,
+        megabytes=58,
         flops=1 << 32,
-        group=1,
+        group=0,
     )(
-        convergence, col_info, jnp.asarray(tw_real), jnp.asarray(tw_imag), row_high, row_low,
-        col_high, col_low, col_high.T.copy(), col_low.T.copy(),
-    )
-    return convergence, shear_one, shear_two
+        *outgoing, source_inv, jnp.asarray(twiddle_tables(order)), row_high, row_low,
+        col_high, col_low, back_high, back_low,
+    )
 
 
 def solution(mesh):
@@ -832,7 +898,8 @@
             shells == 2
             and cell_index.shape[0] == 2
             and groups == OUTER
-            and cell_index.shape[2] % (4 * TC) == 0
+            and cell_index.shape[2] == 4 * TC
+            and cell_index.shape[1] * 2 == groups * 8
         )
         return (local_fast if fits else local)(block_tile, cell_index, *rest)
 

time: 251 us -> 217 us (0.86)
  Pallas kernels: 233 us -> 203 us
  local copies, waits for them, and re-layouts: 6.05 us -> 12.4 us
  starting transfers between devices: 5.22 us -> 0 us
  other arithmetic: 4.89 us -> 0 us
    pallas_call x4 -> x2, Pallas kernels: 233 us -> 203 us  [the longest x1 199 us: local_fast(): call(lensing_kernel, [shape(planes, slab, L)] * 3, [vmem(2 * planes, grou...]
    unnamed x26 -> x21, local copies, waits for them, and re-layouts: 3.73 us -> 12.4 us
    ppermute x2 -> x0, starting transfers between devices: 5.22 us -> none  [the longest x1 3.92 us: local_fast(): lax.ppermute(jnp.concatenate([plane_coef, plane_dist]), 'shell', pairs)]
  transfers between devices with their start and end apart: 2 -> 0, of which waited for: 0 -> 0; matrix products, arithmetic and copies ran while one was open for 2% -> 0% of each run, Pallas kernels for 0% -> 0%
where the time goes in v2:
time: 217 us; the launch traced here: 216 us
  Pallas kernels  203 us (94%)
  local copies, waits for them, and re-layouts  12.4 us (6%)
    pallas_call x1, Pallas kernels, local_fast(): call(lensing_kernel, [shape(planes, slab, L)] * 3, [vmem(2 * planes, grou...  199 us
    unnamed x21, local copies, waits for them, and re-layouts  12.4 us

profile of v2, /device:TPU:1, one launch (start us, length us, event | category | flops | bytes accessed | tf_op | source)
XLA Modules:
  0.0 216.3 jit_solution(11056107669107823371)
XLA Ops:
  0.6 0.0 copy-start
  0.6 0.9 copy-done
  1.6 0.0 copy-start.1
  1.6 0.9 copy-done.1
  2.5 0.0 copy-start.2
  2.5 0.7 copy-done.2
  3.2 0.0 copy-start.3
  3.2 0.7 copy-done.3
  3.8 0.0 copy-start.4
  3.8 0.7 copy-done.4
  4.5 3.9 %shard_map.148 = (f32[16,72,128]{2,1,0:T(8,128)S(1)}, f32[16,72,128]{2,1,0:T(8,128)S(1)}) custom-call(s32[2,1024]{1,0:T(2,128)S(1)} %copy-done.2, f32[2]{0:T(128)S(1)} %copy-done.3, f32[2]{0:T(128)S(1)} %copy-done.4, s32[2,64,512]{2,1,0:T(8,128)S(1)} %copy-done, bf16[2,64,512]{2,1,0:T(8,128)(2,1)S(1)} %copy-done.1), custom_call_target="tpu_custom_call" | custom-call | flops 1048576 | bytes 4194304 | tf_op jit(solution)/shard_map/pallas_call | solution.py:832
  8.4 0.0 copy-start.5
  8.4 0.8 copy-done.5
  9.2 0.0 copy-start.6
  9.2 0.8 copy-done.6
  10.0 199.3 %shard_map.149 = (f32[2,128,2048]{2,1,0:T(8,128)}, f32[2,128,2048]{2,1,0:T(8,128)}, f32[2,128,2048]{2,1,0:T(8,128)}) custom-call(f32[16,72,128]{2,1,0:T(8,128)} %copy-done.5, f32[16,72,128]{2,1,0:T(8,128)} %copy-done.6, f32[2]{0:T(128)} %inv_ref.1, f32[4,16,128]{2,1,0:T(8,128)} %constant.14.clone.twist_ref, bf16[8,256,256]{2,1,0:T(8,128)(2,1)} %constant.15.clone.high_ref, ...), custom_call_target="tpu_custom_call" | custom-call | flops 4294967296 | bytes 4194304 | tf_op jit(solution)/shard_map/pallas_call | solution.py:848
  209.3 0.0 copy-start.8
  209.3 3.3 %copy.19 = f32[2,128,2048]{2,1,0:T(8,128)} copy(f32[2,128,2048]{2,1,0:T(8,128)} %get-tuple-element.10) | data formatting | bytes 4194304
  212.6 0.0 copy-done.8
  212.6 0.0 copy-start.7
  212.6 1.3 copy.20
  213.9 1.0 copy-done.7
  215.0 1.3 copy.21
Async XLA Ops:
  0.6 1.0 copy-start
  1.6 0.9 copy-start.1
  2.5 0.7 copy-start.2
  3.2 0.7 copy-start.3
  3.8 0.7 copy-start.4
  8.4 0.8 copy-start.5
  9.2 0.8 copy-start.6
  209.3 3.3 %copy-start.8 = (f32[2,128,2048]{2,1,0:T(8,128)S(1)}, f32[2,128,2048]{2,1,0:T(8,128)}, u32[]{:S(2)}) copy-start(f32[2,128,2048]{2,1,0:T(8,128)} %get-tuple-element.11) | copy-start | bytes 6291460
  212.6 2.3 %copy-start.7 = (f32[2,128,2048]{2,1,0:T(8,128)S(1)}, f32[2,128,2048]{2,1,0:T(8,128)}, u32[]{:S(2)}) copy-start(f32[2,128,2048]{2,1,0:T(8,128)} %get-tuple-element.12) | copy-start | bytes 6291460

commit v3 on v2

--- a/solution.py
+++ b/solution.py
@@ -324,15 +324,33 @@
     return dot(left[0], right[0]) + (dot(left[0], right[1]) + dot(left[1], right[0]))
 
 
-def flipped(me, mask):
-    for bit in (1, 2, 4, 8):
-        me = me + ((mask // bit) % 2) * (bit - 2 * bit * ((me // bit) % 2))
-    return me
-
-
-def pack_kernel(tile_ref, coef_ref, dist_ref, cell_ref, mass_ref, *refs):
-    out_refs, (wide, taken) = refs[:-2], refs[-2:]
-    planes, tiles, per_tile = cell_ref.shape
+def partners(me):
+    steps = [(bit, bit - 2 * bit * ((me // bit) % 2)) for bit in (1, 2, 4, 8)]
+
+    def flipped(mask):
+        peer = me
+        for bit, step in steps:
+            if not isinstance(mask, int):
+                peer = peer + ((mask // bit) % 2) * step
+            elif mask & bit:
+                peer = peer + step
+        return peer
+
+    return flipped
+
+
+def fetch(pairs, sems):
+    copies = [pltpu.make_async_copy(a, b, sems.at[i]) for i, (a, b) in enumerate(pairs)]
+    for copy in copies:
+        copy.start()
+    return copies
+
+
+def pack_kernel(tile_in, cell_in, mass_in, *refs):
+    planes, tiles, per_tile = cell_in.shape
+    out_refs = refs[:planes]
+    tile_ref, cell_ref, mass_ref, wide, taken, sems = refs[planes:]
+    copies = fetch(((tile_in, tile_ref), (cell_in, cell_ref), (mass_in, mass_ref)), sems)
     half = per_tile // TC
     size = 2 * half
     groups, rows, _ = out_refs[0].shape
@@ -340,18 +358,19 @@
     per_owner = L // groups // TR * (L // TC)
     me = lax.axis_index("pix")
     lane = lax.broadcasted_iota(jnp.int32, (1, TC), 1)
+    for out_ref in out_refs:
+        out_ref[...] = jnp.zeros_like(out_ref)
+    for copy in copies:
+        copy.wait()
     for p in range(planes):
         out_ref = out_refs[p]
         for i in range(half):
             at = slice(i * TC, (i + 1) * TC)
             wide[i] = cell_ref[p, :, at].astype(jnp.float32)
             wide[half + i] = mass_ref[p, :, at].astype(jnp.float32)
-        out_ref[...] = jnp.zeros_like(out_ref)
         total = jnp.sum(jnp.sum(wide[half:], axis=0), axis=0, keepdims=True)
         total = jnp.sum(total, axis=1, keepdims=True)
         tail = jnp.where(lane < cap, -1.0, jnp.where(lane == cap, total, 0.0))
-        tail = jnp.where(lane == cap + 1, coef_ref[p], tail)
-        tail = jnp.where(lane == cap + 2, dist_ref[p], tail)
         out_ref[:, cap * size :, :] = jnp.broadcast_to(tail[None], (groups, size, TC))
 
         def clear(o, _):
@@ -372,7 +391,7 @@
             out_ref[owner, cap * size : cap * size + 1, :] = jnp.where(lane == rank, where_at, old)
             return 0
 
-        lax.fori_loop(0, tiles, tile, 0)
+        lax.fori_loop(0, tiles, tile, 0, unroll=4)
 
 
 def signal_all(peers):
@@ -394,8 +413,10 @@
 
 
 def lensing_kernel(
-    out0, out1, inv_ref, twist_ref, high_ref, low_ref, colh_ref, coll_ref, backh_ref, backl_ref,
+    out0, out1, coef_in, dist_in, inv_in, twist_in_ref, high_in, low_in, colh_in, coll_in, backh_in, backl_in,
     conv_ref, one_ref, two_ref,
+    coef_ref, dist_ref, inv_ref, twist_ref, high_ref, low_ref, colh_ref, coll_ref, backh_ref, backl_ref,
+    tsem, note, far_note, note_sems,
     box, slots, place, field, held_row, sending, arrived, held, twist_in, kern, back, leaving, landed,
     lsend, lrecv, psend, precv, fsend, frecv, rsend, rrecv,
 ):
@@ -411,33 +432,46 @@
     pitch = slots.shape[1] // (cap * groups)
     tile_rows = slab // TR
     me, shell = lax.axis_index("pix"), lax.axis_index("shell")
-    signal_all([{"pix": flipped(me, m)} for m in range(1, groups)] + [{"shell": 1 - shell}])
+    flipped = partners(me)
+    tables = fetch(
+        zip(
+            (coef_in, dist_in, inv_in, twist_in_ref, high_in, low_in, colh_in, coll_in, backh_in, backl_in),
+            (coef_ref, dist_ref, inv_ref, twist_ref, high_ref, low_ref, colh_ref, coll_ref, backh_ref, backl_ref),
+        ),
+        tsem,
+    )
+    for copy in tables[:3]:
+        copy.wait()
+    note[...] = jnp.zeros_like(note)
+    for p in range(planes):
+        note[p : p + 1, :] = jnp.full((1, TC), coef_ref[p], jnp.float32)
+        note[planes + p : planes + p + 1, :] = jnp.full((1, TC), dist_ref[p], jnp.float32)
+    signal_all([{"pix": flipped(m)} for m in range(1, groups)] + [{"shell": 1 - shell}])
+
+    sent = pl.ds(0, cap * size + 1)
 
     def direct(p, m):
-        peer = flipped(me, m)
+        peer = flipped(m)
         return remote(
-            out_refs[p].at[peer], box.at[p, me], lsend.at[p, m], lrecv.at[p, m], {"pix": peer}
+            out_refs[p].at[peer, sent], box.at[p, me, sent], lsend.at[p, m], lrecv.at[p, m], {"pix": peer}
         )
 
     def landing(p, m):
-        peer = flipped(me, m)
+        peer = flipped(m)
         return remote(
-            out_refs[p].at[peer], box.at[p, peer], lsend.at[p, m], lrecv.at[p, m], {"pix": peer}
+            out_refs[p].at[peer, sent], box.at[p, peer, sent], lsend.at[p, m], lrecv.at[p, m], {"pix": peer}
         )
 
     def onward(p, m):
-        source = flipped(me, m)
-        first = out_refs[p].at[me] if isinstance(m, int) and m == 0 else box.at[p, source]
-        return remote(first, box.at[planes + p, source], psend.at[p, m], precv.at[p, m], {"shell": 1 - shell})
-
-    for low, high in ((1, groups // 2), (groups // 2, groups)):
+        source = flipped(m)
+        first = out_refs[p].at[me, sent] if isinstance(m, int) and m == 0 else box.at[p, source, sent]
+        return remote(first, box.at[planes + p, source, sent], psend.at[p, m], precv.at[p, m], {"shell": 1 - shell})
+
+    for m in range(1, groups):
         for p in range(planes):
-
-            def start(m, _):
-                direct(p, m).start()
-                return 0
-
-            lax.fori_loop(low, high, start, 0)
+            direct(p, m).start()
+    told = remote(note, far_note, note_sems.at[0], note_sems.at[1], {"shell": 1 - shell})
+    told.start()
     for p in range(planes):
         onward(p, 0).start()
         box[p, me] = out_refs[p][me]
@@ -485,7 +519,7 @@
 
     def near_block(m):
         def one_plane(p, _):
-            deposit(p, flipped(me, m))
+            deposit(p, flipped(m))
             return 0
 
         lax.fori_loop(0, planes, one_plane, 0)
@@ -495,7 +529,7 @@
             onward(p, m).wait_recv()
 
         def one_plane(p, _):
-            deposit(planes + p, flipped(me, m))
+            deposit(planes + p, flipped(m))
             return 0
 
         lax.fori_loop(0, planes, one_plane, 0)
@@ -507,7 +541,6 @@
 
     lag = 4
     near_block(0)
-    lax.fori_loop(0, OUTER, prepare, 0)
 
     def early(m, _):
         take(m)
@@ -530,6 +563,9 @@
 
     lax.fori_loop(groups - lag, groups, late, 0)
 
+    for copy in tables[3:]:
+        copy.wait()
+    told.wait()
     lane_id = lax.broadcasted_iota(jnp.int32, (groups, TC), 1)
     tile_id = ((lane_id % tile_rows) * OUTER + lane_id // tile_rows).astype(jnp.float32)
     gains, shifts = [[], []], [0.0, 0.0]
@@ -538,7 +574,8 @@
         hot = [jnp.where(tails[:, c : c + 1] == tile_id, 1.0, 0.0) for c in range(cap)]
         place[q] = jnp.concatenate(hot, axis=0).T.astype(jnp.bfloat16)
         total = jnp.sum(tails[:, cap : cap + 1], axis=0, keepdims=True)
-        coef, dist = tails[0:1, cap + 1 : cap + 2], tails[0:1, cap + 2 : cap + 3]
+        notes, p = (note, q) if q < planes else (far_note, q - planes)
+        coef, dist = notes[p : p + 1, 0:1], notes[planes + p : planes + p + 1, 0:1]
         for i in range(planes):
             mixed = coef * (1.0 - inv_ref[i] * dist)
             if q >= planes:
@@ -551,32 +588,47 @@
     def rows_of(c):
         return pl.ds(pl.multiple_of(c * span, span), span)
 
-    def go_copy(c, m, arriving=False):
-        peer = flipped(me, m)
+    peers = groups - 1
+
+    def go_start(c):
+        for m in range(1, groups):
+            peer = flipped(m)
+            remote(
+                sending.at[peer, :, rows_of(c), :],
+                arrived.at[me, :, rows_of(c), :],
+                fsend.at[c],
+                frecv.at[c],
+                {"pix": peer},
+            ).start()
+
+    def go_all(c):
         return remote(
-            sending.at[peer, :, rows_of(c), :],
-            arrived.at[peer if arriving else me, :, rows_of(c), :],
-            fsend.at[c, m],
-            frecv.at[c, m],
-            {"pix": peer},
+            sending.at[pl.ds(0, peers), :, rows_of(c), :],
+            arrived.at[pl.ds(0, peers), :, rows_of(c), :],
+            fsend.at[c],
+            frecv.at[c],
+            {"pix": flipped(1)},
         )
 
-    def back_copy(f, c, m, arriving=False):
-        peer = flipped(me, m)
+    def back_start(f, c):
+        for m in range(1, groups):
+            peer = flipped(m)
+            remote(
+                leaving.at[peer, f, :, rows_of(c), :],
+                landed.at[me, f, :, rows_of(c), :],
+                rsend.at[f, c],
+                rrecv.at[f, c],
+                {"pix": peer},
+            ).start()
+
+    def back_all(f, c):
         return remote(
-            leaving.at[peer, f, :, rows_of(c), :],
-            landed.at[peer if arriving else me, f, :, rows_of(c), :],
-            rsend.at[f, c, m],
-            rrecv.at[f, c, m],
-            {"pix": peer},
+            leaving.at[pl.ds(0, peers), f, :, rows_of(c), :],
+            landed.at[pl.ds(0, peers), f, :, rows_of(c), :],
+            rsend.at[f, c],
+            rrecv.at[f, c],
+            {"pix": flipped(1)},
         )
-
-    def each_peer(action):
-        def step(m, _):
-            action(m)
-            return 0
-
-        lax.fori_loop(1, groups, step, 0)
 
     def field_rows(r, n):
         return pl.ds(pl.multiple_of(r * TC + n * tile_rows, tile_rows), tile_rows)
@@ -642,7 +694,7 @@
             return 0
 
         lax.fori_loop(0, HALF_BLOCKS, block, 0)
-        each_peer(lambda m: go_copy(c, m).start())
+        go_start(c)
         for part in range(2):
             arrived[me, part, rows_of(c), :] = sending[me, part, rows_of(c), :]
         return 0
@@ -659,9 +711,19 @@
         return 0
 
     lax.fori_loop(0, tile_rows, show, 0)
+    lax.fori_loop(0, OUTER, prepare, 0)
+    for p in range(planes):
+        onward(p, 0).wait_send()
+
+        def settle(m, _):
+            direct(p, m).wait_send()
+            onward(p, m).wait_send()
+            return 0
+
+        lax.fori_loop(1, groups, settle, 0)
 
     def forward_columns(c, _):
-        each_peer(lambda m: go_copy(c, m, True).wait_recv())
+        go_all(c).wait_recv()
 
         def radix(t, _):
             rows = pl.ds(pl.multiple_of(c * span + t * 8, 8), 8)
@@ -679,6 +741,8 @@
         return 0
 
     lax.fori_loop(0, chunks, forward_columns, 0)
+    for c in range(chunks):
+        go_all(c).wait_send()
 
     def middle(j, _):
         pair = jnp.concatenate([held[2 * j + i].reshape(2 * INNER, INNER) for i in range(2)], axis=1)
@@ -716,7 +780,7 @@
             return 0
 
         lax.fori_loop(0, span // 8, radix, 0)
-        each_peer(lambda m: back_copy(f, c, m).start())
+        back_start(f, c)
         for part in range(2):
             landed[me, f, part, rows_of(c), :] = leaving[me, f, part, rows_of(c), :]
         return 0
@@ -726,7 +790,7 @@
     for f, out_ref in enumerate((one_ref, two_ref)):
 
         def inverse_rows(c, _):
-            each_peer(lambda m: back_copy(f, c, m, True).wait_recv())
+            back_all(f, c).wait_recv()
 
             def block(b, _):
                 value = jnp.concatenate(
@@ -768,22 +832,15 @@
 
         lax.fori_loop(0, chunks, inverse_rows, 0)
 
-    def drain(c, _):
-        each_peer(lambda m: go_copy(c, m).wait_send())
+    for c in range(chunks):
         for f in range(2):
-            each_peer(lambda m: back_copy(f, c, m).wait_send())
-        return 0
-
-    lax.fori_loop(0, chunks, drain, 0)
-    for p in range(planes):
-        onward(p, 0).wait_send()
-
-        def settle(m, _):
-            direct(p, m).wait_send()
-            onward(p, m).wait_send()
-            return 0
-
-        lax.fori_loop(1, groups, settle, 0)
+            back_all(f, c).wait_send()
+
+
+def place_kernel(*refs):
+    count = (len(refs) - 1) // 2
+    for copy in fetch(zip(refs[:count], refs[count:-1]), refs[-1]):
+        copy.wait()
 
 
 def column_info(me, groups):
@@ -797,15 +854,18 @@
     return jnp.where(mine >= L // 2, mine - L, mine).astype(jnp.float32), weight
 
 
-def call(body, outs, scratch=(), smem=(0,), count=1, megabytes=48, flops=0, group=None):
+def call(body, outs, scratch=(), smem=(0,), count=1, megabytes=48, flops=0, group=None, hbm=(), out_space=pltpu.VMEM):
     space = [
-        pl.BlockSpec(memory_space=pltpu.SMEM if i in smem else pltpu.VMEM) for i in range(count)
+        pl.BlockSpec(
+            memory_space=pltpu.SMEM if i in smem else pltpu.HBM if i in hbm else pltpu.VMEM
+        )
+        for i in range(count)
     ]
     return pl.pallas_call(
         body,
         out_shape=outs,
         in_specs=space,
-        out_specs=jax.tree.map(lambda _: pl.BlockSpec(memory_space=pltpu.VMEM), outs),
+        out_specs=jax.tree.map(lambda _: pl.BlockSpec(memory_space=out_space), outs),
         scratch_shapes=list(scratch),
         compiler_params=pltpu.CompilerParams(
             vmem_limit_bytes=megabytes << 20,
@@ -832,11 +892,20 @@
     outgoing = call(
         pack_kernel,
         [shape(groups, message, TC)] * planes,
-        [vmem(size, local_tiles, TC), pltpu.SMEM((groups,), jnp.int32)],
-        smem=(0, 1, 2),
-        count=5,
-        flops=1 << 20,
-    )(block_tile, plane_coef, plane_dist, cell_index, masses)
+        [
+            pltpu.SMEM(block_tile.shape, jnp.int32),
+            pltpu.VMEM(cell_index.shape, jnp.int32),
+            pltpu.VMEM(masses.shape, jnp.bfloat16),
+            vmem(size, local_tiles, TC),
+            pltpu.SMEM((groups,), jnp.int32),
+            dma(3),
+        ],
+        smem=(),
+        hbm=(0, 1, 2),
+        count=3,
+        megabytes=16,
+        flops=1 << 32,
+    )(block_tile, cell_index, masses)
 
     order = row_order(slab)
     row_high, row_low = row_tables()
@@ -845,10 +914,17 @@
     back_high, back_low = split_table(natural.T)
     span = slab // CHUNKS
     pitch = 3 * TR // 2
-    return call(
+    tables = [jnp.asarray(twiddle_tables(order)), row_high, row_low, col_high, col_low, back_high, back_low]
+    results = call(
         lensing_kernel,
         [shape(planes, slab, L)] * 3,
-        [
+        [pltpu.SMEM(source_inv.shape, jnp.float32)] * 3
+        + [pltpu.VMEM(table.shape, table.dtype) for table in tables]
+        + [
+            dma(3 + len(tables)),
+            vmem(8, TC),
+            vmem(8, TC),
+            dma(2),
             vmem(2 * planes, groups, message, TC),
             vmem(2 * planes, cap * groups * pitch, TC),
             pltpu.VMEM((2 * planes, TC, TC), jnp.bfloat16),
@@ -866,20 +942,28 @@
             dma(planes, groups),
             dma(planes, groups),
             dma(planes, groups),
-            dma(CHUNKS, groups),
-            dma(CHUNKS, groups),
-            dma(2, CHUNKS, groups),
-            dma(2, CHUNKS, groups),
+            dma(CHUNKS),
+            dma(CHUNKS),
+            dma(2, CHUNKS),
+            dma(2, CHUNKS),
         ],
-        smem=(2,),
-        count=10,
-        megabytes=58,
+        smem=(),
+        hbm=tuple(range(2, 12)),
+        count=12,
+        megabytes=40,
         flops=1 << 32,
         group=0,
-    )(
-        *outgoing, source_inv, jnp.asarray(twiddle_tables(order)), row_high, row_low,
-        col_high, col_low, back_high, back_low,
-    )
+    )(*outgoing, plane_coef, plane_dist, source_inv, *tables)
+    return call(
+        place_kernel,
+        [shape(planes, slab, L)] * 3,
+        [dma(3)],
+        smem=(),
+        out_space=pltpu.HBM,
+        count=3,
+        megabytes=16,
+        flops=1 << 20,
+    )(*results)
 
 
 def solution(mesh):

time: 217 us -> 195 us (0.90)
  Pallas kernels: 203 us -> 191 us
  local copies, waits for them, and re-layouts: 12.4 us -> 2.6 us
    pallas_call x2 -> x3, Pallas kernels: 203 us -> 191 us  [the longest x1 185 us: local_fast(): call(lensing_kernel, [shape(planes, slab, L)] * 3, [pltpu.SMEM(source_inv...]
    unnamed x21 -> x26, local copies, waits for them, and re-layouts: 12.4 us -> 2.6 us
where the time goes in v3:
time: 195 us; the launch traced here: 194 us
  Pallas kernels  191 us (98%)
  local copies, waits for them, and re-layouts  2.6 us (1%)
    pallas_call x1, Pallas kernels, local_fast(): call(lensing_kernel, [shape(planes, slab, L)] * 3, [pltpu.SMEM(source_inv...  185 us

profile of v3, /device:TPU:1, one launch (start us, length us, event | category | flops | bytes accessed | tf_op | source)
XLA Modules:
  0.0 194.0 jit_solution(8379642384254051779)
XLA Ops:
  0.6 0.0 copy-start
  0.6 0.9 copy-done
  1.6 0.0 copy-start.1
  1.6 0.9 copy-done.1
  2.5 0.0 copy-start.2
  2.5 0.7 copy-done.2
  3.2 0.0 copy-start.3
  3.2 0.0 copy-start.4
  3.2 0.0 copy-start.5
  3.2 0.0 copy-start.6
  3.2 0.0 copy-start.7
  3.2 0.0 copy-start.8
  3.2 0.0 copy-start.9
  3.2 0.0 copy-start.10
  3.2 0.0 copy-start.11
  3.3 0.0 copy-start.12
  3.3 2.5 %shard_map.148 = (f32[16,72,128]{2,1,0:T(8,128)S(1)}, f32[16,72,128]{2,1,0:T(8,128)S(1)}) custom-call(s32[2,1024]{1,0:T(2,128)S(1)} %copy-done.2, s32[2,64,512]{2,1,0:T(8,128)S(1)} %copy-done, bf16[2,64,512]{2,1,0:T(8,128)(2,1)S(1)} %copy-done.1), custom_call_target="tpu_custom_call" | custom-call | flops 4294967296 | bytes 4194304 | tf_op jit(solution)/shard_map/pallas_call | solution.py:892
  5.8 0.0 copy-done.3
  5.8 0.0 copy-done.4
  5.8 0.0 copy-done.5
  5.8 0.0 copy-done.6
  5.8 0.0 copy-done.7
  5.8 0.0 copy-done.8
  5.8 0.0 copy-done.9
  5.8 0.0 copy-done.10
  5.8 0.0 copy-done.11
  5.9 0.0 copy-done.12
  5.9 185.4 %shard_map.149 = (f32[2,128,2048]{2,1,0:T(8,128)S(1)}, f32[2,128,2048]{2,1,0:T(8,128)S(1)}, f32[2,128,2048]{2,1,0:T(8,128)S(1)}) custom-call(f32[16,72,128]{2,1,0:T(8,128)S(1)} %get-tuple-element.8.out0, f32[16,72,128]{2,1,0:T(8,128)S(1)} %get-tuple-element.9.out1, f32[2]{0:T(128)S(1)} %copy-done.3, f32[2]{0:T(128)S(1)} %copy-done.4, f32[2]{0:T(128)S(1)} %copy-done.5, ...), custom_call_target="tpu_custom_call" | custom-call | flops 4294967296 | bytes 4194304 | tf_op jit(solution)/shard_map/pallas_call | solution.py:918
  191.3 2.7 %shard_map.150 = (f32[2,128,2048]{2,1,0:T(8,128)}, f32[2,128,2048]{2,1,0:T(8,128)}, f32[2,128,2048]{2,1,0:T(8,128)}) custom-call(f32[2,128,2048]{2,1,0:T(8,128)S(1)} %get-tuple-element.10.refs_0_, f32[2,128,2048]{2,1,0:T(8,128)S(1)} %get-tuple-element.11.refs_1_, f32[2,128,2048]{2,1,0:T(8,128)S(1)} %get-tuple-element.12.refs_2_), custom_call_target="tpu_custom_call" | custom-call | flops 1048576 | bytes 4194304 | tf_op jit(solution)/shard_map/pallas_call | solution.py:957
Async XLA Ops:
  0.6 1.0 copy-start
  1.6 0.9 copy-start.1
  2.5 0.7 copy-start.2
  3.2 2.6 %copy-start.3 = (f32[2]{0:T(128)S(1)}, f32[2]{0:T(128)}, u32[]{:S(2)}) copy-start(f32[2]{0:T(128)} %coef_in.1) | copy-start | bytes 28
  3.2 2.6 %copy-start.4 = (f32[2]{0:T(128)S(1)}, f32[2]{0:T(128)}, u32[]{:S(2)}) copy-start(f32[2]{0:T(128)} %dist_in.1) | copy-start | bytes 28
  3.2 2.6 %copy-start.5 = (f32[2]{0:T(128)S(1)}, f32[2]{0:T(128)}, u32[]{:S(2)}) copy-start(f32[2]{0:T(128)} %inv_in.1) | copy-start | bytes 28
  3.2 2.6 %copy-start.6 = (bf16[8,256,256]{2,1,0:T(8,128)(2,1)S(1)}, bf16[8,256,256]{2,1,0:T(8,128)(2,1)}, u32[]{:S(2)}) copy-start(bf16[8,256,256]{2,1,0:T(8,128)(2,1)} %constant.16.clone.low_in) | copy-start | bytes 3145732
  3.2 2.6 %copy-start.7 = (bf16[8,256,256]{2,1,0:T(8,128)(2,1)S(1)}, bf16[8,256,256]{2,1,0:T(8,128)(2,1)}, u32[]{:S(2)}) copy-start(bf16[8,256,256]{2,1,0:T(8,128)(2,1)} %constant.15.clone.high_in) | copy-start | bytes 3145732
  3.2 2.6 %copy-start.8 = (bf16[256,256]{1,0:T(8,128)(2,1)S(1)}, bf16[256,256]{1,0:T(8,128)(2,1)}, u32[]{:S(2)}) copy-start(bf16[256,256]{1,0:T(8,128)(2,1)} %constant.20.clone.backl_in) | copy-start | bytes 393220
  3.2 2.6 %copy-start.9 = (bf16[256,256]{1,0:T(8,128)(2,1)S(1)}, bf16[256,256]{1,0:T(8,128)(2,1)}, u32[]{:S(2)}) copy-start(bf16[256,256]{1,0:T(8,128)(2,1)} %constant.19.clone.backh_in) | copy-start | bytes 393220
  3.2 2.6 %copy-start.10 = (bf16[256,256]{1,0:T(8,128)(2,1)S(1)}, bf16[256,256]{1,0:T(8,128)(2,1)}, u32[]{:S(2)}) copy-start(bf16[256,256]{1,0:T(8,128)(2,1)} %constant.18.clone.coll_in) | copy-start | bytes 393220
  3.2 2.6 %copy-start.11 = (bf16[256,256]{1,0:T(8,128)(2,1)S(1)}, bf16[256,256]{1,0:T(8,128)(2,1)}, u32[]{:S(2)}) copy-start(bf16[256,256]{1,0:T(8,128)(2,1)} %constant.17.clone.colh_in) | copy-start | bytes 393220
  3.3 2.6 %copy-start.12 = (f32[4,16,128]{2,1,0:T(8,128)S(1)}, f32[4,16,128]{2,1,0:T(8,128)}, u32[]{:S(2)}) copy-start(f32[4,16,128]{2,1,0:T(8,128)} %constant.14.clone.twist_in_ref) | copy-start | bytes 98308

commit v4 on v3

--- a/solution.py
+++ b/solution.py
@@ -246,7 +246,7 @@
     return high, low
 
 
-def row_tables():
+def row_tables(chunks):
     n2 = np.arange(INNER)
     out = np.zeros((HALF_BLOCKS, 2 * INNER, 2 * INNER))
     cols = block_columns()
@@ -261,7 +261,8 @@
             out[b, :INNER, INNER : INNER + h] = -si[:, :h]
             out[b, INNER:, h:INNER] = co[:, h:]
             out[b, INNER:, INNER + h :] = -si[:, h:]
-    return split_table(out)
+    out = out.reshape(HALF_BLOCKS, 2 * INNER, 2, chunks, INNER // chunks)
+    return split_table(out.transpose(0, 3, 2, 4, 1).reshape(HALF_BLOCKS, 2 * INNER, 2 * INNER))
 
 
 def row_order(slab):
@@ -417,7 +418,7 @@
     conv_ref, one_ref, two_ref,
     coef_ref, dist_ref, inv_ref, twist_ref, high_ref, low_ref, colh_ref, coll_ref, backh_ref, backl_ref,
     tsem, note, far_note, note_sems,
-    box, slots, place, field, held_row, sending, arrived, held, twist_in, kern, back, leaving, landed,
+    box, slots, place, field, held_row, sending, arrived, held, kern, back, leaving, landed, total_rows,
     lsend, lrecv, psend, precv, fsend, frecv, rsend, rrecv,
 ):
     out_refs = (out0, out1)
@@ -427,8 +428,10 @@
     half = 4
     size = 2 * half
     cap = message // size - 1
-    span = held_row.shape[2]
-    chunks = slab // span
+    chunks = sending.shape[1]
+    span = INNER // chunks
+    both = chunks - 1
+    flip = groups // 2
     pitch = slots.shape[1] // (cap * groups)
     tile_rows = slab // TR
     me, shell = lax.axis_index("pix"), lax.axis_index("shell")
@@ -476,12 +479,14 @@
         onward(p, 0).start()
         box[p, me] = out_refs[p][me]
 
-    signed_v, weight = column_info(me, groups)
-    inner_id = lax.broadcasted_iota(jnp.int32, (INNER, INNER), 0)
+    own_lines, mirror_lines = column_info(me), column_info((me + flip) % groups)
+    signed_v, weight = (
+        jnp.concatenate([ours, theirs[both * span :]], axis=0)
+        for ours, theirs in zip(own_lines, mirror_lines)
+    )
+    inner_id = lax.broadcasted_iota(jnp.int32, (INNER + span, INNER), 1)
 
     def prepare(k, _):
-        for i in range(4):
-            twist_in[i, k] = jnp.broadcast_to(twist_ref[i, pl.ds(k, 1), :], (INNER, INNER)).T
         u = k + OUTER * inner_id
         signed_u = jnp.where(u >= L // 2, u - L, u).astype(jnp.float32)
         scale = jnp.where(u == L // 2, 0.0, weight)
@@ -565,7 +570,7 @@
 
     for copy in tables[3:]:
         copy.wait()
-    told.wait()
+    told.wait_recv()
     lane_id = lax.broadcasted_iota(jnp.int32, (groups, TC), 1)
     tile_id = ((lane_id % tile_rows) * OUTER + lane_id // tile_rows).astype(jnp.float32)
     gains, shifts = [[], []], [0.0, 0.0]
@@ -585,121 +590,98 @@
             gains[i].append(mixed * ((L * L) / total))
             shifts[i] = shifts[i] + mixed
 
-    def rows_of(c):
-        return pl.ds(pl.multiple_of(c * span, span), span)
-
     peers = groups - 1
 
-    def go_start(c):
-        for m in range(1, groups):
-            peer = flipped(m)
-            remote(
-                sending.at[peer, :, rows_of(c), :],
-                arrived.at[me, :, rows_of(c), :],
-                fsend.at[c],
-                frecv.at[c],
-                {"pix": peer},
-            ).start()
+    def go(c, peer):
+        source = sending.at[peer, c] if c < chunks else sending.at[(peer + flip) % groups, both]
+        return remote(source, arrived.at[me, c], fsend.at[c], frecv.at[c], {"pix": peer})
 
     def go_all(c):
+        every = pl.ds(0, peers)
         return remote(
-            sending.at[pl.ds(0, peers), :, rows_of(c), :],
-            arrived.at[pl.ds(0, peers), :, rows_of(c), :],
-            fsend.at[c],
-            frecv.at[c],
-            {"pix": flipped(1)},
+            sending.at[every, 0], arrived.at[every, c], fsend.at[c], frecv.at[c], {"pix": flipped(1)}
         )
 
-    def back_start(f, c):
-        for m in range(1, groups):
-            peer = flipped(m)
-            remote(
-                leaving.at[peer, f, :, rows_of(c), :],
-                landed.at[me, f, :, rows_of(c), :],
-                rsend.at[f, c],
-                rrecv.at[f, c],
-                {"pix": peer},
-            ).start()
-
-    def back_all(f, c):
+    def home_any(c, count=peers):
+        every = pl.ds(0, count)
         return remote(
-            leaving.at[pl.ds(0, peers), f, :, rows_of(c), :],
-            landed.at[pl.ds(0, peers), f, :, rows_of(c), :],
-            rsend.at[f, c],
-            rrecv.at[f, c],
-            {"pix": flipped(1)},
+            leaving.at[every, c], landed.at[every, 0], rsend.at[c], rrecv.at[c], {"pix": flipped(1)}
         )
+
+    def home_all(c):
+        return home_any(c, peers if c < both else flip - 1)
 
     def field_rows(r, n):
         return pl.ds(pl.multiple_of(r * TC + n * tile_rows, tile_rows), tile_rows)
 
-    def forward_rows(c, _):
-        def mass_rows(j, _):
-            r = c * (span // tile_rows) + 2 * j
-            sums = []
-            for q in range(2 * planes):
-                pair = jnp.concatenate(
-                    [slots[q, pl.ds(r + i, cap * groups, stride=pitch), :] for i in range(2)], axis=1
-                )
-                high = pair.astype(jnp.bfloat16)
-                rest = pair - high.astype(jnp.float32)
-                middle = rest.astype(jnp.bfloat16)
-                low = (rest - middle.astype(jnp.float32)).astype(jnp.bfloat16)
-                dot = lambda part: jnp.dot(place[q], part, preferred_element_type=jnp.float32)
-                sums.append(dot(high) + (dot(middle) + dot(low)))
-            for i in range(planes):
-                value = gains[i][0] * sums[0]
-                for q in range(1, 2 * planes):
-                    value = value + gains[i][q] * sums[q]
-                value = value - shifts[i]
-                for e in range(2):
-                    at = pl.ds(pl.multiple_of((r + e) * TC, TC), TC)
-                    field[i, at, :] = value[:, e * TC : (e + 1) * TC]
-            return 0
-
-        lax.fori_loop(0, span // tile_rows // 2, mass_rows, 0)
-
-        def radix(j, _):
-            r = c * (span // tile_rows) + j
-            near = pl.ds(pl.multiple_of(j * tile_rows, tile_rows), tile_rows)
-            z = fft_list(
-                [
-                    tuple(field[i, field_rows(r, n), :] for i in range(2))
-                    for n in range(OUTER)
-                ],
-                -1,
+    def mass_rows(j, _):
+        r = 2 * j
+        sums = []
+        for q in range(2 * planes):
+            pair = jnp.concatenate(
+                [slots[q, pl.ds(r + i, cap * groups, stride=pitch), :] for i in range(2)], axis=1
             )
-            for k in range(1, HALF_BLOCKS):
-                (ar, ai), (br, bi) = z[k], z[OUTER - k]
-                held_row[k - 1, 0, near, :INNER] = 0.5 * (ar + br)
-                held_row[k - 1, 0, near, INNER:] = 0.5 * (ai - bi)
-                held_row[k - 1, 1, near, :INNER] = 0.5 * (ai + bi)
-                held_row[k - 1, 1, near, INNER:] = 0.5 * (br - ar)
-            for p in range(2):
-                held_row[HALF_BLOCKS - 1, p, near, :INNER] = z[0][p]
-                held_row[HALF_BLOCKS - 1, p, near, INNER:] = z[HALF_BLOCKS][p]
-            return 0
-
-        lax.fori_loop(0, span // tile_rows, radix, 0)
-
-        def block(j, _):
-            b = (me // 2 + 1 + j) % HALF_BLOCKS
-            value = held_row[b].reshape(2 * span, 2 * INNER)
-            result = three_pass(split_value(value), (high_ref[b], low_ref[b]), ((1,), (0,)))
-            for p in range(2):
-                for part in range(2):
-                    sending[2 * b + p, part, rows_of(c), :] = result[
-                        p * span : (p + 1) * span, part * INNER : (part + 1) * INNER
-                    ]
-            return 0
-
-        lax.fori_loop(0, HALF_BLOCKS, block, 0)
-        go_start(c)
-        for part in range(2):
-            arrived[me, part, rows_of(c), :] = sending[me, part, rows_of(c), :]
-        return 0
-
-    lax.fori_loop(0, chunks, forward_rows, 0)
+            high = pair.astype(jnp.bfloat16)
+            rest = pair - high.astype(jnp.float32)
+            middle = rest.astype(jnp.bfloat16)
+            low = (rest - middle.astype(jnp.float32)).astype(jnp.bfloat16)
+            dot = lambda part: jnp.dot(place[q], part, preferred_element_type=jnp.float32)
+            sums.append(dot(high) + (dot(middle) + dot(low)))
+        for i in range(planes):
+            value = gains[i][0] * sums[0]
+            for q in range(1, 2 * planes):
+                value = value + gains[i][q] * sums[q]
+            value = value - shifts[i]
+            for e in range(2):
+                at = pl.ds(pl.multiple_of((r + e) * TC, TC), TC)
+                field[i, at, :] = value[:, e * TC : (e + 1) * TC]
+        return 0
+
+    lax.fori_loop(0, TR // 2, mass_rows, 0)
+
+    def row_radix(r, _):
+        near = pl.ds(pl.multiple_of(r * tile_rows, tile_rows), tile_rows)
+        z = fft_list(
+            [tuple(field[i, field_rows(r, n), :] for i in range(2)) for n in range(OUTER)], -1
+        )
+        for k in range(1, HALF_BLOCKS):
+            (ar, ai), (br, bi) = z[k], z[OUTER - k]
+            held_row[k - 1, 0, near, :INNER] = 0.5 * (ar + br)
+            held_row[k - 1, 0, near, INNER:] = 0.5 * (ai - bi)
+            held_row[k - 1, 1, near, :INNER] = 0.5 * (ai + bi)
+            held_row[k - 1, 1, near, INNER:] = 0.5 * (br - ar)
+        for p in range(2):
+            held_row[HALF_BLOCKS - 1, p, near, :INNER] = z[0][p]
+            held_row[HALF_BLOCKS - 1, p, near, INNER:] = z[HALF_BLOCKS][p]
+        return 0
+
+    lax.fori_loop(0, TR, row_radix, 0)
+
+    def row_block(b):
+        value = held_row[b].reshape(2 * slab, 2 * INNER)
+        result = three_pass((high_ref[b], low_ref[b]), split_value(value), ((1,), (1,)))
+        for p in range(2):
+            for c in range(chunks):
+                sending[2 * b + p, c] = result[
+                    2 * span * c : 2 * span * (c + 1), p * slab : (p + 1) * slab
+                ]
+
+    def send_block(j, _):
+        b = (me // 2 + 1 + j) % HALF_BLOCKS
+        row_block(b)
+        for p in range(2):
+            for c in (both, chunks):
+                peer = 2 * b + p if c < chunks else (2 * b + p + flip) % groups
+                pl.when(peer != me)(lambda: go(c, peer).start())
+        return 0
+
+    lax.fori_loop(0, HALF_BLOCKS, send_block, 0)
+    for c in range(both):
+        for m in range(1, groups):
+            go(c, flipped(m)).start()
+    for c in range(chunks):
+        arrived[me, c] = sending[me, c]
+    arrived[me, chunks] = sending[(me + flip) % groups, both]
 
     def show(t, _):
         for i in range(planes):
@@ -710,8 +692,70 @@
                     conv_ref[i, rows, n * TC : (n + 1) * TC] = field[i, held_at, :]
         return 0
 
+    lax.fori_loop(0, OUTER, prepare, 0)
+
+    def columns(c):
+        for t in range(span // 8):
+            at, past = slice(t * 8, t * 8 + 8), slice(span + t * 8, span + t * 8 + 8)
+            z = fft_list([(arrived[n, c, at, :], arrived[n, c, past, :]) for n in range(OUTER)], -1)
+            for k in range(OUTER):
+                re, im = z[k]
+                if k:
+                    cs, sn = twist_ref[0, k : k + 1, :], twist_ref[1, k : k + 1, :]
+                    re, im = re * cs - im * sn, re * sn + im * cs
+                rows = slice(k * span + t * 8, k * span + t * 8 + 8)
+                held[rows, :INNER] = re
+                held[rows, INNER:] = im
+        rank = pl.ds(pl.multiple_of(c * span, span), span)
+        part = 2 * INNER // span
+        for g in range(OUTER // part):
+            value = held[g * part * span : (g + 1) * part * span, :]
+            spectrum = three_pass(split_value(value), (colh_ref[...], coll_ref[...]), ((1,), (0,)))
+            for f in range(2):
+                gain = kern[f, g * part : (g + 1) * part, rank, :].reshape(part * span, INNER)
+                shaped = spectrum * jnp.concatenate([gain, gain], axis=1)
+                result = three_pass(split_value(shaped), (backh_ref[...], backl_ref[...]), ((1,), (0,)))
+                for i in range(part):
+                    k = g * part + i
+                    re, im = result[i * span : (i + 1) * span, :INNER], result[i * span : (i + 1) * span, INNER:]
+                    cs, sn = twist_ref[2, k : k + 1, :], twist_ref[3, k : k + 1, :]
+                    back[f, k, :, :INNER] = re * cs + im * sn
+                    back[f, k, :, INNER:] = im * cs - re * sn
+        for f in range(2):
+            for t in range(span // 8):
+                at, past = slice(t * 8, t * 8 + 8), slice(span + t * 8, span + t * 8 + 8)
+                x = fft_list([(back[f, k, at, :INNER], back[f, k, at, INNER:]) for k in range(OUTER)], 1)
+                for n in range(OUTER):
+                    leaving[n, c, f, at, :] = x[n][0]
+                    leaving[n, c, f, past, :] = x[n][1]
+
+    def send_home(c, masks, slot):
+        for m in masks:
+            peer = flipped(m)
+            remote(
+                leaving.at[peer, c], landed.at[slot[0], slot[1]], rsend.at[c], rrecv.at[c], {"pix": peer}
+            ).start()
+        landed[slot[0], slot[1]] = leaving[me, c]
+
+    def shared_columns(c, _):
+        go_all(c).wait_recv()
+        columns(c)
+        send_home(c, range(1, flip), ((me + (c - both) * flip) % groups, both))
+        return 0
+
+    lax.fori_loop(both, chunks + 1, shared_columns, 0)
+
+    def single_columns(c, _):
+        go_all(c).wait_recv()
+        columns(c)
+        send_home(c, range(1, groups), (me, c))
+        return 0
+
+    lax.fori_loop(0, both, single_columns, 0)
     lax.fori_loop(0, tile_rows, show, 0)
-    lax.fori_loop(0, OUTER, prepare, 0)
+    for c in range(chunks + 1):
+        go_all(c).wait_send()
+    told.wait_send()
     for p in range(planes):
         onward(p, 0).wait_send()
 
@@ -722,119 +766,58 @@
 
         lax.fori_loop(1, groups, settle, 0)
 
-    def forward_columns(c, _):
-        go_all(c).wait_recv()
+    def gather(c, first):
+        def block(b, _):
+            at = pl.ds(pl.multiple_of(c * 2 * span, 2 * span), 2 * span)
+            high, low = high_ref[b, at, :], low_ref[b, at, :]
+            table = jnp.concatenate([high, high, low], axis=0)
+            for f in range(2):
+                value = jnp.concatenate([landed[2 * b + p, c, f] for p in range(2)], axis=1)
+                top, rest = split_value(value)
+                result = lax.dot_general(
+                    jnp.concatenate([top, rest, top], axis=0),
+                    table,
+                    (((0,), (0,)), ((), ())),
+                    preferred_element_type=jnp.float32,
+                ).reshape(2, slab, 2 * INNER)
+                total_rows[f, b] = result if first else total_rows[f, b] + result
+            return 0
+
+        lax.fori_loop(0, HALF_BLOCKS, block, 0)
+
+    home_all(both).wait_recv()
+    home_all(chunks).wait_recv()
+    gather(both, True)
+
+    def more(c, _):
+        home_any(c).wait_recv()
+        gather(c, False)
+        return 0
+
+    lax.fori_loop(0, both, more, 0)
+    for f, out_ref in enumerate((one_ref, two_ref)):
 
         def radix(t, _):
-            rows = pl.ds(pl.multiple_of(c * span + t * 8, 8), 8)
-            z = fft_list([(arrived[n, 0, rows, :], arrived[n, 1, rows, :]) for n in range(OUTER)], -1)
-            for k in range(OUTER):
-                re, im = z[k]
-                if k:
-                    cs, sn = twist_in[0, k, rows, :], twist_in[1, k, rows, :]
-                    re, im = re * cs - im * sn, re * sn + im * cs
-                held[k, 0, rows, :] = re
-                held[k, 1, rows, :] = im
+            rows = pl.ds(pl.multiple_of(t * 8, 8), 8)
+            at = lambda k, p, part: total_rows[f, k, p, rows, part * INNER : (part + 1) * INNER]
+            z = [None] * OUTER
+            last = HALF_BLOCKS - 1
+            z[0] = (at(last, 0, 0), at(last, 1, 0))
+            z[HALF_BLOCKS] = (at(last, 0, 1), at(last, 1, 1))
+            for k in range(1, HALF_BLOCKS):
+                ar, ai = at(k - 1, 0, 0), at(k - 1, 0, 1)
+                br, bi = at(k - 1, 1, 0), at(k - 1, 1, 1)
+                z[k] = (ar - bi, ai + br)
+                z[OUTER - k] = (ar + bi, br - ai)
+            x = fft_list(z, 1)
+            for n in range(OUTER):
+                for p in range(2):
+                    out_ref[p, rows, n * INNER : (n + 1) * INNER] = x[n][p]
             return 0
 
-        lax.fori_loop(0, span // 8, radix, 0)
-        return 0
-
-    lax.fori_loop(0, chunks, forward_columns, 0)
-    for c in range(chunks):
-        go_all(c).wait_send()
-
-    def middle(j, _):
-        pair = jnp.concatenate([held[2 * j + i].reshape(2 * INNER, INNER) for i in range(2)], axis=1)
-        spectrum = three_pass((colh_ref[...], coll_ref[...]), split_value(pair), ((1,), (0,)))
-        for i in range(2):
-            k = 2 * j + i
-            mine = spectrum[:, i * INNER : (i + 1) * INNER]
-            fields = jnp.concatenate(
-                [
-                    jnp.concatenate([mine[:INNER] * kern[f, k], mine[INNER:] * kern[f, k]], axis=0)
-                    for f in range(2)
-                ],
-                axis=1,
-            )
-            result = three_pass((backh_ref[...], backl_ref[...]), split_value(fields), ((1,), (0,)))
-            cs, sn = twist_in[2, k], twist_in[3, k]
-            for f in range(2):
-                at = slice(f * INNER, (f + 1) * INNER)
-                re, im = result[:INNER, at], result[INNER:, at]
-                back[f, k, 0] = re * cs + im * sn
-                back[f, k, 1] = im * cs - re * sn
-        return 0
-
-    lax.fori_loop(0, OUTER // 2, middle, 0)
-
-    def inverse_columns(q, _):
-        f, c = q // chunks, q % chunks
-
-        def radix(t, _):
-            rows = pl.ds(pl.multiple_of(c * span + t * 8, 8), 8)
-            x = fft_list([(back[f, k, 0, rows, :], back[f, k, 1, rows, :]) for k in range(OUTER)], 1)
-            for n in range(OUTER):
-                leaving[n, f, 0, rows, :] = x[n][0]
-                leaving[n, f, 1, rows, :] = x[n][1]
-            return 0
-
-        lax.fori_loop(0, span // 8, radix, 0)
-        back_start(f, c)
-        for part in range(2):
-            landed[me, f, part, rows_of(c), :] = leaving[me, f, part, rows_of(c), :]
-        return 0
-
-    lax.fori_loop(0, 2 * chunks, inverse_columns, 0)
-
-    for f, out_ref in enumerate((one_ref, two_ref)):
-
-        def inverse_rows(c, _):
-            back_all(f, c).wait_recv()
-
-            def block(b, _):
-                value = jnp.concatenate(
-                    [
-                        jnp.concatenate(
-                            [landed[2 * b + p, f, part, rows_of(c), :] for part in range(2)], axis=1
-                        )
-                        for p in range(2)
-                    ],
-                    axis=0,
-                )
-                held_row[b] = three_pass(
-                    split_value(value), (high_ref[b], low_ref[b]), ((1,), (1,))
-                ).reshape(2, span, 2 * INNER)
-                return 0
-
-            lax.fori_loop(0, HALF_BLOCKS, block, 0)
-
-            def radix(t, _):
-                near = pl.ds(pl.multiple_of(t * 8, 8), 8)
-                rows = pl.ds(pl.multiple_of(c * span + t * 8, 8), 8)
-                z = [None] * OUTER
-                last = HALF_BLOCKS - 1
-                z[0] = (held_row[last, 0, near, :INNER], held_row[last, 1, near, :INNER])
-                z[HALF_BLOCKS] = (held_row[last, 0, near, INNER:], held_row[last, 1, near, INNER:])
-                for k in range(1, HALF_BLOCKS):
-                    ar, ai = held_row[k - 1, 0, near, :INNER], held_row[k - 1, 0, near, INNER:]
-                    br, bi = held_row[k - 1, 1, near, :INNER], held_row[k - 1, 1, near, INNER:]
-                    z[k] = (ar - bi, ai + br)
-                    z[OUTER - k] = (ar + bi, br - ai)
-                x = fft_list(z, 1)
-                for n in range(OUTER):
-                    for p in range(2):
-                        out_ref[p, rows, n * INNER : (n + 1) * INNER] = x[n][p]
-                return 0
-
-            lax.fori_loop(0, span // 8, radix, 0)
-            return 0
-
-        lax.fori_loop(0, chunks, inverse_rows, 0)
-
-    for c in range(chunks):
-        for f in range(2):
-            back_all(f, c).wait_send()
+        lax.fori_loop(0, slab // 8, radix, 0)
+    for c in range(chunks + 1):
+        home_all(c).wait_send()
 
 
 def place_kernel(*refs):
@@ -843,13 +826,13 @@
         copy.wait()
 
 
-def column_info(me, groups):
-    lane = lax.broadcasted_iota(jnp.int32, (1, INNER), 1)
+def column_info(me):
+    line = lax.broadcasted_iota(jnp.int32, (INNER, INNER), 0)
     b = me // 2
     last = b == HALF_BLOCKS - 1
-    upper = lane // (INNER // 2)
-    folded = OUTER * (lane - upper * (INNER // 2)) + HALF_BLOCKS * upper
-    mine = jnp.where(last, folded, b + 1 + OUTER * lane)
+    upper = line // (INNER // 2)
+    folded = OUTER * (line - upper * (INNER // 2)) + HALF_BLOCKS * upper
+    mine = jnp.where(last, folded, b + 1 + OUTER * line)
     weight = jnp.where(last & (mine > 0), 2.0, 1.0) / (L * L)
     return jnp.where(mine >= L // 2, mine - L, mine).astype(jnp.float32), weight
 
@@ -908,11 +891,10 @@
     )(block_tile, cell_index, masses)
 
     order = row_order(slab)
-    row_high, row_low = row_tables()
-    forth, natural = column_table(order), column_table(np.arange(INNER))
-    col_high, col_low = split_table(forth)
-    back_high, back_low = split_table(natural.T)
-    span = slab // CHUNKS
+    row_high, row_low = row_tables(CHUNKS)
+    col_high, col_low = split_table(column_table(order).T)
+    back_high, back_low = split_table(column_table(np.arange(INNER)))
+    span = INNER // CHUNKS
     pitch = 3 * TR // 2
     tables = [jnp.asarray(twiddle_tables(order)), row_high, row_low, col_high, col_low, back_high, back_low]
     results = call(
@@ -929,23 +911,23 @@
             vmem(2 * planes, cap * groups * pitch, TC),
             pltpu.VMEM((2 * planes, TC, TC), jnp.bfloat16),
             vmem(planes, TR * TC, TC),
-            vmem(HALF_BLOCKS, planes, span, 2 * INNER),
-            vmem(groups, 2, slab, INNER),
-            vmem(groups, 2, slab, INNER),
-            vmem(OUTER, 2, INNER, INNER),
-            vmem(4, OUTER, INNER, INNER),
-            vmem(2, OUTER, INNER, INNER),
-            vmem(2, OUTER, 2, INNER, INNER),
-            vmem(groups, 2, 2, slab, INNER),
-            vmem(groups, 2, 2, slab, INNER),
+            vmem(HALF_BLOCKS, planes, slab, 2 * INNER),
+            vmem(groups, CHUNKS, 2 * span, slab),
+            vmem(groups, CHUNKS + 1, 2 * span, slab),
+            vmem(OUTER * span, 2 * INNER),
+            vmem(2, OUTER, INNER + span, INNER),
+            vmem(2, OUTER, span, 2 * INNER),
+            vmem(groups, CHUNKS + 1, 2, 2 * span, slab),
+            vmem(groups, CHUNKS, 2, 2 * span, slab),
+            vmem(2, HALF_BLOCKS, planes, slab, 2 * INNER),
             dma(planes, groups),
             dma(planes, groups),
             dma(planes, groups),
             dma(planes, groups),
-            dma(CHUNKS),
-            dma(CHUNKS),
-            dma(2, CHUNKS),
-            dma(2, CHUNKS),
+            dma(CHUNKS + 1),
+            dma(CHUNKS + 1),
+            dma(CHUNKS + 1),
+            dma(CHUNKS + 1),
         ],
         smem=(),
         hbm=tuple(range(2, 12)),

time: 195 us -> 179 us (0.918); the launches traced: 194 us -> 176 us
  Pallas kernels: 191 us -> 172 us
    pallas_call x1, Pallas kernels: 185 us -> 167 us  [local_fast(): call(lensing_kernel, [shape(planes, slab, L)] * 3, [pltpu.SMEM(source_inv...]
where the time goes in v4:
time: 179 us; the launch traced here: 176 us
  Pallas kernels  172 us (96%)
  local copies, waits for them, and re-layouts  2.6 us (1%)
    pallas_call x1, Pallas kernels, local_fast(): call(lensing_kernel, [shape(planes, slab, L)] * 3, [pltpu.SMEM(source_inv...  167 us

profile of v4, /device:TPU:1, one launch (start us, length us, event | category | flops | bytes accessed | tf_op | source)
XLA Modules:
  0.0 175.8 jit_solution(13139908549797127522)
XLA Ops:
  0.6 0.0 copy-start
  0.6 0.9 copy-done
  1.6 0.0 copy-start.1
  1.6 0.9 copy-done.1
  2.5 0.0 copy-start.2
  2.5 0.7 copy-done.2
  3.2 0.0 copy-start.3
  3.2 0.0 copy-start.4
  3.2 0.0 copy-start.5
  3.2 0.0 copy-start.6
  3.2 0.0 copy-start.7
  3.2 0.0 copy-start.8
  3.2 0.0 copy-start.9
  3.2 0.0 copy-start.10
  3.2 0.0 copy-start.11
  3.3 0.0 copy-start.12
  3.3 2.5 %shard_map.148 = (f32[16,72,128]{2,1,0:T(8,128)S(1)}, f32[16,72,128]{2,1,0:T(8,128)S(1)}) custom-call(s32[2,1024]{1,0:T(2,128)S(1)} %copy-done.2, s32[2,64,512]{2,1,0:T(8,128)S(1)} %copy-done, bf16[2,64,512]{2,1,0:T(8,128)(2,1)S(1)} %copy-done.1), custom_call_target="tpu_custom_call" | custom-call | flops 4294967296 | bytes 4194304 | tf_op jit(solution)/shard_map/pallas_call | solution.py:875
  5.8 0.0 copy-done.3
  5.8 0.0 copy-done.4
  5.8 0.0 copy-done.5
  5.8 0.0 copy-done.6
  5.8 0.0 copy-done.7
  5.8 0.0 copy-done.8
  5.8 0.0 copy-done.9
  5.8 0.0 copy-done.10
  5.8 0.0 copy-done.11
  5.9 0.0 copy-done.12
  5.9 167.2 %shard_map.149 = (f32[2,128,2048]{2,1,0:T(8,128)S(1)}, f32[2,128,2048]{2,1,0:T(8,128)S(1)}, f32[2,128,2048]{2,1,0:T(8,128)S(1)}) custom-call(f32[16,72,128]{2,1,0:T(8,128)S(1)} %get-tuple-element.8.out0, f32[16,72,128]{2,1,0:T(8,128)S(1)} %get-tuple-element.9.out1, f32[2]{0:T(128)S(1)} %copy-done.3, f32[2]{0:T(128)S(1)} %copy-done.4, f32[2]{0:T(128)S(1)} %copy-done.5, ...), custom_call_target="tpu_custom_call" | custom-call | flops 4294967296 | bytes 4194304 | tf_op jit(solution)/shard_map/pallas_call | solution.py:900
  173.0 2.7 %shard_map.150 = (f32[2,128,2048]{2,1,0:T(8,128)}, f32[2,128,2048]{2,1,0:T(8,128)}, f32[2,128,2048]{2,1,0:T(8,128)}) custom-call(f32[2,128,2048]{2,1,0:T(8,128)S(1)} %get-tuple-element.10.refs_0_, f32[2,128,2048]{2,1,0:T(8,128)S(1)} %get-tuple-element.11.refs_1_, f32[2,128,2048]{2,1,0:T(8,128)S(1)} %get-tuple-element.12.refs_2_), custom_call_target="tpu_custom_call" | custom-call | flops 1048576 | bytes 4194304 | tf_op jit(solution)/shard_map/pallas_call | solution.py:939
Async XLA Ops:
  0.6 1.0 copy-start
  1.6 0.9 copy-start.1
  2.5 0.7 copy-start.2
  3.2 2.6 %copy-start.3 = (f32[2]{0:T(128)S(1)}, f32[2]{0:T(128)}, u32[]{:S(2)}) copy-start(f32[2]{0:T(128)} %coef_in.1) | copy-start | bytes 28
  3.2 2.6 %copy-start.4 = (f32[2]{0:T(128)S(1)}, f32[2]{0:T(128)}, u32[]{:S(2)}) copy-start(f32[2]{0:T(128)} %dist_in.1) | copy-start | bytes 28
  3.2 2.6 %copy-start.5 = (f32[2]{0:T(128)S(1)}, f32[2]{0:T(128)}, u32[]{:S(2)}) copy-start(f32[2]{0:T(128)} %inv_in.1) | copy-start | bytes 28
  3.2 2.6 %copy-start.6 = (bf16[8,256,256]{2,1,0:T(8,128)(2,1)S(1)}, bf16[8,256,256]{2,1,0:T(8,128)(2,1)}, u32[]{:S(2)}) copy-start(bf16[8,256,256]{2,1,0:T(8,128)(2,1)} %constant.16.clone.low_in) | copy-start | bytes 3145732
  3.2 2.6 %copy-start.7 = (bf16[8,256,256]{2,1,0:T(8,128)(2,1)S(1)}, bf16[8,256,256]{2,1,0:T(8,128)(2,1)}, u32[]{:S(2)}) copy-start(bf16[8,256,256]{2,1,0:T(8,128)(2,1)} %constant.15.clone.high_in) | copy-start | bytes 3145732
  3.2 2.6 %copy-start.8 = (bf16[256,256]{1,0:T(8,128)(2,1)S(1)}, bf16[256,256]{1,0:T(8,128)(2,1)}, u32[]{:S(2)}) copy-start(bf16[256,256]{1,0:T(8,128)(2,1)} %constant.20.clone.backl_in) | copy-start | bytes 393220
  3.2 2.6 %copy-start.9 = (bf16[256,256]{1,0:T(8,128)(2,1)S(1)}, bf16[256,256]{1,0:T(8,128)(2,1)}, u32[]{:S(2)}) copy-start(bf16[256,256]{1,0:T(8,128)(2,1)} %constant.19.clone.backh_in) | copy-start | bytes 393220
  3.2 2.6 %copy-start.10 = (bf16[256,256]{1,0:T(8,128)(2,1)S(1)}, bf16[256,256]{1,0:T(8,128)(2,1)}, u32[]{:S(2)}) copy-start(bf16[256,256]{1,0:T(8,128)(2,1)} %constant.18.clone.coll_in) | copy-start | bytes 393220
  3.2 2.6 %copy-start.11 = (bf16[256,256]{1,0:T(8,128)(2,1)S(1)}, bf16[256,256]{1,0:T(8,128)(2,1)}, u32[]{:S(2)}) copy-start(bf16[256,256]{1,0:T(8,128)(2,1)} %constant.17.clone.colh_in) | copy-start | bytes 393220
  3.3 2.6 %copy-start.12 = (f32[4,16,128]{2,1,0:T(8,128)S(1)}, f32[4,16,128]{2,1,0:T(8,128)}, u32[]{:S(2)}) copy-start(f32[4,16,128]{2,1,0:T(8,128)} %constant.14.clone.twist_in_ref) | copy-start | bytes 98308

commit v5 on v4

--- a/solution.py
+++ b/solution.py
@@ -228,6 +228,7 @@
 OUTER = L // INNER
 HALF_BLOCKS = OUTER // 2
 CHUNKS = 4
+SHARED = 3
 MESH = pl.DeviceIdType.MESH
 
 
@@ -414,10 +415,9 @@
 
 
 def lensing_kernel(
-    out0, out1, coef_in, dist_in, inv_in, twist_in_ref, high_in, low_in, colh_in, coll_in, backh_in, backl_in,
+    out0, out1, coef_in, dist_in, inv_in, twist_ref, high_ref, low_ref, colh_ref, coll_ref, backh_ref, backl_ref,
     conv_ref, one_ref, two_ref,
-    coef_ref, dist_ref, inv_ref, twist_ref, high_ref, low_ref, colh_ref, coll_ref, backh_ref, backl_ref,
-    tsem, note, far_note, note_sems,
+    coef_ref, dist_ref, inv_ref, tsem, note, far_note, note_sems,
     box, slots, place, field, held_row, sending, arrived, held, kern, back, leaving, landed, total_rows,
     lsend, lrecv, psend, precv, fsend, frecv, rsend, rrecv,
 ):
@@ -430,20 +430,15 @@
     cap = message // size - 1
     chunks = sending.shape[1]
     span = INNER // chunks
-    both = chunks - 1
+    single = chunks - SHARED
+    units = chunks + SHARED
     flip = groups // 2
     pitch = slots.shape[1] // (cap * groups)
     tile_rows = slab // TR
     me, shell = lax.axis_index("pix"), lax.axis_index("shell")
     flipped = partners(me)
-    tables = fetch(
-        zip(
-            (coef_in, dist_in, inv_in, twist_in_ref, high_in, low_in, colh_in, coll_in, backh_in, backl_in),
-            (coef_ref, dist_ref, inv_ref, twist_ref, high_ref, low_ref, colh_ref, coll_ref, backh_ref, backl_ref),
-        ),
-        tsem,
-    )
-    for copy in tables[:3]:
+    factors = fetch(((coef_in, coef_ref), (dist_in, dist_ref), (inv_in, inv_ref)), tsem)
+    for copy in factors:
         copy.wait()
     note[...] = jnp.zeros_like(note)
     for p in range(planes):
@@ -481,10 +476,10 @@
 
     own_lines, mirror_lines = column_info(me), column_info((me + flip) % groups)
     signed_v, weight = (
-        jnp.concatenate([ours, theirs[both * span :]], axis=0)
+        jnp.concatenate([ours, theirs[single * span :]], axis=0)
         for ours, theirs in zip(own_lines, mirror_lines)
     )
-    inner_id = lax.broadcasted_iota(jnp.int32, (INNER + span, INNER), 1)
+    inner_id = lax.broadcasted_iota(jnp.int32, (units * span, INNER), 1)
 
     def prepare(k, _):
         u = k + OUTER * inner_id
@@ -544,7 +539,7 @@
             landing(p, m).wait_recv()
             onward(p, m).start()
 
-    lag = 4
+    lag = 2
     near_block(0)
 
     def early(m, _):
@@ -568,8 +563,6 @@
 
     lax.fori_loop(groups - lag, groups, late, 0)
 
-    for copy in tables[3:]:
-        copy.wait()
     told.wait_recv()
     lane_id = lax.broadcasted_iota(jnp.int32, (groups, TC), 1)
     tile_id = ((lane_id % tile_rows) * OUTER + lane_id // tile_rows).astype(jnp.float32)
@@ -593,7 +586,7 @@
     peers = groups - 1
 
     def go(c, peer):
-        source = sending.at[peer, c] if c < chunks else sending.at[(peer + flip) % groups, both]
+        source = sending.at[peer, c] if c < chunks else sending.at[(peer + flip) % groups, c - SHARED]
         return remote(source, arrived.at[me, c], fsend.at[c], frecv.at[c], {"pix": peer})
 
     def go_all(c):
@@ -609,7 +602,7 @@
         )
 
     def home_all(c):
-        return home_any(c, peers if c < both else flip - 1)
+        return home_any(c, peers if c < single else flip - 1)
 
     def field_rows(r, n):
         return pl.ds(pl.multiple_of(r * TC + n * tile_rows, tile_rows), tile_rows)
@@ -670,18 +663,20 @@
         b = (me // 2 + 1 + j) % HALF_BLOCKS
         row_block(b)
         for p in range(2):
-            for c in (both, chunks):
+            for c in (single, chunks):
                 peer = 2 * b + p if c < chunks else (2 * b + p + flip) % groups
                 pl.when(peer != me)(lambda: go(c, peer).start())
         return 0
 
     lax.fori_loop(0, HALF_BLOCKS, send_block, 0)
-    for c in range(both):
+    later = [c + i for i in range(1, SHARED) for c in (single, chunks)]
+    for c in later + list(range(single)):
         for m in range(1, groups):
             go(c, flipped(m)).start()
     for c in range(chunks):
         arrived[me, c] = sending[me, c]
-    arrived[me, chunks] = sending[(me + flip) % groups, both]
+    for c in range(chunks, units):
+        arrived[me, c] = sending[(me + flip) % groups, c - SHARED]
 
     def show(t, _):
         for i in range(planes):
@@ -737,13 +732,14 @@
             ).start()
         landed[slot[0], slot[1]] = leaving[me, c]
 
-    def shared_columns(c, _):
+    def shared_columns(j, _):
+        c = single + j // 2 + (j % 2) * SHARED
         go_all(c).wait_recv()
         columns(c)
-        send_home(c, range(1, flip), ((me + (c - both) * flip) % groups, both))
-        return 0
-
-    lax.fori_loop(both, chunks + 1, shared_columns, 0)
+        send_home(c, range(1, flip), ((me + (j % 2) * flip) % groups, single + j // 2))
+        return 0
+
+    lax.fori_loop(0, 2 * SHARED, shared_columns, 0)
 
     def single_columns(c, _):
         go_all(c).wait_recv()
@@ -751,9 +747,9 @@
         send_home(c, range(1, groups), (me, c))
         return 0
 
-    lax.fori_loop(0, both, single_columns, 0)
+    lax.fori_loop(0, single, single_columns, 0)
     lax.fori_loop(0, tile_rows, show, 0)
-    for c in range(chunks + 1):
+    for c in range(units):
         go_all(c).wait_send()
     told.wait_send()
     for p in range(planes):
@@ -785,16 +781,17 @@
 
         lax.fori_loop(0, HALF_BLOCKS, block, 0)
 
-    home_all(both).wait_recv()
-    home_all(chunks).wait_recv()
-    gather(both, True)
+    for c in range(single, chunks):
+        home_all(c).wait_recv()
+        home_all(c + SHARED).wait_recv()
+        gather(c, c == single)
 
     def more(c, _):
         home_any(c).wait_recv()
         gather(c, False)
         return 0
 
-    lax.fori_loop(0, both, more, 0)
+    lax.fori_loop(0, single, more, 0)
     for f, out_ref in enumerate((one_ref, two_ref)):
 
         def radix(t, _):
@@ -816,7 +813,7 @@
             return 0
 
         lax.fori_loop(0, slab // 8, radix, 0)
-    for c in range(chunks + 1):
+    for c in range(units):
         home_all(c).wait_send()
 
 
@@ -901,9 +898,8 @@
         lensing_kernel,
         [shape(planes, slab, L)] * 3,
         [pltpu.SMEM(source_inv.shape, jnp.float32)] * 3
-        + [pltpu.VMEM(table.shape, table.dtype) for table in tables]
         + [
-            dma(3 + len(tables)),
+            dma(3),
             vmem(8, TC),
             vmem(8, TC),
             dma(2),
@@ -913,24 +909,24 @@
             vmem(planes, TR * TC, TC),
             vmem(HALF_BLOCKS, planes, slab, 2 * INNER),
             vmem(groups, CHUNKS, 2 * span, slab),
-            vmem(groups, CHUNKS + 1, 2 * span, slab),
+            vmem(groups, CHUNKS + SHARED, 2 * span, slab),
             vmem(OUTER * span, 2 * INNER),
-            vmem(2, OUTER, INNER + span, INNER),
+            vmem(2, OUTER, INNER + SHARED * span, INNER),
             vmem(2, OUTER, span, 2 * INNER),
-            vmem(groups, CHUNKS + 1, 2, 2 * span, slab),
+            vmem(groups, CHUNKS + SHARED, 2, 2 * span, slab),
             vmem(groups, CHUNKS, 2, 2 * span, slab),
             vmem(2, HALF_BLOCKS, planes, slab, 2 * INNER),
             dma(planes, groups),
             dma(planes, groups),
             dma(planes, groups),
             dma(planes, groups),
-            dma(CHUNKS + 1),
-            dma(CHUNKS + 1),
-            dma(CHUNKS + 1),
-            dma(CHUNKS + 1),
+            dma(CHUNKS + SHARED),
+            dma(CHUNKS + SHARED),
+            dma(CHUNKS + SHARED),
+            dma(CHUNKS + SHARED),
         ],
         smem=(),
-        hbm=tuple(range(2, 12)),
+        hbm=(2, 3, 4),
         count=12,
         megabytes=40,
         flops=1 << 32,

time: 179 us -> 166 us (0.927); the launches traced: 176 us -> 166 us
  Pallas kernels: 172 us -> 163 us
    pallas_call x1, Pallas kernels: 167 us -> 158 us  [local_fast(): call(lensing_kernel, [shape(planes, slab, L)] * 3, [pltpu.SMEM(source_inv...]
where the time goes in v5:
time: 166 us
  Pallas kernels  163 us (98%)
  local copies, waits for them, and re-layouts  2.6 us (2%)
    pallas_call x1, Pallas kernels, local_fast(): call(lensing_kernel, [shape(planes, slab, L)] * 3, [pltpu.SMEM(source_inv...  158 us

profile of v5, /device:TPU:1, one launch (start us, length us, event | category | flops | bytes accessed | tf_op | source)
XLA Modules:
  0.0 166.2 jit_solution(11052781420654520862)
XLA Ops:
  0.6 0.0 copy-start
  0.6 0.9 copy-done
  1.6 0.0 copy-start.1
  1.6 0.9 copy-done.1
  2.5 0.0 copy-start.2
  2.5 0.7 copy-done.2
  3.2 0.0 copy-start.3
  3.2 0.0 copy-start.4
  3.2 0.0 copy-start.5
  3.2 0.0 copy-start.6
  3.2 0.0 copy-start.7
  3.2 0.0 copy-start.8
  3.2 0.0 copy-start.9
  3.2 0.0 copy-start.10
  3.2 0.0 copy-start.11
  3.3 0.0 copy-start.12
  3.3 2.5 %shard_map.148 = (f32[16,72,128]{2,1,0:T(8,128)S(1)}, f32[16,72,128]{2,1,0:T(8,128)S(1)}) custom-call(s32[2,1024]{1,0:T(2,128)S(1)} %copy-done.2, s32[2,64,512]{2,1,0:T(8,128)S(1)} %copy-done, bf16[2,64,512]{2,1,0:T(8,128)(2,1)S(1)} %copy-done.1), custom_call_target="tpu_custom_call" | custom-call | flops 4294967296 | bytes 4194304 | tf_op jit(solution)/shard_map/pallas_call | solution.py:872
  5.8 0.0 copy-done.3
  5.8 0.0 copy-done.4
  5.8 0.0 copy-done.5
  5.8 0.0 copy-done.6
  5.8 0.0 copy-done.7
  5.8 0.0 copy-done.8
  5.8 0.0 copy-done.9
  5.8 0.0 copy-done.10
  5.8 0.0 copy-done.11
  5.9 0.0 copy-done.12
  5.9 157.6 %shard_map.149 = (f32[2,128,2048]{2,1,0:T(8,128)S(1)}, f32[2,128,2048]{2,1,0:T(8,128)S(1)}, f32[2,128,2048]{2,1,0:T(8,128)S(1)}) custom-call(f32[16,72,128]{2,1,0:T(8,128)S(1)} %get-tuple-element.8.out0, f32[16,72,128]{2,1,0:T(8,128)S(1)} %get-tuple-element.9.out1, f32[2]{0:T(128)S(1)} %copy-done.3, f32[2]{0:T(128)S(1)} %copy-done.4, f32[2]{0:T(128)S(1)} %copy-done.5, ...), custom_call_target="tpu_custom_call" | custom-call | flops 4294967296 | bytes 4194304 | tf_op jit(solution)/shard_map/pallas_call | solution.py:897
  163.4 2.7 %shard_map.150 = (f32[2,128,2048]{2,1,0:T(8,128)}, f32[2,128,2048]{2,1,0:T(8,128)}, f32[2,128,2048]{2,1,0:T(8,128)}) custom-call(f32[2,128,2048]{2,1,0:T(8,128)S(1)} %get-tuple-element.10.refs_0_, f32[2,128,2048]{2,1,0:T(8,128)S(1)} %get-tuple-element.11.refs_1_, f32[2,128,2048]{2,1,0:T(8,128)S(1)} %get-tuple-element.12.refs_2_), custom_call_target="tpu_custom_call" | custom-call | flops 1048576 | bytes 4194304 | tf_op jit(solution)/shard_map/pallas_call | solution.py:935
Async XLA Ops:
  0.6 1.0 copy-start
  1.6 0.9 copy-start.1
  2.5 0.7 copy-start.2
  3.2 2.6 %copy-start.3 = (f32[2]{0:T(128)S(1)}, f32[2]{0:T(128)}, u32[]{:S(2)}) copy-start(f32[2]{0:T(128)} %coef_in.1) | copy-start | bytes 28
  3.2 2.6 %copy-start.4 = (f32[2]{0:T(128)S(1)}, f32[2]{0:T(128)}, u32[]{:S(2)}) copy-start(f32[2]{0:T(128)} %dist_in.1) | copy-start | bytes 28
  3.2 2.6 %copy-start.5 = (f32[2]{0:T(128)S(1)}, f32[2]{0:T(128)}, u32[]{:S(2)}) copy-start(f32[2]{0:T(128)} %inv_in.1) | copy-start | bytes 28
  3.2 2.6 %copy-start.6 = (bf16[8,256,256]{2,1,0:T(8,128)(2,1)S(1)}, bf16[8,256,256]{2,1,0:T(8,128)(2,1)}, u32[]{:S(2)}) copy-start(bf16[8,256,256]{2,1,0:T(8,128)(2,1)} %constant.16.clone.low_ref) | copy-start | bytes 3145732
  3.2 2.6 %copy-start.7 = (bf16[8,256,256]{2,1,0:T(8,128)(2,1)S(1)}, bf16[8,256,256]{2,1,0:T(8,128)(2,1)}, u32[]{:S(2)}) copy-start(bf16[8,256,256]{2,1,0:T(8,128)(2,1)} %constant.15.clone.high_ref) | copy-start | bytes 3145732
  3.2 2.6 %copy-start.8 = (bf16[256,256]{1,0:T(8,128)(2,1)S(1)}, bf16[256,256]{1,0:T(8,128)(2,1)}, u32[]{:S(2)}) copy-start(bf16[256,256]{1,0:T(8,128)(2,1)} %constant.20.clone.backl_ref) | copy-start | bytes 393220
  3.2 2.6 %copy-start.9 = (bf16[256,256]{1,0:T(8,128)(2,1)S(1)}, bf16[256,256]{1,0:T(8,128)(2,1)}, u32[]{:S(2)}) copy-start(bf16[256,256]{1,0:T(8,128)(2,1)} %constant.19.clone.backh_ref) | copy-start | bytes 393220
  3.2 2.6 %copy-start.10 = (bf16[256,256]{1,0:T(8,128)(2,1)S(1)}, bf16[256,256]{1,0:T(8,128)(2,1)}, u32[]{:S(2)}) copy-start(bf16[256,256]{1,0:T(8,128)(2,1)} %constant.18.clone.coll_ref) | copy-start | bytes 393220
  3.2 2.6 %copy-start.11 = (bf16[256,256]{1,0:T(8,128)(2,1)S(1)}, bf16[256,256]{1,0:T(8,128)(2,1)}, u32[]{:S(2)}) copy-start(bf16[256,256]{1,0:T(8,128)(2,1)} %constant.17.clone.colh_ref) | copy-start | bytes 393220
  3.3 2.6 %copy-start.12 = (f32[4,16,128]{2,1,0:T(8,128)S(1)}, f32[4,16,128]{2,1,0:T(8,128)}, u32[]{:S(2)}) copy-start(f32[4,16,128]{2,1,0:T(8,128)} %constant.14.clone.twist_ref) | copy-start | bytes 98308

commit v6 on v5

--- a/solution.py
+++ b/solution.py
@@ -229,6 +229,7 @@
 HALF_BLOCKS = OUTER // 2
 CHUNKS = 4
 SHARED = 3
+ALONE_AT = 1
 MESH = pl.DeviceIdType.MESH
 
 
@@ -659,18 +660,20 @@
                     2 * span * c : 2 * span * (c + 1), p * slab : (p + 1) * slab
                 ]
 
+    order = [(single + i, chunks + i) for i in range(SHARED)]
+    order[ALONE_AT:ALONE_AT] = [(c,) for c in range(single)]
+
     def send_block(j, _):
         b = (me // 2 + 1 + j) % HALF_BLOCKS
         row_block(b)
         for p in range(2):
-            for c in (single, chunks):
+            for c in order[0]:
                 peer = 2 * b + p if c < chunks else (2 * b + p + flip) % groups
                 pl.when(peer != me)(lambda: go(c, peer).start())
         return 0
 
     lax.fori_loop(0, HALF_BLOCKS, send_block, 0)
-    later = [c + i for i in range(1, SHARED) for c in (single, chunks)]
-    for c in later + list(range(single)):
+    for c in [c for group in order[1:] for c in group]:
         for m in range(1, groups):
             go(c, flipped(m)).start()
     for c in range(chunks):
@@ -739,15 +742,15 @@
         send_home(c, range(1, flip), ((me + (j % 2) * flip) % groups, single + j // 2))
         return 0
 
-    lax.fori_loop(0, 2 * SHARED, shared_columns, 0)
-
     def single_columns(c, _):
         go_all(c).wait_recv()
         columns(c)
         send_home(c, range(1, groups), (me, c))
         return 0
 
+    lax.fori_loop(0, 2 * ALONE_AT, shared_columns, 0)
     lax.fori_loop(0, single, single_columns, 0)
+    lax.fori_loop(2 * ALONE_AT, 2 * SHARED, shared_columns, 0)
     lax.fori_loop(0, tile_rows, show, 0)
     for c in range(units):
         go_all(c).wait_send()
@@ -781,17 +784,10 @@
 
         lax.fori_loop(0, HALF_BLOCKS, block, 0)
 
-    for c in range(single, chunks):
-        home_all(c).wait_recv()
-        home_all(c + SHARED).wait_recv()
-        gather(c, c == single)
-
-    def more(c, _):
-        home_any(c).wait_recv()
-        gather(c, False)
-        return 0
-
-    lax.fori_loop(0, single, more, 0)
+    for at, group in enumerate(order):
+        for c in group:
+            home_all(c).wait_recv()
+        gather(group[0], at == 0)
     for f, out_ref in enumerate((one_ref, two_ref)):
 
         def radix(t, _):

time: 166 us -> 166 us (level)
  Pallas kernels: 163 us -> 161 us
where the time goes in v6:
time: 166 us; the launch traced here: 165 us
  Pallas kernels  161 us (97%)
  local copies, waits for them, and re-layouts  2.6 us (2%)
    pallas_call x1, Pallas kernels, local_fast(): call(lensing_kernel, [shape(planes, slab, L)] * 3, [pltpu.SMEM(source_inv...  156 us

profile of v6, /device:TPU:1, one launch (start us, length us, event | category | flops | bytes accessed | tf_op | source)
XLA Modules:
  0.0 164.7 jit_solution(5392217460397309593)
XLA Ops:
  0.6 0.0 copy-start
  0.6 0.9 copy-done
  1.6 0.0 copy-start.1
  1.6 0.9 copy-done.1
  2.5 0.0 copy-start.2
  2.5 0.7 copy-done.2
  3.2 0.0 copy-start.3
  3.2 0.0 copy-start.4
  3.2 0.0 copy-start.5
  3.2 0.0 copy-start.6
  3.2 0.0 copy-start.7
  3.2 0.0 copy-start.8
  3.2 0.0 copy-start.9
  3.2 0.0 copy-start.10
  3.2 0.0 copy-start.11
  3.3 0.0 copy-start.12
  3.3 2.5 %shard_map.148 = (f32[16,72,128]{2,1,0:T(8,128)S(1)}, f32[16,72,128]{2,1,0:T(8,128)S(1)}) custom-call(s32[2,1024]{1,0:T(2,128)S(1)} %copy-done.2, s32[2,64,512]{2,1,0:T(8,128)S(1)} %copy-done, bf16[2,64,512]{2,1,0:T(8,128)(2,1)S(1)} %copy-done.1), custom_call_target="tpu_custom_call" | custom-call | flops 4294967296 | bytes 4194304 | tf_op jit(solution)/shard_map/pallas_call | solution.py:868
  5.8 0.0 copy-done.3
  5.8 0.0 copy-done.4
  5.8 0.0 copy-done.5
  5.8 0.0 copy-done.6
  5.8 0.0 copy-done.7
  5.8 0.0 copy-done.8
  5.8 0.0 copy-done.9
  5.8 0.0 copy-done.10
  5.8 0.0 copy-done.11
  5.9 0.0 copy-done.12
  5.9 156.1 %shard_map.149 = (f32[2,128,2048]{2,1,0:T(8,128)S(1)}, f32[2,128,2048]{2,1,0:T(8,128)S(1)}, f32[2,128,2048]{2,1,0:T(8,128)S(1)}) custom-call(f32[16,72,128]{2,1,0:T(8,128)S(1)} %get-tuple-element.8.out0, f32[16,72,128]{2,1,0:T(8,128)S(1)} %get-tuple-element.9.out1, f32[2]{0:T(128)S(1)} %copy-done.3, f32[2]{0:T(128)S(1)} %copy-done.4, f32[2]{0:T(128)S(1)} %copy-done.5, ...), custom_call_target="tpu_custom_call" | custom-call | flops 4294967296 | bytes 4194304 | tf_op jit(solution)/shard_map/pallas_call | solution.py:893
  161.9 2.7 %shard_map.150 = (f32[2,128,2048]{2,1,0:T(8,128)}, f32[2,128,2048]{2,1,0:T(8,128)}, f32[2,128,2048]{2,1,0:T(8,128)}) custom-call(f32[2,128,2048]{2,1,0:T(8,128)S(1)} %get-tuple-element.10.refs_0_, f32[2,128,2048]{2,1,0:T(8,128)S(1)} %get-tuple-element.11.refs_1_, f32[2,128,2048]{2,1,0:T(8,128)S(1)} %get-tuple-element.12.refs_2_), custom_call_target="tpu_custom_call" | custom-call | flops 1048576 | bytes 4194304 | tf_op jit(solution)/shard_map/pallas_call | solution.py:931
Async XLA Ops:
  0.6 1.0 copy-start
  1.6 0.9 copy-start.1
  2.5 0.7 copy-start.2
  3.2 2.6 %copy-start.3 = (f32[2]{0:T(128)S(1)}, f32[2]{0:T(128)}, u32[]{:S(2)}) copy-start(f32[2]{0:T(128)} %coef_in.1) | copy-start | bytes 28
  3.2 2.6 %copy-start.4 = (f32[2]{0:T(128)S(1)}, f32[2]{0:T(128)}, u32[]{:S(2)}) copy-start(f32[2]{0:T(128)} %dist_in.1) | copy-start | bytes 28
  3.2 2.6 %copy-start.5 = (f32[2]{0:T(128)S(1)}, f32[2]{0:T(128)}, u32[]{:S(2)}) copy-start(f32[2]{0:T(128)} %inv_in.1) | copy-start | bytes 28
  3.2 2.6 %copy-start.6 = (bf16[8,256,256]{2,1,0:T(8,128)(2,1)S(1)}, bf16[8,256,256]{2,1,0:T(8,128)(2,1)}, u32[]{:S(2)}) copy-start(bf16[8,256,256]{2,1,0:T(8,128)(2,1)} %constant.16.clone.low_ref) | copy-start | bytes 3145732
  3.2 2.6 %copy-start.7 = (bf16[8,256,256]{2,1,0:T(8,128)(2,1)S(1)}, bf16[8,256,256]{2,1,0:T(8,128)(2,1)}, u32[]{:S(2)}) copy-start(bf16[8,256,256]{2,1,0:T(8,128)(2,1)} %constant.15.clone.high_ref) | copy-start | bytes 3145732
  3.2 2.6 %copy-start.8 = (bf16[256,256]{1,0:T(8,128)(2,1)S(1)}, bf16[256,256]{1,0:T(8,128)(2,1)}, u32[]{:S(2)}) copy-start(bf16[256,256]{1,0:T(8,128)(2,1)} %constant.20.clone.backl_ref) | copy-start | bytes 393220
  3.2 2.6 %copy-start.9 = (bf16[256,256]{1,0:T(8,128)(2,1)S(1)}, bf16[256,256]{1,0:T(8,128)(2,1)}, u32[]{:S(2)}) copy-start(bf16[256,256]{1,0:T(8,128)(2,1)} %constant.19.clone.backh_ref) | copy-start | bytes 393220
  3.2 2.6 %copy-start.10 = (bf16[256,256]{1,0:T(8,128)(2,1)S(1)}, bf16[256,256]{1,0:T(8,128)(2,1)}, u32[]{:S(2)}) copy-start(bf16[256,256]{1,0:T(8,128)(2,1)} %constant.18.clone.coll_ref) | copy-start | bytes 393220
  3.2 2.6 %copy-start.11 = (bf16[256,256]{1,0:T(8,128)(2,1)S(1)}, bf16[256,256]{1,0:T(8,128)(2,1)}, u32[]{:S(2)}) copy-start(bf16[256,256]{1,0:T(8,128)(2,1)} %constant.17.clone.colh_ref) | copy-start | bytes 393220
  3.3 2.6 %copy-start.12 = (f32[4,16,128]{2,1,0:T(8,128)S(1)}, f32[4,16,128]{2,1,0:T(8,128)}, u32[]{:S(2)}) copy-start(f32[4,16,128]{2,1,0:T(8,128)} %constant.14.clone.twist_ref) | copy-start | bytes 98308
